TPU v7x, 512 devices: a 4x2x32 block of a 4x16x32 slice. The times are simulated.
512 devices in a mesh: groups: 2 (over y), row: 32 (over z), col: 4 (over x), sub: 2 (over core).
Axes of the slice: x: 4, y: 2, z: 32, core: 2. Of those that a mesh axis runs over, the one named last changes fastest.
The devices are a block of a 4x16x32 slice.
Arguments:
- matrix: float32 [16384, 8192], P(('groups', 'row'), ('col', 'sub')), parts along dimension 0, may hold values from -60 to 60
- basis_vectors: float32 [16384, 1024], P(('groups', 'row'), ('col', 'sub')), parts along dimension 0, may hold values from -0.0625 to 0.0625
- split_size: int32 [2], P('groups'), parts along dimension 0, may hold values from 256 to 767
Outputs:
- children: float32 [2, 2048, 1024], P('sub', ('groups', 'row'), 'col'), parts along dimension 1
There are 2 independent parts, one for each index of `groups`. A program takes and returns all parts, laid end to end along the dimension named above; each array names one. Nothing has to cross between parts.
Inputs may be any that keep to these rules, and one draw needn't show every extreme that they name: The second subspace has 1024 minus split_size vectors.
All inputs are finite; a program needn't handle non-finite values.
Results may differ from a plain program's by a relative error of at most 0.00011.
Values sent between devices are 32-bit elements; how exact they have to be, the bound alone decides.
No kernel may reach another device: no remote copies, remote signals or barrier semaphores. Data moves between devices by JAX's collectives and lax.ppermute only.
A program may use at most 64 MiB of HBM per device.

v0:
```python
import jax
import jax.numpy as jnp
from jax import lax
from jax.sharding import PartitionSpec as P


def cut_along(array, dim, size):
    before, after = (array.shape[:dim], array.shape[dim + 1 :])
    return jnp.moveaxis(array.reshape(*before, size, -1, *after), dim, 0)


def sent_and_summed(array, axis, dim):
    size = lax.axis_size(axis)
    pieces = lax.all_to_all(cut_along(array, dim, size), axis, 0, 0, tiled=True)
    return jnp.sum(pieces, axis=0)


def copy_for_each(array, axis):
    size = lax.axis_size(axis)
    return lax.all_to_all(
        jnp.broadcast_to(array[None], (size, *array.shape)), axis, 0, 0, tiled=True
    )


def laid_out(pieces, dim):
    dims = list(pieces.shape[1:])
    dims[dim] *= pieces.shape[0]
    return jnp.moveaxis(pieces, 0, dim).reshape(dims)


def gathered_copies(array, axis, dim):
    pieces = copy_for_each(array, axis)
    return laid_out(pieces, dim)


def shards(matrix, basis_vectors, split_size):
    strip = lax.all_gather(basis_vectors, "row", axis=0, tiled=True)
    row_panel = lax.all_to_all(strip, ("col", "sub"), split_axis=0, concat_axis=1, tiled=True)
    partial_image = jnp.dot(
        matrix, row_panel, precision=lax.Precision.HIGHEST, preferred_element_type=jnp.float32
    )
    image = sent_and_summed(partial_image, ("col", "sub"), 1)
    partial_proj = lax.dot_general(
        gathered_copies(basis_vectors, ("col", "sub"), 1),
        image,
        (((0,), (0,)), ((), ())),
        precision=lax.Precision.HIGHEST,
        preferred_element_type=jnp.float32,
    )
    proj_block = sent_and_summed(partial_proj, "row", 0)
    child_block = lax.all_gather(proj_block, "sub", axis=1, tiled=True)
    row_ids = (
        jnp.arange(child_block.shape[0], dtype=jnp.int32)
        + lax.axis_index("row") * child_block.shape[0]
    )
    col_ids = (
        jnp.arange(child_block.shape[1], dtype=jnp.int32)
        + lax.axis_index("col") * child_block.shape[1]
    )
    leading = split_size[0]
    row_first = row_ids < leading
    col_first = col_ids < leading
    mask_one = row_first[:, None] & col_first[None, :]
    mask_two = jnp.logical_not(row_first)[:, None] & jnp.logical_not(col_first)[None, :]
    selected = jnp.where(lax.axis_index("sub") == 0, mask_one, mask_two)
    return jnp.where(selected, child_block, jnp.zeros((), jnp.float32))[None]


def solution(mesh):
    placed = (
        P(("groups", "row"), ("col", "sub")),
        P(("groups", "row"), ("col", "sub")),
        P("groups"),
    )
    return jax.shard_map(
        shards,
        mesh=mesh,
        in_specs=placed,
        out_specs=P("sub", ("groups", "row"), "col"),
        check_vma=False,
    )
```

profile of v0, /device:TPU:33, one launch (start us, length us, event | category | flops | bytes accessed | tf_op | source)
XLA Modules:
  0.0 370.7 jit_solution(7150744775797212419)
XLA Ops:
  6.5 0.0 copy-start
  6.6 0.0 all-gather.2.cloned.1.call-start
  6.6 0.7 all-gather.2.cloned.1.call-update
  7.3 148.1 %all-gather.2.cloned.1.call-done = f32[8192,128]{1,0:T(8,128)} async-done(((f32[256,128]{1,0:T(8,128)}), f32[8192,128]{1,0:T(8,128)}) %all-gather.2.cloned.1.call-update) | async-done | bytes 4194320 | tf_op jit(solution)/shard_map/all_gather | solution.py:37
  155.4 74.3 %all_to_all.34 = f32[8,1024,128]{2,1,0:T(8,128)} all-to-all(f32[8,1024,128]{2,1,0:T(8,128)} %bitcast.30), channel_id=1, replica_groups=mesh['groups'=2,'row'=32,'col'=4,'sub'=2] {'col','sub'}, dimensions={0} | all-to-all | bytes 8388608 | tf_op jit(solution)/shard_map/all_to_all | solution.py:38
  229.7 5.4 %copy.6 = f32[1024,8,128]{0,2,1:T(8,128)} copy(f32[1024,8,128]{2,0,1:T(8,128)} %bitcast.29) | data formatting | bytes 8388608 | tf_op jit(solution)/shard_map/all_to_all | solution.py:38
  235.1 0.0 copy-done
  235.1 0.0 copy-start.1
  235.1 6.3 %fusion.2 = f32[8,256,128]{2,1,0:T(8,128)} fusion(f32[1024,8,128]{0,2,1:T(8,128)} %copy.6, f32[256,1024]{1,0:T(8,128)S(1)} %copy-done), kind=kOutput, calls=%fused_computation.2 | convolution fusion | flops 3221225472 | bytes 6291456 | tf_op jit(solution)/shard_map/dot_general | solution.py:39
  241.4 4.5 %all-to-all-start.1 = ((f32[8,256,128]{2,1,0:T(8,128)}), f32[8,256,128]{2,1,0:T(8,128)S(1)}, u32[]{:S(2)}, u32[]{:S(2)}) async-start(f32[8,256,128]{2,1,0:T(8,128)} %fusion.2), calls=%async_computation.1 | async-start | bytes 2097152 | tf_op jit(solution)/shard_map/all_to_all | solution.py:14
  245.9 0.0 copy-done.1
  245.9 0.1 copy.7
  246.0 15.0 %all-to-all-done.1 = f32[8,256,128]{2,1,0:T(8,128)S(1)} async-done(((f32[8,256,128]{2,1,0:T(8,128)}), f32[8,256,128]{2,1,0:T(8,128)S(1)}, u32[]{:S(2)}, u32[]{:S(2)}) %all-to-all-start.1) | async-done | bytes 1048608 | tf_op jit(solution)/shard_map/all_to_all | solution.py:14
  261.0 1.1 broadcast_in_dim.7
  262.0 4.4 %all-to-all-start.2 = ((f32[8,256,128]{1,2,0:T(8,128)}), f32[8,256,128]{1,2,0:T(8,128)S(1)}, u32[]{:S(2)}, u32[]{:S(2)}) async-start(f32[8,256,128]{1,2,0:T(8,128)} %broadcast_in_dim.7), calls=%async_computation.2 | async-start | bytes 2097152 | tf_op jit(solution)/shard_map/all_to_all | solution.py:20
  266.4 0.1 reduce_sum.18
  266.5 15.0 %all-to-all-done.2 = f32[8,256,128]{1,2,0:T(8,128)S(1)} async-done(((f32[8,256,128]{1,2,0:T(8,128)}), f32[8,256,128]{1,2,0:T(8,128)S(1)}, u32[]{:S(2)}, u32[]{:S(2)}) %all-to-all-start.2) | async-done | bytes 1048608 | tf_op jit(solution)/shard_map/all_to_all | solution.py:20
  281.5 1.2 convolution_bitcast_fusion
  282.7 1.0 copy.8
  283.7 12.6 %all-to-all-start.3 = ((f32[32,32,128]{2,1,0:T(8,128)}), f32[32,32,128]{2,1,0:T(8,128)S(1)}, u32[]{:S(2)}, u32[]{:S(2)}) async-start(f32[32,32,128]{2,1,0:T(8,128)} %bitcast.11), calls=%async_computation.3 | async-start | bytes 1048576 | tf_op jit(solution)/shard_map/all_to_all | solution.py:14
  297.0 63.0 %all-to-all-done.3 = f32[32,32,128]{2,1,0:T(8,128)S(1)} async-done(((f32[32,32,128]{2,1,0:T(8,128)}), f32[32,32,128]{2,1,0:T(8,128)S(1)}, u32[]{:S(2)}, u32[]{:S(2)}) %all-to-all-start.3) | async-done | bytes 524320 | tf_op jit(solution)/shard_map/all_to_all | solution.py:14
  360.1 3.1 all_gather.7
  363.2 0.7 select_bitcast_fusion
  (3 shorter events, 0.1 us)
Async XLA Ops:
  6.5 228.5 %copy-start = (f32[256,1024]{1,0:T(8,128)S(1)}, f32[256,1024]{1,0:T(8,128)}, u32[]{:S(2)}) copy-start(f32[256,1024]{1,0:T(8,128)} %param.3) | copy-start | bytes 3145732
  6.6 148.8 %all-gather.2.cloned.1.call-start = ((), (), s32[]{:S(2)}) async-start(), calls=%async_computation.4 | async-start | bytes 4325376 | tf_op jit(solution)/shard_map/all_gather | solution.py:37
  235.1 10.8 %copy-start.1 = (f32[256,128]{1,0:T(8,128)S(1)}, f32[256,128]{1,0:T(8,128)}, u32[]{:S(2)}) copy-start(f32[256,128]{1,0:T(8,128)} %param.4) | copy-start | bytes 393220
  241.4 19.6 %all-to-all-start.1 = ((f32[8,256,128]{2,1,0:T(8,128)}), f32[8,256,128]{2,1,0:T(8,128)S(1)}, u32[]{:S(2)}, u32[]{:S(2)}) async-start(f32[8,256,128]{2,1,0:T(8,128)} %fusion.2), calls=%async_computation.1 | async-start | bytes 2097152 | tf_op jit(solution)/shard_map/all_to_all | solution.py:14
  262.0 19.5 %all-to-all-start.2 = ((f32[8,256,128]{1,2,0:T(8,128)}), f32[8,256,128]{1,2,0:T(8,128)S(1)}, u32[]{:S(2)}, u32[]{:S(2)}) async-start(f32[8,256,128]{1,2,0:T(8,128)} %broadcast_in_dim.7), calls=%async_computation.2 | async-start | bytes 2097152 | tf_op jit(solution)/shard_map/all_to_all | solution.py:20
  283.7 76.3 %all-to-all-start.3 = ((f32[32,32,128]{2,1,0:T(8,128)}), f32[32,32,128]{2,1,0:T(8,128)S(1)}, u32[]{:S(2)}, u32[]{:S(2)}) async-start(f32[32,32,128]{2,1,0:T(8,128)} %bitcast.11), calls=%async_computation.3 | async-start | bytes 1048576 | tf_op jit(solution)/shard_map/all_to_all | solution.py:14
Sparse Core Ops, SparseCore 0:
  9.4 145.8 all-gather.1
where the time goes:
time: 371 us
  waiting for transfers between devices  242 us (65%)
  blocking collectives  77.4 us (21%)
  starting transfers between devices  21.5 us (6%)
  between operations  14.1 us (4%)
  matrix products  7.56 us (2%)
  local copies, waits for them, and re-layouts  7.52 us (2%)
    all_gather x1, waiting for transfers between devices, shards(): strip = lax.all_gather(basis_vectors, 'row', axis=0, tiled=True)  148 us
    all_to_all x2, waiting for transfers between devices, sent_and_summed(): pieces = lax.all_to_all(cut_along(array, dim, size), axis, 0, 0, tiled=True)  78 us
    all_to_all x1, blocking collectives, shards(): lax.all_to_all(strip, ('col', 'sub'), split_axis=0, concat_axis=1, tiled=...  74.3 us
    all_to_all x2, starting transfers between devices, sent_and_summed(): pieces = lax.all_to_all(cut_along(array, dim, size), axis, 0, 0, tiled=True)  17.1 us
    all_to_all x1, waiting for transfers between devices, copy_for_each(): lax.all_to_all(jnp.broadcast_to(array[None], (size, *array.shape)), axis,...  15 us
  transfers between devices with their start and end apart: 4, of which 4 were waited for; matrix products, arithmetic and copies ran while one was open for 0% of the time, Pallas kernels for 0%

commit v1 on v0

v1 whole, which is shorter than its diff:
```python
import jax
import jax.numpy as jnp
from jax import lax
from jax.sharding import PartitionSpec as P

PRECISION = lax.Precision.HIGHEST
NEAR = 4


def shifted(array, axis, step):
    size = lax.axis_size(axis)
    return lax.ppermute(array, axis, [(i, (i + step) % size) for i in range(size)])


def swapped(array, axis):
    size = lax.axis_size(axis)
    return lax.ppermute(array, axis, [(i, i ^ 1) for i in range(size)])


def product(left, right, contract):
    return lax.dot_general(
        left, right, (contract, ((), ())), precision=PRECISION, preferred_element_type=jnp.float32
    )


def all_columns(basis):
    half = basis.shape[0] // 2
    parts = [lax.all_gather(basis[i * half : (i + 1) * half], ("col", "sub"), axis=0) for i in range(2)]
    return parts


def shards(matrix, basis_vectors, split_size):
    rows_here, width = matrix.shape
    n_row = lax.axis_size("row")
    n_col = lax.axis_size("col")
    row = lax.axis_index("row")
    col = lax.axis_index("col")
    sub = lax.axis_index("sub")
    parity = row % 2

    every_other = [[first + 2 * i for i in range(n_row // 2)] for first in range(2)]
    strip = lax.all_gather(
        basis_vectors, "row", axis=0, tiled=True, axis_index_groups=every_other
    )

    blocks = matrix.reshape(rows_here, width // (2 * rows_here), 2, rows_here)
    keep = jnp.where(parity == 0, blocks[:, :, 0], blocks[:, :, 1]).reshape(rows_here, width // 2)
    give = jnp.where(parity == 0, blocks[:, :, 1], blocks[:, :, 0]).reshape(rows_here, width // 2)
    own = jnp.concatenate([keep, swapped(give, "row")], axis=0)

    before = shifted(own, "col", 1)
    after = shifted(own, "col", -1)
    half = own.shape[0] // 2
    across = jnp.concatenate(
        [shifted(before[:half], "col", 1), shifted(after[half:], "col", -1)], axis=0
    )
    pieces = {0: own, 1: before, 2: across, 3: after}

    mate = swapped(basis_vectors, "row")
    pair_basis = jnp.concatenate(all_columns(basis_vectors) + all_columns(mate), axis=1)

    span = own.shape[1]
    image = None
    for distance, piece in pieces.items():
        source = (col - distance) % n_col
        other = swapped(piece, "sub")
        for core, operand in ((sub, piece), (1 - sub, other)):
            rows = lax.dynamic_slice_in_dim(strip, (source * 2 + core) * span, span, 0)
            part = product(operand, rows, ((1,), (0,)))
            image = part if image is None else image + part

    partial = product(pair_basis, image, ((1,), (0,)))
    total = partial.shape[0] * partial.shape[1]
    share = total // n_row
    far = n_row // NEAR
    partial = partial.reshape(far, NEAR, share, -1).swapaxes(0, 1)
    near_groups = [[NEAR * g + q for q in range(NEAR)] for g in range(far)]
    far_groups = [[NEAR * g + q for g in range(far)] for q in range(NEAR)]
    partial = lax.all_to_all(
        partial, "row", 0, 0, tiled=True, axis_index_groups=near_groups
    ).sum(0)
    proj_block = lax.all_to_all(
        partial, "row", 0, 0, tiled=True, axis_index_groups=far_groups
    ).sum(0)

    child_block = lax.all_gather(proj_block, "sub", axis=1, tiled=True)
    row_ids = jnp.arange(child_block.shape[0], dtype=jnp.int32) + row * child_block.shape[0]
    col_ids = jnp.arange(child_block.shape[1], dtype=jnp.int32) + col * child_block.shape[1]
    leading = split_size[0]
    row_first = row_ids < leading
    col_first = col_ids < leading
    mask_one = row_first[:, None] & col_first[None, :]
    mask_two = jnp.logical_not(row_first)[:, None] & jnp.logical_not(col_first)[None, :]
    selected = jnp.where(sub == 0, mask_one, mask_two)
    return jnp.where(selected, child_block, jnp.zeros((), jnp.float32))[None]


def solution(mesh):
    placed = (
        P(("groups", "row"), ("col", "sub")),
        P(("groups", "row"), ("col", "sub")),
        P("groups"),
    )
    return jax.shard_map(
        shards,
        mesh=mesh,
        in_specs=placed,
        out_specs=P("sub", ("groups", "row"), "col"),
        check_vma=False,
    )
```

time: 371 us -> 286 us (0.77)
  waiting for transfers between devices: 242 us -> 30.5 us
  blocking collectives: 77.4 us -> 142 us
  starting transfers between devices: 21.5 us -> 61.3 us
  matrix products: 7.56 us -> 17.1 us
  local copies, waits for them, and re-layouts: 7.52 us -> 14.2 us
  other arithmetic: 0.82 us -> 4.92 us
    all_gather x1, waiting for transfers between devices: 148 us -> 0.02 us  [shards(): lax.all_gather(basis_vectors, 'row', axis=0, tiled=True, axis_index_group...]
    all_gather x0 -> x4, blocking collectives: none -> 117 us  [all_columns(): lax.all_gather(basis[i * half:(i + 1) * half], ('col', 'sub'), axis=0)]
    all_to_all x3 -> x1, waiting for transfers between devices: 93 us -> 23.3 us  [shards(): lax.all_to_all(partial, 'row', 0, 0, tiled=True, axis_index_groups=far_gr...]
    all_to_all x1, blocking collectives: 74.3 us -> 16.7 us  [shards(): lax.all_to_all(partial, 'row', 0, 0, tiled=True, axis_index_groups=near_g...]
    ppermute x0 -> x10, starting transfers between devices: none -> 36.8 us  [the longest x4 19.7 us: shifted(): lax.ppermute(array, axis, [(i, (i + step) % size) for i in range(size)])]
    dot_general x2 -> x9, matrix products: 7.56 us -> 17.1 us  [product(): lax.dot_general(left, right, (contract, ((), ())), precision=PRECISION, p...]
    all_gather x0 -> x4, local copies, waits for them, and re-layouts: none -> 8.25 us  [all_columns(): lax.all_gather(basis[i * half:(i + 1) * half], ('col', 'sub'), axis=0)]
    ppermute x0 -> x10, waiting for transfers between devices: none -> 6.49 us  [the longest x6 6.48 us: swapped(): return lax.ppermute(array, axis, [(i, i ^ 1) for i in range(size)])]
  transfers between devices with their start and end apart: 4 -> 12, of which waited for: 4 -> 2; matrix products, arithmetic and copies ran while one was open for 0% -> 11% of each run, Pallas kernels for 0% -> 0%
where the time goes in v1:
time: 286 us; the launch traced here: 284 us
  blocking collectives  142 us (50%)
  starting transfers between devices  61.3 us (21%)
  waiting for transfers between devices  30.5 us (11%)
  matrix products  17.1 us (6%)
  between operations  14.5 us (5%)
  local copies, waits for them, and re-layouts  14.2 us (5%)
  other arithmetic  4.92 us (2%)
    all_gather x4, blocking collectives, all_columns(): lax.all_gather(basis[i * half:(i + 1) * half], ('col', 'sub'), axis=0)  117 us
    all_to_all x1, starting transfers between devices, shards(): lax.all_to_all(partial, 'row', 0, 0, tiled=True, axis_index_groups=far_gr...  24.5 us
    all_to_all x1, waiting for transfers between devices, shards(): lax.all_to_all(partial, 'row', 0, 0, tiled=True, axis_index_groups=far_gr...  23.3 us
    ppermute x4, starting transfers between devices, shifted(): lax.ppermute(array, axis, [(i, (i + step) % size) for i in range(size)])  19.7 us
    dot_general x9, matrix products, product(): lax.dot_general(left, right, (contract, ((), ())), precision=PRECISION, p...  17.1 us
    ppermute x6, starting transfers between devices, swapped(): return lax.ppermute(array, axis, [(i, i ^ 1) for i in range(size)])  17.1 us
    all_to_all x1, blocking collectives, shards(): lax.all_to_all(partial, 'row', 0, 0, tiled=True, axis_index_groups=near_g...  16.7 us
    all_gather x4, local copies, waits for them, and re-layouts, all_columns(): lax.all_gather(basis[i * half:(i + 1) * half], ('col', 'sub'), axis=0)  8.25 us
  transfers between devices with their start and end apart: 12, of which 2 were waited for; matrix products, arithmetic and copies ran while one was open for 11% of the time, Pallas kernels for 0%

profile of v1, /device:TPU:33, one launch (start us, length us, event | category | flops | bytes accessed | tf_op | source)
XLA Modules:
  0.0 284.1 jit_solution(17117127371487717278)
XLA Ops:
  7.3 2.1 reshape.32
  9.4 3.5 %fusion.14 = (f32[256,2,256]{2,1,0:T(2,128)S(1)}, f32[256,2,256]{2,1,0:T(2,128)S(1)}) fusion(pred[]{:T(512)S(6)} %eq.14, f32[256,2,2,256]{3,2,1,0:T(2,128)S(1)} %reshape.32), kind=kLoop, calls=%fused_computation.19 | loop fusion | flops 262144 | bytes 2097153 | tf_op jit(solution)/shard_map/jit(_where)/select_n | solution.py:48
  13.0 5.3 %collective-permute-start.1 = (f32[256,512]{1,0:T(8,128)S(1)}, f32[256,512]{1,0:T(8,128)S(1)}, u32[]{:S(2)}, u32[]{:S(2)}) collective-permute-start(f32[256,512]{1,0:T(8,128)S(1)} %bitcast.36), channel_id=1, source_target_pairs={{0,8},{8,0},{16,24},{24,16},{32,40},{40,32},{48,56},{56,48},{64,72... | collective-permute-start | bytes 1572872 | tf_op jit(solution)/shard_map/ppermute | solution.py:17
  18.4 6.5 %collective-permute-done.1 = f32[256,512]{1,0:T(8,128)S(1)} collective-permute-done((f32[256,512]{1,0:T(8,128)S(1)}, f32[256,512]{1,0:T(8,128)S(1)}, u32[]{:S(2)}, u32[]{:S(2)}) %collective-permute-start.1) | collective-permute-done | bytes 524320 | tf_op jit(solution)/shard_map/ppermute | solution.py:17
  24.9 8.4 %collective-permute-start.3 = (f32[512,512]{1,0:T(8,128)S(1)}, f32[512,512]{1,0:T(8,128)S(1)}, u32[]{:S(2)}, u32[]{:S(2)}) collective-permute-start(f32[512,512]{1,0:T(8,128)S(1)} %constant_dynamic-update-slice_fusion), channel_id=1, source_target_pairs={{0,2},{2,4},{4,6},{6,0},{1,3},{3,5},{5,7},{7,1},{8,10},{10,12},{12... | collective-permute-start | bytes 3145736 | tf_op jit(solution)/shard_map/ppermute | solution.py:12
  33.3 3.5 %collective-permute-start.6 = (f32[512,512]{1,0:T(8,128)S(1)}, f32[512,512]{1,0:T(8,128)S(1)}, u32[]{:S(2)}, u32[]{:S(2)}) collective-permute-start(f32[512,512]{1,0:T(8,128)S(1)} %constant_dynamic-update-slice_fusion), channel_id=1, source_target_pairs={{0,6},{2,0},{4,2},{6,4},{1,7},{3,1},{5,3},{7,5},{8,14},{10,8},{12,... | collective-permute-start | bytes 3145736 | tf_op jit(solution)/shard_map/ppermute | solution.py:12
  36.8 3.1 %collective-permute-start = (f32[256,128]{1,0:T(8,128)S(1)}, f32[256,128]{1,0:T(8,128)S(1)}, u32[]{:S(2)}, u32[]{:S(2)}) collective-permute-start(f32[256,128]{1,0:T(8,128)S(1)} %copy-done.5), channel_id=1, source_target_pairs={{0,8},{8,0},{16,24},{24,16},{32,40},{40,32},{48,56},{56,48},{64,72... | collective-permute-start | bytes 393224 | tf_op jit(solution)/shard_map/ppermute | solution.py:17
  39.9 57.4 %all-gather = f32[1024,128]{1,0:T(8,128)} all-gather(f32[128,128]{1,0:T(8,128)S(1)} %get-tuple-element.11), channel_id=2, replica_groups=mesh['groups'=2,'row'=32,'col'=4,'sub'=2] {'col','sub'}, dimensions={0}, use_global_device_ids=true | all-gather | bytes 589824 | tf_op jit(solution)/shard_map/all_gather | solution.py:28
  98.1 4.4 %collective-permute-start.5 = (f32[256,512]{1,0:T(8,128)}, f32[256,512]{1,0:T(8,128)}, u32[]{:S(2)}, u32[]{:S(2)}) collective-permute-start(f32[256,512]{1,0:T(8,128)} %slice.38), channel_id=1, source_target_pairs={{0,2},{2,4},{4,6},{6,0},{1,3},{3,5},{5,7},{7,1},{8,10},{10,12},{12... | collective-permute-start | bytes 1572872 | tf_op jit(solution)/shard_map/ppermute | solution.py:12
  102.5 23.2 %all-gather.1 = f32[1024,128]{1,0:T(8,128)} all-gather(f32[128,128]{1,0:T(8,128)S(1)} %get-tuple-element.12), channel_id=3, replica_groups=mesh['groups'=2,'row'=32,'col'=4,'sub'=2] {'col','sub'}, dimensions={0}, use_global_device_ids=true | all-gather | bytes 589824 | tf_op jit(solution)/shard_map/all_gather | solution.py:28
  125.8 2.1 copy.13
  127.8 2.1 copy.14
  129.9 3.4 %collective-permute-start.7 = (f32[256,512]{1,0:T(8,128)S(1)}, f32[256,512]{1,0:T(8,128)S(1)}, u32[]{:S(2)}, u32[]{:S(2)}) collective-permute-start(f32[256,512]{1,0:T(8,128)S(1)} %slice.39), channel_id=1, source_target_pairs={{0,6},{2,0},{4,2},{6,4},{1,7},{3,1},{5,3},{7,5},{8,14},{10,8},{12,... | collective-permute-start | bytes 1572872 | tf_op jit(solution)/shard_map/ppermute | solution.py:12
  133.4 21.8 %all-gather.2 = f32[1024,128]{1,0:T(8,128)} all-gather(f32[128,128]{1,0:T(8,128)S(1)} %get-tuple-element.13), channel_id=4, replica_groups=mesh['groups'=2,'row'=32,'col'=4,'sub'=2] {'col','sub'}, dimensions={0}, use_global_device_ids=true | all-gather | bytes 589824 | tf_op jit(solution)/shard_map/all_gather | solution.py:28
  155.1 2.1 collective-permute-start.2
  157.3 1.9 constant_dynamic-update-slice_fusion.3
  160.0 2.3 collective-permute-start.8
  162.2 14.5 %all-gather.3 = f32[1024,128]{1,0:T(8,128)} all-gather(f32[128,128]{1,0:T(8,128)S(1)} %get-tuple-element.14), channel_id=5, replica_groups=mesh['groups'=2,'row'=32,'col'=4,'sub'=2] {'col','sub'}, dimensions={0}, use_global_device_ids=true | all-gather | bytes 589824 | tf_op jit(solution)/shard_map/all_gather | solution.py:28
  176.8 2.1 copy.15
  178.8 2.1 copy.16
  180.9 2.1 collective-permute-start.4
  183.0 2.3 collective-permute-start.9
  185.3 2.1 fusion.23
  187.4 2.3 fusion.20
  190.7 2.2 fusion.25
  192.9 2.2 fusion.18
  196.2 2.4 fusion.11
  198.6 2.2 fusion.8
  202.7 16.7 %all_to_all.10 = f32[4,8,32,128]{3,2,1,0:T(8,128)S(1)} all-to-all(f32[4,8,32,128]{3,2,1,0:T(8,128)S(1)} %bitcast.35), channel_id=1, replica_groups={{0,8,16,24},{32,40,48,56},{64,72,80,88},{96,104,112,120},{128,136,144,1..., dimensions={0} | all-to-all | bytes 1048576 | tf_op jit(solution)/shard_map/all_to_all | solution.py:79
  220.1 24.5 %all-to-all-start.1 = ((f32[8,32,128]{2,1,0:T(8,128)}), f32[8,32,128]{2,1,0:T(8,128)S(1)}, u32[]{:S(2)}, u32[]{:S(2)}) async-start(f32[8,32,128]{2,1,0:T(8,128)} %reduce_sum.18), calls=%async_computation.1 | async-start | bytes 262144 | tf_op jit(solution)/shard_map/all_to_all | solution.py:82
  245.3 23.3 %all-to-all-done.1 = f32[8,32,128]{2,1,0:T(8,128)S(1)} async-done(((f32[8,32,128]{2,1,0:T(8,128)}), f32[8,32,128]{2,1,0:T(8,128)S(1)}, u32[]{:S(2)}, u32[]{:S(2)}) %all-to-all-start.1) | async-done | bytes 131104 | tf_op jit(solution)/shard_map/all_to_all | solution.py:82
  268.5 8.0 %all_gather.39 = f32[32,256]{1,0:T(8,128)S(1)} all-gather(f32[32,128]{1,0:T(8,128)S(1)} %reduce_sum.19), channel_id=1, replica_groups=mesh['groups'=2,'row'=32,'col'=4,'sub'=2] {'sub'}, dimensions={1}, use_global_device_ids=true | all-gather | bytes 49152 | tf_op jit(solution)/shard_map/all_gather | solution.py:86
  (42 shorter events, 7.9 us)
Async XLA Ops:
  6.5 178.8 %all-gather.6.cloned.1.call-start = ((), (), s32[]{:S(2)}) async-start(), calls=%async_computation.2 | async-start | bytes 2228224 | tf_op jit(solution)/shard_map/all_gather | solution.py:42
  13.0 23.8 %copy-start.5 = (f32[256,128]{1,0:T(8,128)S(1)}, f32[256,128]{1,0:T(8,128)}, u32[]{:S(2)}) copy-start(f32[256,128]{1,0:T(8,128)} %param.4) | copy-start | bytes 393220
  13.0 11.8 %collective-permute-start.1 = (f32[256,512]{1,0:T(8,128)S(1)}, f32[256,512]{1,0:T(8,128)S(1)}, u32[]{:S(2)}, u32[]{:S(2)}) collective-permute-start(f32[256,512]{1,0:T(8,128)S(1)} %bitcast.36), channel_id=1, source_target_pairs={{0,8},{8,0},{16,24},{24,16},{32,40},{40,32},{48,56},{56,48},{64,72... | collective-permute-start | bytes 1572872 | tf_op jit(solution)/shard_map/ppermute | solution.py:17
  24.9 72.4 %collective-permute-start.3 = (f32[512,512]{1,0:T(8,128)S(1)}, f32[512,512]{1,0:T(8,128)S(1)}, u32[]{:S(2)}, u32[]{:S(2)}) collective-permute-start(f32[512,512]{1,0:T(8,128)S(1)} %constant_dynamic-update-slice_fusion), channel_id=1, source_target_pairs={{0,2},{2,4},{4,6},{6,0},{1,3},{3,5},{5,7},{7,1},{8,10},{10,12},{12... | collective-permute-start | bytes 3145736 | tf_op jit(solution)/shard_map/ppermute | solution.py:12
  33.3 96.6 %collective-permute-start.6 = (f32[512,512]{1,0:T(8,128)S(1)}, f32[512,512]{1,0:T(8,128)S(1)}, u32[]{:S(2)}, u32[]{:S(2)}) collective-permute-start(f32[512,512]{1,0:T(8,128)S(1)} %constant_dynamic-update-slice_fusion), channel_id=1, source_target_pairs={{0,6},{2,0},{4,2},{6,4},{1,7},{3,1},{5,3},{7,5},{8,14},{10,8},{12,... | collective-permute-start | bytes 3145736 | tf_op jit(solution)/shard_map/ppermute | solution.py:12
  36.8 96.5 %collective-permute-start = (f32[256,128]{1,0:T(8,128)S(1)}, f32[256,128]{1,0:T(8,128)S(1)}, u32[]{:S(2)}, u32[]{:S(2)}) collective-permute-start(f32[256,128]{1,0:T(8,128)S(1)} %copy-done.5), channel_id=1, source_target_pairs={{0,8},{8,0},{16,24},{24,16},{32,40},{40,32},{48,56},{56,48},{64,72... | collective-permute-start | bytes 393224 | tf_op jit(solution)/shard_map/ppermute | solution.py:17
  98.1 59.1 %collective-permute-start.5 = (f32[256,512]{1,0:T(8,128)}, f32[256,512]{1,0:T(8,128)}, u32[]{:S(2)}, u32[]{:S(2)}) collective-permute-start(f32[256,512]{1,0:T(8,128)} %slice.38), channel_id=1, source_target_pairs={{0,2},{2,4},{4,6},{6,0},{1,3},{3,5},{5,7},{7,1},{8,10},{10,12},{12... | collective-permute-start | bytes 1572872 | tf_op jit(solution)/shard_map/ppermute | solution.py:12
  129.9 29.2 %collective-permute-start.7 = (f32[256,512]{1,0:T(8,128)S(1)}, f32[256,512]{1,0:T(8,128)S(1)}, u32[]{:S(2)}, u32[]{:S(2)}) collective-permute-start(f32[256,512]{1,0:T(8,128)S(1)} %slice.39), channel_id=1, source_target_pairs={{0,6},{2,0},{4,2},{6,4},{1,7},{3,1},{5,3},{7,5},{8,14},{10,8},{12,... | collective-permute-start | bytes 1572872 | tf_op jit(solution)/shard_map/ppermute | solution.py:12
  155.1 35.6 %collective-permute-start.2 = (f32[512,512]{1,0:T(8,128)S(1)}, f32[512,512]{1,0:T(8,128)}, u32[]{:S(2)}, u32[]{:S(2)}) collective-permute-start(f32[512,512]{1,0:T(8,128)S(1)} %constant_dynamic-update-slice_fusion), channel_id=1, source_target_pairs={{0,1},{1,0},{2,3},{3,2},{4,5},{5,4},{6,7},{7,6},{8,9},{9,8},{10,11... | collective-permute-start | bytes 3145736 | tf_op jit(solution)/shard_map/ppermute | solution.py:17
  160.0 33.0 %collective-permute-start.8 = (f32[512,512]{1,0:T(8,128)}, f32[512,512]{1,0:T(8,128)}, u32[]{:S(2)}, u32[]{:S(2)}) collective-permute-start(f32[512,512]{1,0:T(8,128)} %constant_dynamic-update-slice_fusion.2), channel_id=1, source_target_pairs={{0,1},{1,0},{2,3},{3,2},{4,5},{5,4},{6,7},{7,6},{8,9},{9,8},{10,11... | collective-permute-start | bytes 3145736 | tf_op jit(solution)/shard_map/ppermute | solution.py:17
  180.9 15.3 %collective-permute-start.4 = (f32[512,512]{1,0:T(8,128)S(1)}, f32[512,512]{1,0:T(8,128)}, u32[]{:S(2)}, u32[]{:S(2)}) collective-permute-start(f32[512,512]{1,0:T(8,128)S(1)} %collective-permute-done.3), channel_id=1, source_target_pairs={{0,1},{1,0},{2,3},{3,2},{4,5},{5,4},{6,7},{7,6},{8,9},{9,8},{10,11... | collective-permute-start | bytes 3145736 | tf_op jit(solution)/shard_map/ppermute | solution.py:17
  183.0 15.6 %collective-permute-start.9 = (f32[512,512]{1,0:T(8,128)S(1)}, f32[512,512]{1,0:T(8,128)}, u32[]{:S(2)}, u32[]{:S(2)}) collective-permute-start(f32[512,512]{1,0:T(8,128)S(1)} %collective-permute-done.6), channel_id=1, source_target_pairs={{0,1},{1,0},{2,3},{3,2},{4,5},{5,4},{6,7},{7,6},{8,9},{9,8},{10,11... | collective-permute-start | bytes 3145736 | tf_op jit(solution)/shard_map/ppermute | solution.py:17
  185.3 4.4 %copy-start = (f32[4096,128]{1,0:T(8,128)S(1)}, f32[4096,128]{1,0:T(8,128)}, u32[]{:S(2)}) copy-start(f32[4096,128]{1,0:T(8,128)} %all-gather.6.cloned.1.call-done) | copy-start | bytes 6291460
  196.2 4.7 %copy-start.1 = (f32[8,128,128]{1,2,0:T(8,128)S(1)}, f32[8,128,128]{1,2,0:T(8,128)}, u32[]{:S(2)}) copy-start(f32[8,128,128]{1,2,0:T(8,128)} %copy.13) | copy-start | bytes 1572868
  196.2 4.7 %copy-start.2 = (f32[8,128,128]{1,2,0:T(8,128)S(1)}, f32[8,128,128]{1,2,0:T(8,128)}, u32[]{:S(2)}) copy-start(f32[8,128,128]{1,2,0:T(8,128)} %copy.14) | copy-start | bytes 1572868
  196.2 4.7 %copy-start.3 = (f32[8,128,128]{1,2,0:T(8,128)S(1)}, f32[8,128,128]{1,2,0:T(8,128)}, u32[]{:S(2)}) copy-start(f32[8,128,128]{1,2,0:T(8,128)} %copy.15) | copy-start | bytes 1572868
  196.2 4.7 %copy-start.4 = (f32[8,128,128]{1,2,0:T(8,128)S(1)}, f32[8,128,128]{1,2,0:T(8,128)}, u32[]{:S(2)}) copy-start(f32[8,128,128]{1,2,0:T(8,128)} %copy.16) | copy-start | bytes 1572868
  220.1 48.4 %all-to-all-start.1 = ((f32[8,32,128]{2,1,0:T(8,128)}), f32[8,32,128]{2,1,0:T(8,128)S(1)}, u32[]{:S(2)}, u32[]{:S(2)}) async-start(f32[8,32,128]{2,1,0:T(8,128)} %reduce_sum.18), calls=%async_computation.1 | async-start | bytes 262144 | tf_op jit(solution)/shard_map/all_to_all | solution.py:82
Sparse Core Ops, SparseCore 0:
  9.4 125.4 all-gather.5

commit v2 on v1

v2 whole, which is shorter than its diff:
```python
import functools

import jax
import jax.numpy as jnp
from jax import lax
from jax.experimental import pallas as pl
from jax.experimental.pallas import tpu as pltpu
from jax.sharding import PartitionSpec as P


NEAR = 4
STEPS = 4


def shifted(array, axis, step):
    size = lax.axis_size(axis)
    return lax.ppermute(array, axis, [(i, (i + step) % size) for i in range(size)])


def swapped(array, axis):
    size = lax.axis_size(axis)
    return lax.ppermute(array, axis, [(i, i ^ 1) for i in range(size)])


def halves(value):
    high = value.astype(jnp.bfloat16)
    low = (value - high.astype(jnp.float32)).astype(jnp.bfloat16)
    return high, low


def dot(left, right):
    return jnp.dot(left, right, preferred_element_type=jnp.float32)


def project_kernel(starts, strip, basis_t, *refs, n_whole, near):
    whole, (top, bottom), (top_o, bottom_o) = refs[:n_whole], refs[n_whole : n_whole + 2], refs[n_whole + 2 : n_whole + 4]
    out, strip2, image2 = refs[n_whole + 4 :]
    step = pl.program_id(0)
    steps = pl.num_programs(0)
    wide = strip.shape[1]
    tile, span = whole[0].shape

    @pl.when(step == 0)
    def _():
        high, low = halves(strip[...])
        strip2[:, :wide] = high
        strip2[:, wide:] = low

    first = step < steps // 2
    pieces = [ref[...] for ref in whole]
    pieces.append(jnp.where(first, top[...], bottom[...]))
    pieces.append(jnp.where(first, top_o[...], bottom_o[...]))
    both = jnp.zeros((tile, 2 * wide), jnp.float32)
    rest = jnp.zeros((tile, wide), jnp.float32)
    for n, piece in enumerate(pieces):
        high, low = halves(piece)
        start = pl.multiple_of(starts[n] * span, span)
        both += dot(high, strip2[pl.ds(start, span), :])
        rest += dot(low, strip2[pl.ds(start, span), :wide])
    high, low = halves(both[:, :wide] + (both[:, wide:] + rest))
    image2[pl.ds(pl.multiple_of(step * tile, tile), tile), :wide] = high
    image2[pl.ds(pl.multiple_of(step * tile, tile), tile), wide:] = low

    @pl.when(step == steps - 1)
    def _():
        high, low = halves(basis_t[...])
        both = dot(high, image2[...])
        proj = both[:, :wide] + (both[:, wide:] + dot(low, image2[:, :wide]))
        far, share = out.shape[1], out.shape[2]
        for f in range(far):
            for q in range(near):
                begin = (f * near + q) * share
                out[q, f] = proj[begin : begin + share]


def projected(starts, strip, basis_t, whole, across, across_other, share):
    rows, span = whole[0].shape
    tile = rows // STEPS
    total, wide = basis_t.shape[0], strip.shape[1]
    last = STEPS // 2 - 1
    far = total // share // NEAR
    tiled = pl.BlockSpec((tile, span), lambda i, s: (i, 0))
    low = pl.BlockSpec((tile, span), lambda i, s: (jnp.minimum(i, last), 0))
    high = pl.BlockSpec((tile, span), lambda i, s: (jnp.maximum(i - last - 1, 0), 0))
    fixed = lambda shape: pl.BlockSpec(shape, lambda i, s: (0,) * len(shape))
    out_shape = (NEAR, far, share, wide)
    return pl.pallas_call(
        functools.partial(project_kernel, n_whole=len(whole), near=NEAR),
        grid_spec=pltpu.PrefetchScalarGridSpec(
            num_scalar_prefetch=1,
            grid=(STEPS,),
            in_specs=[fixed(strip.shape), fixed(basis_t.shape)]
            + [tiled] * len(whole)
            + [low, high, low, high],
            out_specs=fixed(out_shape),
            scratch_shapes=[
                pltpu.VMEM((strip.shape[0], 2 * wide), jnp.bfloat16),
                pltpu.VMEM((rows, 2 * wide), jnp.bfloat16),
            ],
        ),
        out_shape=jax.ShapeDtypeStruct(out_shape, jnp.float32),
        compiler_params=pltpu.CompilerParams(
            dimension_semantics=("arbitrary",), vmem_limit_bytes=40 * 2**20
        ),
        cost_estimate=pl.CostEstimate(
            flops=3 * 2 * rows * wide * (strip.shape[0] + total),
            bytes_accessed=4 * (strip.size + basis_t.size + rows * strip.shape[0]),
            transcendentals=0,
        ),
        name="project",
    )(starts, strip, basis_t, *whole, *across, *across_other)


def split_projection(matrix, basis_vectors, split_size):
    block, width = matrix.shape
    n_row = lax.axis_size("row")
    n_col = lax.axis_size("col")
    row = lax.axis_index("row")
    col = lax.axis_index("col")
    sub = lax.axis_index("sub")
    even = row % 2 == 0

    every_other = [[first + 2 * i for i in range(n_row // 2)] for first in range(2)]
    strip = lax.all_gather(
        basis_vectors, "row", axis=0, tiled=True, axis_index_groups=every_other
    )

    mate = swapped(basis_vectors, "row")
    pair_t = jnp.concatenate([basis_vectors, mate], axis=0).T
    pair_t = jnp.broadcast_to(pair_t[None], (n_col * lax.axis_size("sub"), *pair_t.shape))

    blocks = [matrix[:, i * block : (i + 1) * block] for i in range(width // block)]
    keep = jnp.concatenate(
        [jnp.where(even, a, b) for a, b in zip(blocks[::2], blocks[1::2])], axis=1
    )
    give = jnp.concatenate(
        [jnp.where(even, b, a) for a, b in zip(blocks[::2], blocks[1::2])], axis=1
    )
    basis_t = lax.all_to_all(pair_t, ("col", "sub"), 0, 0, tiled=True).reshape(-1, 2 * block)
    received = swapped(give, "row")
    own = jnp.concatenate([keep, received], axis=0)

    before = shifted(own, "col", 1)
    after = shifted(own, "col", -1)
    across = (shifted(before[:block], "col", 1), shifted(after[block:], "col", -1))
    mine = [own, before, after]
    theirs = [swapped(piece, "sub") for piece in mine]
    across_other = tuple(swapped(piece, "sub") for piece in across)

    sources = [col, (col - 1) % n_col, (col + 1) % n_col]
    opposite = (col + 2) % n_col
    starts = jnp.stack(
        [2 * s + sub for s in sources]
        + [2 * s + 1 - sub for s in sources]
        + [2 * opposite + sub, 2 * opposite + 1 - sub]
    ).astype(jnp.int32)
    share = basis_t.shape[0] // n_row
    partial = projected(starts, strip, basis_t, mine + theirs, across, across_other, share)

    far = n_row // NEAR
    near_groups = [[NEAR * g + q for q in range(NEAR)] for g in range(far)]
    far_groups = [[NEAR * g + q for g in range(far)] for q in range(NEAR)]
    partial = lax.all_to_all(
        partial, "row", 0, 0, tiled=True, axis_index_groups=near_groups
    ).sum(0)
    proj_block = lax.all_to_all(
        partial, "row", 0, 0, tiled=True, axis_index_groups=far_groups
    ).sum(0)

    child_block = lax.all_gather(proj_block, "sub", axis=1, tiled=True)
    row_ids = jnp.arange(child_block.shape[0], dtype=jnp.int32) + row * child_block.shape[0]
    col_ids = jnp.arange(child_block.shape[1], dtype=jnp.int32) + col * child_block.shape[1]
    leading = split_size[0]
    row_first = row_ids < leading
    col_first = col_ids < leading
    mask_one = row_first[:, None] & col_first[None, :]
    mask_two = jnp.logical_not(row_first)[:, None] & jnp.logical_not(col_first)[None, :]
    selected = jnp.where(sub == 0, mask_one, mask_two)
    return jnp.where(selected, child_block, jnp.zeros((), jnp.float32))[None]


def solution(mesh):
    placed = (
        P(("groups", "row"), ("col", "sub")),
        P(("groups", "row"), ("col", "sub")),
        P("groups"),
    )
    return jax.shard_map(
        split_projection,
        mesh=mesh,
        in_specs=placed,
        out_specs=P("sub", ("groups", "row"), "col"),
        check_vma=False,
    )
```

time: 286 us -> 210 us (0.73)
  blocking collectives: 142 us -> 17.1 us
  waiting for transfers between devices: 30.5 us -> 66.2 us
  starting transfers between devices: 61.3 us -> 96 us
  matrix products: 17.1 us -> 0 us
  local copies, waits for them, and re-layouts: 14.2 us -> 5.55 us
  Pallas kernels: 0 us -> 7.03 us
    all_gather x5 -> x1, blocking collectives: 125 us -> 5.29 us  [split_projection(): child_block = lax.all_gather(proj_block, 'sub', axis=1, tiled=True)]
    all_to_all x1 -> x2, starting transfers between devices: 24.5 us -> 57.6 us  [the longest x1 40.3 us: split_projection(): lax.all_to_all(pair_t, ('col', 'sub'), 0, 0, tiled=True)]
    ppermute x4, waiting for transfers between devices: 0.01 us -> 20.7 us  [shifted(): lax.ppermute(array, axis, [(i, (i + step) % size) for i in range(size)])]
    dot_general x9 -> x0, matrix products: 17.1 us -> none  [product(): lax.dot_general(left, right, (contract, ((), ())), precision=PRECISION, p...]
    all_gather x4 -> x0, local copies, waits for them, and re-layouts: 8.25 us -> none  [all_columns(): lax.all_gather(basis[i * half:(i + 1) * half], ('col', 'sub'), axis=0)]
    all_gather x1, waiting for transfers between devices: 0.02 us -> 8.15 us  [split_projection(): lax.all_gather(basis_vectors, 'row', axis=0, tiled=True, axis_index_group...]
    pallas_call x0 -> x1, Pallas kernels: none -> 7.03 us  [projected(): pl.pallas_call(functools.partial(project_kernel, n_whole=len(whole), near...]
    all_to_all x1, blocking collectives: 16.7 us -> 11.8 us  [split_projection(): lax.all_to_all(partial, 'row', 0, 0, tiled=True, axis_index_groups=near_g...]
  transfers between devices with their start and end apart: 12 -> 14, of which waited for: 2 -> 6; matrix products, arithmetic and copies ran while one was open for 11% -> 3% of each run, Pallas kernels for 0% -> 0%
where the time goes in v2:
time: 210 us; the launch traced here: 209 us
  starting transfers between devices  96 us (46%)
  waiting for transfers between devices  66.2 us (32%)
  blocking collectives  17.1 us (8%)
  between operations  14.3 us (7%)
  Pallas kernels  7.03 us (3%)
  local copies, waits for them, and re-layouts  5.55 us (3%)
  other arithmetic  2.86 us (1%)
    all_to_all x1, starting transfers between devices, split_projection(): lax.all_to_all(pair_t, ('col', 'sub'), 0, 0, tiled=True)  40.3 us
    all_to_all x1, waiting for transfers between devices, split_projection(): lax.all_to_all(partial, 'row', 0, 0, tiled=True, axis_index_groups=far_gr...  25.4 us
    ppermute x4, waiting for transfers between devices, shifted(): lax.ppermute(array, axis, [(i, (i + step) % size) for i in range(size)])  20.7 us
    ppermute x7, starting transfers between devices, swapped(): return lax.ppermute(array, axis, [(i, i ^ 1) for i in range(size)])  19.8 us
    ppermute x4, starting transfers between devices, shifted(): lax.ppermute(array, axis, [(i, (i + step) % size) for i in range(size)])  18.5 us
    all_to_all x1, starting transfers between devices, split_projection(): lax.all_to_all(partial, 'row', 0, 0, tiled=True, axis_index_groups=far_gr...  17.4 us
    all_to_all x1, blocking collectives, split_projection(): lax.all_to_all(partial, 'row', 0, 0, tiled=True, axis_index_groups=near_g...  11.8 us
    ppermute x7, waiting for transfers between devices, swapped(): return lax.ppermute(array, axis, [(i, i ^ 1) for i in range(size)])  11.2 us
  transfers between devices with their start and end apart: 14, of which 6 were waited for; matrix products, arithmetic and copies ran while one was open for 3% of the time, Pallas kernels for 0%

profile of v2, /device:TPU:33, one launch (start us, length us, event | category | flops | bytes accessed | tf_op | source)
XLA Modules:
  0.0 209.1 jit_solution(12649734553469806093)
XLA Ops:
  6.6 0.7 all-gather.2.cloned.1.call-update
  7.3 1.3 slice_select_fusion.3
  8.7 5.3 %collective-permute-start.1 = (f32[256,512]{1,0:T(8,128)S(1)}, f32[256,512]{1,0:T(8,128)S(1)}, u32[]{:S(2)}, u32[]{:S(2)}) collective-permute-start(f32[256,512]{1,0:T(8,128)S(1)} %pad_maximum_fusion.1), channel_id=1, source_target_pairs={{0,8},{8,0},{16,24},{24,16},{32,40},{40,32},{48,56},{56,48},{64,72... | collective-permute-start | bytes 1572872 | tf_op jit(solution)/shard_map/ppermute | solution.py:22
  13.9 6.6 %collective-permute-done.1 = f32[256,512]{1,0:T(8,128)S(1)} collective-permute-done((f32[256,512]{1,0:T(8,128)S(1)}, f32[256,512]{1,0:T(8,128)S(1)}, u32[]{:S(2)}, u32[]{:S(2)}) %collective-permute-start.1) | collective-permute-done | bytes 524320 | tf_op jit(solution)/shard_map/ppermute | solution.py:22
  20.5 0.1 pad_maximum_fusion.refs_0_
  20.6 9.9 %collective-permute-start.3 = (f32[512,512]{1,0:T(8,128)S(1)}, f32[512,512]{1,0:T(8,128)}, u32[]{:S(2)}, u32[]{:S(2)}) collective-permute-start(f32[512,512]{1,0:T(8,128)S(1)} %pad_maximum_fusion.refs_0_), channel_id=1, source_target_pairs={{0,6},{2,0},{4,2},{6,4},{1,7},{3,1},{5,3},{7,5},{8,14},{10,8},{12,... | collective-permute-start | bytes 3145736 | tf_op jit(solution)/shard_map/ppermute | solution.py:17
  30.6 2.0 collective-permute-start.2
  32.5 3.1 %collective-permute-start = (f32[256,128]{1,0:T(8,128)S(1)}, f32[256,128]{1,0:T(8,128)S(1)}, u32[]{:S(2)}, u32[]{:S(2)}) collective-permute-start(f32[256,128]{1,0:T(8,128)S(1)} %copy-done.1), channel_id=1, source_target_pairs={{0,8},{8,0},{16,24},{24,16},{32,40},{40,32},{48,56},{56,48},{64,72... | collective-permute-start | bytes 393224 | tf_op jit(solution)/shard_map/ppermute | solution.py:22
  35.6 2.6 %collective-permute-done = f32[256,128]{1,0:T(8,128)S(1)} collective-permute-done((f32[256,128]{1,0:T(8,128)S(1)}, f32[256,128]{1,0:T(8,128)S(1)}, u32[]{:S(2)}, u32[]{:S(2)}) %collective-permute-start) | collective-permute-done | bytes 131104 | tf_op jit(solution)/shard_map/ppermute | solution.py:22
  38.3 0.1 copy.5
  38.4 1.6 broadcast_in_dim.7
  40.0 40.3 %all-to-all-start = ((f32[8,128,512]{2,1,0:T(8,128)}), f32[8,128,512]{2,1,0:T(8,128)S(1)}, u32[]{:S(2)}, u32[]{:S(2)}) async-start(f32[8,128,512]{2,1,0:T(8,128)} %broadcast_in_dim.7), calls=%async_computation | async-start | bytes 4194304 | tf_op jit(solution)/shard_map/all_to_all | solution.py:139
  80.3 2.2 %collective-permute-start.4 = (f32[512,512]{1,0:T(8,128)S(1)}, f32[512,512]{1,0:T(8,128)}, u32[]{:S(2)}, u32[]{:S(2)}) collective-permute-start(f32[512,512]{1,0:T(8,128)S(1)} %pad_maximum_fusion.refs_0_), channel_id=1, source_target_pairs={{0,1},{1,0},{2,3},{3,2},{4,5},{5,4},{6,7},{7,6},{8,9},{9,8},{10,11... | collective-permute-start | bytes 3145736 | tf_op jit(solution)/shard_map/ppermute | solution.py:22
  82.5 1.1 slice.25
  83.6 4.7 %collective-permute-start.8 = (f32[256,512]{1,0:T(8,128)S(1)}, f32[256,512]{1,0:T(8,128)}, u32[]{:S(2)}, u32[]{:S(2)}) collective-permute-start(f32[256,512]{1,0:T(8,128)S(1)} %slice.25), channel_id=1, source_target_pairs={{0,6},{2,0},{4,2},{6,4},{1,7},{3,1},{5,3},{7,5},{8,14},{10,8},{12,... | collective-permute-start | bytes 1572872 | tf_op jit(solution)/shard_map/ppermute | solution.py:17
  88.3 1.1 slice.24
  89.4 2.0 collective-permute-start.7
  91.4 2.4 %collective-permute-start.5 = (f32[512,512]{1,0:T(8,128)}, f32[512,512]{1,0:T(8,128)}, u32[]{:S(2)}, u32[]{:S(2)}) collective-permute-start(f32[512,512]{1,0:T(8,128)} %collective-permute-done.2.refs_1_), channel_id=1, source_target_pairs={{0,1},{1,0},{2,3},{3,2},{4,5},{5,4},{6,7},{7,6},{8,9},{9,8},{10,11... | collective-permute-start | bytes 3145736 | tf_op jit(solution)/shard_map/ppermute | solution.py:22
  93.7 2.0 collective-permute-start.6
  95.8 20.7 %collective-permute-done.8.refs_7_ = f32[256,512]{1,0:T(8,128)} collective-permute-done((f32[256,512]{1,0:T(8,128)S(1)}, f32[256,512]{1,0:T(8,128)}, u32[]{:S(2)}, u32[]{:S(2)}) %collective-permute-start.8) | collective-permute-done | bytes 524320 | tf_op jit(solution)/shard_map/ppermute | solution.py:17
  116.4 2.9 %collective-permute-start.10 = (f32[256,512]{1,0:T(8,128)}, f32[256,512]{1,0:T(8,128)}, u32[]{:S(2)}, u32[]{:S(2)}) collective-permute-start(f32[256,512]{1,0:T(8,128)} %collective-permute-done.8.refs_7_), channel_id=1, source_target_pairs={{0,1},{1,0},{2,3},{3,2},{4,5},{5,4},{6,7},{7,6},{8,9},{9,8},{10,11... | collective-permute-start | bytes 1572872 | tf_op jit(solution)/shard_map/ppermute | solution.py:22
  119.3 2.0 collective-permute-start.9
  121.4 2.1 collective-permute-done.9.refs_8_
  123.5 8.2 %all-gather.2.cloned.1.call-done.strip = f32[4096,128]{1,0:T(8,128)} async-done(((f32[256,128]{1,0:T(8,128)}), f32[4096,128]{1,0:T(8,128)}) %all-gather.2.cloned.1.call-update) | async-done | bytes 2097168 | tf_op jit(solution)/shard_map/all_gather | solution.py:124
  131.7 1.6 copy-done
  133.3 7.0 %project.1 = f32[4,8,32,128]{3,2,1,0:T(8,128)S(1)} custom-call(s32[8]{0:T(128)S(1)} %stack.35.starts, f32[4096,128]{1,0:T(8,128)S(1)} %copy-done, f32[1024,512]{1,0:T(8,128)S(1)} %bitcast.16, f32[512,512]{1,0:T(8,128)S(1)} %pad_maximum_fusion.refs_0_, f32[512,512]{1,0:T(8,128)} %collective-permute-done.2.refs_1_, f32[512,512]{1,0:T(8,128)} %collective-permute-done.3.refs_2_, ...), custom_call_target="tpu_custom_call" | custom-call | flops 2013265920 | bytes 12582912 | tf_op jit(solution)/shard_map/project/pallas_call | solution.py:87
  140.3 11.8 %all_to_all.15 = f32[4,8,32,128]{3,2,1,0:T(8,128)S(1)} all-to-all(f32[4,8,32,128]{3,2,1,0:T(8,128)S(1)} %project.1), channel_id=1, replica_groups={{0,8,16,24},{32,40,48,56},{64,72,80,88},{96,104,112,120},{128,136,144,1..., dimensions={0} | all-to-all | bytes 1048576 | tf_op jit(solution)/shard_map/all_to_all | solution.py:163
  152.1 0.7 reduce_sum.18
  152.8 17.4 %all-to-all-start.2 = ((f32[8,32,128]{2,1,0:T(8,128)}), f32[8,32,128]{2,1,0:T(8,128)S(1)}, u32[]{:S(2)}, u32[]{:S(2)}) async-start(f32[8,32,128]{2,1,0:T(8,128)} %reduce_sum.18), calls=%async_computation.2 | async-start | bytes 262144 | tf_op jit(solution)/shard_map/all_to_all | solution.py:166
  170.9 25.4 %all-to-all-done.2 = f32[8,32,128]{2,1,0:T(8,128)S(1)} async-done(((f32[8,32,128]{2,1,0:T(8,128)}), f32[8,32,128]{2,1,0:T(8,128)S(1)}, u32[]{:S(2)}, u32[]{:S(2)}) %all-to-all-start.2) | async-done | bytes 131104 | tf_op jit(solution)/shard_map/all_to_all | solution.py:166
  196.3 5.3 %all_gather.7 = f32[32,256]{1,0:T(8,128)S(1)} all-gather(f32[32,128]{1,0:T(8,128)S(1)} %reduce_sum.19), channel_id=1, replica_groups=mesh['groups'=2,'row'=32,'col'=4,'sub'=2] {'sub'}, dimensions={1}, use_global_device_ids=true | all-gather | bytes 49152 | tf_op jit(solution)/shard_map/all_gather | solution.py:170
  201.6 0.7 select_bitcast_fusion
  (18 shorter events, 0.2 us)
Async XLA Ops:
  6.5 125.1 %all-gather.2.cloned.1.call-start = ((), (), s32[]{:S(2)}) async-start(), calls=%async_computation.3 | async-start | bytes 2228224 | tf_op jit(solution)/shard_map/all_gather | solution.py:124
  8.6 23.9 %copy-start.1 = (f32[256,128]{1,0:T(8,128)S(1)}, f32[256,128]{1,0:T(8,128)}, u32[]{:S(2)}) copy-start(f32[256,128]{1,0:T(8,128)} %param.4) | copy-start | bytes 393220
  8.7 11.8 %collective-permute-start.1 = (f32[256,512]{1,0:T(8,128)S(1)}, f32[256,512]{1,0:T(8,128)S(1)}, u32[]{:S(2)}, u32[]{:S(2)}) collective-permute-start(f32[256,512]{1,0:T(8,128)S(1)} %pad_maximum_fusion.1), channel_id=1, source_target_pairs={{0,8},{8,0},{16,24},{24,16},{32,40},{40,32},{48,56},{56,48},{64,72... | collective-permute-start | bytes 1572872 | tf_op jit(solution)/shard_map/ppermute | solution.py:22
  20.6 61.9 %collective-permute-start.3 = (f32[512,512]{1,0:T(8,128)S(1)}, f32[512,512]{1,0:T(8,128)}, u32[]{:S(2)}, u32[]{:S(2)}) collective-permute-start(f32[512,512]{1,0:T(8,128)S(1)} %pad_maximum_fusion.refs_0_), channel_id=1, source_target_pairs={{0,6},{2,0},{4,2},{6,4},{1,7},{3,1},{5,3},{7,5},{8,14},{10,8},{12,... | collective-permute-start | bytes 3145736 | tf_op jit(solution)/shard_map/ppermute | solution.py:17
  30.6 57.8 %collective-permute-start.2 = (f32[512,512]{1,0:T(8,128)S(1)}, f32[512,512]{1,0:T(8,128)}, u32[]{:S(2)}, u32[]{:S(2)}) collective-permute-start(f32[512,512]{1,0:T(8,128)S(1)} %pad_maximum_fusion.refs_0_), channel_id=1, source_target_pairs={{0,2},{2,4},{4,6},{6,0},{1,3},{3,5},{5,7},{7,1},{8,10},{10,12},{12... | collective-permute-start | bytes 3145736 | tf_op jit(solution)/shard_map/ppermute | solution.py:17
  32.5 5.7 %collective-permute-start = (f32[256,128]{1,0:T(8,128)S(1)}, f32[256,128]{1,0:T(8,128)S(1)}, u32[]{:S(2)}, u32[]{:S(2)}) collective-permute-start(f32[256,128]{1,0:T(8,128)S(1)} %copy-done.1), channel_id=1, source_target_pairs={{0,8},{8,0},{16,24},{24,16},{32,40},{40,32},{48,56},{56,48},{64,72... | collective-permute-start | bytes 393224 | tf_op jit(solution)/shard_map/ppermute | solution.py:22
  40.0 81.4 %all-to-all-start = ((f32[8,128,512]{2,1,0:T(8,128)}), f32[8,128,512]{2,1,0:T(8,128)S(1)}, u32[]{:S(2)}, u32[]{:S(2)}) async-start(f32[8,128,512]{2,1,0:T(8,128)} %broadcast_in_dim.7), calls=%async_computation | async-start | bytes 4194304 | tf_op jit(solution)/shard_map/all_to_all | solution.py:139
  80.3 41.1 %collective-permute-start.4 = (f32[512,512]{1,0:T(8,128)S(1)}, f32[512,512]{1,0:T(8,128)}, u32[]{:S(2)}, u32[]{:S(2)}) collective-permute-start(f32[512,512]{1,0:T(8,128)S(1)} %pad_maximum_fusion.refs_0_), channel_id=1, source_target_pairs={{0,1},{1,0},{2,3},{3,2},{4,5},{5,4},{6,7},{7,6},{8,9},{9,8},{10,11... | collective-permute-start | bytes 3145736 | tf_op jit(solution)/shard_map/ppermute | solution.py:22
  83.6 32.8 %collective-permute-start.8 = (f32[256,512]{1,0:T(8,128)S(1)}, f32[256,512]{1,0:T(8,128)}, u32[]{:S(2)}, u32[]{:S(2)}) collective-permute-start(f32[256,512]{1,0:T(8,128)S(1)} %slice.25), channel_id=1, source_target_pairs={{0,6},{2,0},{4,2},{6,4},{1,7},{3,1},{5,3},{7,5},{8,14},{10,8},{12,... | collective-permute-start | bytes 1572872 | tf_op jit(solution)/shard_map/ppermute | solution.py:17
  89.4 29.9 %collective-permute-start.7 = (f32[256,512]{1,0:T(8,128)S(1)}, f32[256,512]{1,0:T(8,128)}, u32[]{:S(2)}, u32[]{:S(2)}) collective-permute-start(f32[256,512]{1,0:T(8,128)S(1)} %slice.24), channel_id=1, source_target_pairs={{0,2},{2,4},{4,6},{6,0},{1,3},{3,5},{5,7},{7,1},{8,10},{10,12},{12... | collective-permute-start | bytes 1572872 | tf_op jit(solution)/shard_map/ppermute | solution.py:17
  91.4 32.1 %collective-permute-start.5 = (f32[512,512]{1,0:T(8,128)}, f32[512,512]{1,0:T(8,128)}, u32[]{:S(2)}, u32[]{:S(2)}) collective-permute-start(f32[512,512]{1,0:T(8,128)} %collective-permute-done.2.refs_1_), channel_id=1, source_target_pairs={{0,1},{1,0},{2,3},{3,2},{4,5},{5,4},{6,7},{7,6},{8,9},{9,8},{10,11... | collective-permute-start | bytes 3145736 | tf_op jit(solution)/shard_map/ppermute | solution.py:22
  93.7 29.8 %collective-permute-start.6 = (f32[512,512]{1,0:T(8,128)}, f32[512,512]{1,0:T(8,128)}, u32[]{:S(2)}, u32[]{:S(2)}) collective-permute-start(f32[512,512]{1,0:T(8,128)} %collective-permute-done.3.refs_2_), channel_id=1, source_target_pairs={{0,1},{1,0},{2,3},{3,2},{4,5},{5,4},{6,7},{7,6},{8,9},{9,8},{10,11... | collective-permute-start | bytes 3145736 | tf_op jit(solution)/shard_map/ppermute | solution.py:22
  116.4 5.0 %collective-permute-start.10 = (f32[256,512]{1,0:T(8,128)}, f32[256,512]{1,0:T(8,128)}, u32[]{:S(2)}, u32[]{:S(2)}) collective-permute-start(f32[256,512]{1,0:T(8,128)} %collective-permute-done.8.refs_7_), channel_id=1, source_target_pairs={{0,1},{1,0},{2,3},{3,2},{4,5},{5,4},{6,7},{7,6},{8,9},{9,8},{10,11... | collective-permute-start | bytes 1572872 | tf_op jit(solution)/shard_map/ppermute | solution.py:22
  119.3 4.2 %collective-permute-start.9 = (f32[256,512]{1,0:T(8,128)}, f32[256,512]{1,0:T(8,128)}, u32[]{:S(2)}, u32[]{:S(2)}) collective-permute-start(f32[256,512]{1,0:T(8,128)} %collective-permute-done.7.refs_6_), channel_id=1, source_target_pairs={{0,1},{1,0},{2,3},{3,2},{4,5},{5,4},{6,7},{7,6},{8,9},{9,8},{10,11... | collective-permute-start | bytes 1572872 | tf_op jit(solution)/shard_map/ppermute | solution.py:22
  131.7 1.6 copy-start
  152.8 43.4 %all-to-all-start.2 = ((f32[8,32,128]{2,1,0:T(8,128)}), f32[8,32,128]{2,1,0:T(8,128)S(1)}, u32[]{:S(2)}, u32[]{:S(2)}) async-start(f32[8,32,128]{2,1,0:T(8,128)} %reduce_sum.18), calls=%async_computation.2 | async-start | bytes 262144 | tf_op jit(solution)/shard_map/all_to_all | solution.py:166
Sparse Core Ops, SparseCore 0:
  9.4 122.1 all-gather.1

commit v3 on v2

--- a/solution.py
+++ b/solution.py
@@ -9,7 +9,7 @@
 
 
 NEAR = 4
-STEPS = 4
+TILE = 256
 
 
 def shifted(array, axis, step):
@@ -32,76 +32,76 @@
     return jnp.dot(left, right, preferred_element_type=jnp.float32)
 
 
-def project_kernel(starts, strip, basis_t, *refs, n_whole, near):
-    whole, (top, bottom), (top_o, bottom_o) = refs[:n_whole], refs[n_whole : n_whole + 2], refs[n_whole + 2 : n_whole + 4]
-    out, strip2, image2 = refs[n_whole + 4 :]
-    step = pl.program_id(0)
-    steps = pl.num_programs(0)
+def project_kernel(starts, strip, basis_t, *refs, n_whole):
+    parts = [(ref,) for ref in refs[:n_whole]]
+    parts += [refs[n_whole : n_whole + 2], refs[n_whole + 2 : n_whole + 4]]
+    out, chunks, tiles, arrived, landed, image = refs[n_whole + 4 :]
     wide = strip.shape[1]
-    tile, span = whole[0].shape
+    span = chunks.shape[1]
+    per_piece = tiles.shape[1] // TILE
 
-    @pl.when(step == 0)
-    def _():
-        high, low = halves(strip[...])
-        strip2[:, :wide] = high
-        strip2[:, wide:] = low
+    def chunk_copy(n):
+        rows = pl.ds(pl.multiple_of(starts[n] * span, span), span)
+        return pltpu.make_async_copy(strip.at[rows], chunks.at[n], arrived.at[n])
 
-    first = step < steps // 2
-    pieces = [ref[...] for ref in whole]
-    pieces.append(jnp.where(first, top[...], bottom[...]))
-    pieces.append(jnp.where(first, top_o[...], bottom_o[...]))
-    both = jnp.zeros((tile, 2 * wide), jnp.float32)
-    rest = jnp.zeros((tile, wide), jnp.float32)
-    for n, piece in enumerate(pieces):
-        high, low = halves(piece)
-        start = pl.multiple_of(starts[n] * span, span)
-        both += dot(high, strip2[pl.ds(start, span), :])
-        rest += dot(low, strip2[pl.ds(start, span), :wide])
-    high, low = halves(both[:, :wide] + (both[:, wide:] + rest))
-    image2[pl.ds(pl.multiple_of(step * tile, tile), tile), :wide] = high
-    image2[pl.ds(pl.multiple_of(step * tile, tile), tile), wide:] = low
+    def tile_copy(n, t):
+        ref, row = parts[n][t * len(parts[n]) // per_piece], t * TILE
+        source = ref.at[pl.ds(row % ref.shape[0], TILE)]
+        return pltpu.make_async_copy(source, tiles.at[n, pl.ds(row, TILE)], landed.at[n, t])
 
-    @pl.when(step == steps - 1)
-    def _():
-        high, low = halves(basis_t[...])
-        both = dot(high, image2[...])
-        proj = both[:, :wide] + (both[:, wide:] + dot(low, image2[:, :wide]))
-        far, share = out.shape[1], out.shape[2]
-        for f in range(far):
-            for q in range(near):
-                begin = (f * near + q) * share
-                out[q, f] = proj[begin : begin + share]
+    for n in range(len(parts)):
+        chunk_copy(n).start()
+        for t in range(per_piece):
+            tile_copy(n, t).start()
+    for n in range(len(parts)):
+        chunk_copy(n).wait()
+        high, low = halves(chunks[n])
+        right = jnp.concatenate([high, low], axis=1)
+        for t in range(per_piece):
+            tile_copy(n, t).wait()
+            here = slice(t * TILE, (t + 1) * TILE)
+            left_high, left_low = halves(tiles[n, here])
+            both = dot(left_high, right)
+            value = both[:, :wide] + (both[:, wide:] + dot(left_low, high))
+            if n == 0:
+                image[here, :] = value
+            else:
+                image[here, :] += value
+
+    high, low = halves(image[...])
+    right = jnp.concatenate([high, low], axis=1)
+    near, far, share = out.shape[:3]
+    for f in range(far):
+        rows = near * share
+        left_high, left_low = halves(basis_t[f * rows : (f + 1) * rows, :])
+        both = dot(left_high, right)
+        proj = both[:, :wide] + (both[:, wide:] + dot(left_low, high))
+        for q in range(near):
+            out[q, f] = proj[q * share : (q + 1) * share]
 
 
 def projected(starts, strip, basis_t, whole, across, across_other, share):
     rows, span = whole[0].shape
-    tile = rows // STEPS
     total, wide = basis_t.shape[0], strip.shape[1]
-    last = STEPS // 2 - 1
-    far = total // share // NEAR
-    tiled = pl.BlockSpec((tile, span), lambda i, s: (i, 0))
-    low = pl.BlockSpec((tile, span), lambda i, s: (jnp.minimum(i, last), 0))
-    high = pl.BlockSpec((tile, span), lambda i, s: (jnp.maximum(i - last - 1, 0), 0))
-    fixed = lambda shape: pl.BlockSpec(shape, lambda i, s: (0,) * len(shape))
-    out_shape = (NEAR, far, share, wide)
+    n_pieces = len(whole) + 2
+    out_shape = (NEAR, total // share // NEAR, share, wide)
+    vmem = pl.BlockSpec(memory_space=pltpu.VMEM)
+    anywhere = pl.BlockSpec(memory_space=pl.ANY)
+    strip = pltpu.with_memory_space_constraint(strip, pltpu.HBM)
     return pl.pallas_call(
-        functools.partial(project_kernel, n_whole=len(whole), near=NEAR),
-        grid_spec=pltpu.PrefetchScalarGridSpec(
-            num_scalar_prefetch=1,
-            grid=(STEPS,),
-            in_specs=[fixed(strip.shape), fixed(basis_t.shape)]
-            + [tiled] * len(whole)
-            + [low, high, low, high],
-            out_specs=fixed(out_shape),
-            scratch_shapes=[
-                pltpu.VMEM((strip.shape[0], 2 * wide), jnp.bfloat16),
-                pltpu.VMEM((rows, 2 * wide), jnp.bfloat16),
-            ],
-        ),
+        functools.partial(project_kernel, n_whole=len(whole)),
+        in_specs=[pl.BlockSpec(memory_space=pltpu.SMEM), anywhere, vmem]
+        + [anywhere] * (len(whole) + 4),
+        out_specs=vmem,
+        scratch_shapes=[
+            pltpu.VMEM((n_pieces, span, wide), jnp.float32),
+            pltpu.VMEM((n_pieces, rows, span), jnp.float32),
+            pltpu.SemaphoreType.DMA((n_pieces,)),
+            pltpu.SemaphoreType.DMA((n_pieces, rows // TILE)),
+            pltpu.VMEM((rows, wide), jnp.float32),
+        ],
         out_shape=jax.ShapeDtypeStruct(out_shape, jnp.float32),
-        compiler_params=pltpu.CompilerParams(
-            dimension_semantics=("arbitrary",), vmem_limit_bytes=40 * 2**20
-        ),
+        compiler_params=pltpu.CompilerParams(vmem_limit_bytes=32 * 2**20),
         cost_estimate=pl.CostEstimate(
             flops=3 * 2 * rows * wide * (strip.shape[0] + total),
             bytes_accessed=4 * (strip.size + basis_t.size + rows * strip.shape[0]),

time: 210 us -> 210 us (level)
  no operation moved by 1% of the time
where the time goes in v3:
time: 210 us; the launch traced here: 209 us
  starting transfers between devices  96 us (46%)
  waiting for transfers between devices  66.2 us (32%)
  blocking collectives  17.1 us (8%)
  between operations  14.3 us (7%)
  Pallas kernels  8.29 us (4%)
  local copies, waits for them, and re-layouts  3.97 us (2%)
  other arithmetic  2.87 us (1%)
    all_to_all x1, starting transfers between devices, split_projection(): lax.all_to_all(pair_t, ('col', 'sub'), 0, 0, tiled=True)  40.3 us
    all_to_all x1, waiting for transfers between devices, split_projection(): lax.all_to_all(partial, 'row', 0, 0, tiled=True, axis_index_groups=far_gr...  25.4 us
    ppermute x4, waiting for transfers between devices, shifted(): lax.ppermute(array, axis, [(i, (i + step) % size) for i in range(size)])  20.7 us
    ppermute x7, starting transfers between devices, swapped(): return lax.ppermute(array, axis, [(i, i ^ 1) for i in range(size)])  19.8 us
    ppermute x4, starting transfers between devices, shifted(): lax.ppermute(array, axis, [(i, (i + step) % size) for i in range(size)])  18.5 us
    all_to_all x1, starting transfers between devices, split_projection(): lax.all_to_all(partial, 'row', 0, 0, tiled=True, axis_index_groups=far_gr...  17.4 us
    all_to_all x1, blocking collectives, split_projection(): lax.all_to_all(partial, 'row', 0, 0, tiled=True, axis_index_groups=near_g...  11.9 us
    ppermute x7, waiting for transfers between devices, swapped(): return lax.ppermute(array, axis, [(i, i ^ 1) for i in range(size)])  11.2 us
  transfers between devices with their start and end apart: 14, of which 6 were waited for; matrix products, arithmetic and copies ran while one was open for 3% of the time, Pallas kernels for 0%

profile of v3, /device:TPU:33, one launch (start us, length us, event | category | flops | bytes accessed | tf_op | source)
XLA Modules:
  0.0 208.8 jit_solution(8993153166898509548)
XLA Ops:
  6.6 0.7 all-gather.2.cloned.1.call-update
  7.3 1.3 slice_select_fusion.3
  8.7 5.3 %collective-permute-start.1 = (f32[256,512]{1,0:T(8,128)S(1)}, f32[256,512]{1,0:T(8,128)S(1)}, u32[]{:S(2)}, u32[]{:S(2)}) collective-permute-start(f32[256,512]{1,0:T(8,128)S(1)} %pad_maximum_fusion.1), channel_id=1, source_target_pairs={{0,8},{8,0},{16,24},{24,16},{32,40},{40,32},{48,56},{56,48},{64,72... | collective-permute-start | bytes 1572872 | tf_op jit(solution)/shard_map/ppermute | solution.py:22
  13.9 6.6 %collective-permute-done.1 = f32[256,512]{1,0:T(8,128)S(1)} collective-permute-done((f32[256,512]{1,0:T(8,128)S(1)}, f32[256,512]{1,0:T(8,128)S(1)}, u32[]{:S(2)}, u32[]{:S(2)}) %collective-permute-start.1) | collective-permute-done | bytes 524320 | tf_op jit(solution)/shard_map/ppermute | solution.py:22
  20.5 0.1 pad_maximum_fusion.refs_0_
  20.6 9.9 %collective-permute-start.3 = (f32[512,512]{1,0:T(8,128)S(1)}, f32[512,512]{1,0:T(8,128)}, u32[]{:S(2)}, u32[]{:S(2)}) collective-permute-start(f32[512,512]{1,0:T(8,128)S(1)} %pad_maximum_fusion.refs_0_), channel_id=1, source_target_pairs={{0,6},{2,0},{4,2},{6,4},{1,7},{3,1},{5,3},{7,5},{8,14},{10,8},{12,... | collective-permute-start | bytes 3145736 | tf_op jit(solution)/shard_map/ppermute | solution.py:17
  30.6 2.0 collective-permute-start.2
  32.5 3.1 %collective-permute-start = (f32[256,128]{1,0:T(8,128)S(1)}, f32[256,128]{1,0:T(8,128)S(1)}, u32[]{:S(2)}, u32[]{:S(2)}) collective-permute-start(f32[256,128]{1,0:T(8,128)S(1)} %copy-done), channel_id=1, source_target_pairs={{0,8},{8,0},{16,24},{24,16},{32,40},{40,32},{48,56},{56,48},{64,72... | collective-permute-start | bytes 393224 | tf_op jit(solution)/shard_map/ppermute | solution.py:22
  35.6 2.6 %collective-permute-done = f32[256,128]{1,0:T(8,128)S(1)} collective-permute-done((f32[256,128]{1,0:T(8,128)S(1)}, f32[256,128]{1,0:T(8,128)S(1)}, u32[]{:S(2)}, u32[]{:S(2)}) %collective-permute-start) | collective-permute-done | bytes 131104 | tf_op jit(solution)/shard_map/ppermute | solution.py:22
  38.3 0.1 copy.5
  38.4 1.6 broadcast_in_dim.7
  40.0 40.3 %all-to-all-start = ((f32[8,128,512]{2,1,0:T(8,128)}), f32[8,128,512]{2,1,0:T(8,128)S(1)}, u32[]{:S(2)}, u32[]{:S(2)}) async-start(f32[8,128,512]{2,1,0:T(8,128)} %broadcast_in_dim.7), calls=%async_computation | async-start | bytes 4194304 | tf_op jit(solution)/shard_map/all_to_all | solution.py:139
  80.3 2.2 %collective-permute-start.4 = (f32[512,512]{1,0:T(8,128)S(1)}, f32[512,512]{1,0:T(8,128)}, u32[]{:S(2)}, u32[]{:S(2)}) collective-permute-start(f32[512,512]{1,0:T(8,128)S(1)} %pad_maximum_fusion.refs_0_), channel_id=1, source_target_pairs={{0,1},{1,0},{2,3},{3,2},{4,5},{5,4},{6,7},{7,6},{8,9},{9,8},{10,11... | collective-permute-start | bytes 3145736 | tf_op jit(solution)/shard_map/ppermute | solution.py:22
  82.5 1.1 slice.25
  83.6 4.7 %collective-permute-start.8 = (f32[256,512]{1,0:T(8,128)S(1)}, f32[256,512]{1,0:T(8,128)}, u32[]{:S(2)}, u32[]{:S(2)}) collective-permute-start(f32[256,512]{1,0:T(8,128)S(1)} %slice.25), channel_id=1, source_target_pairs={{0,6},{2,0},{4,2},{6,4},{1,7},{3,1},{5,3},{7,5},{8,14},{10,8},{12,... | collective-permute-start | bytes 1572872 | tf_op jit(solution)/shard_map/ppermute | solution.py:17
  88.3 1.1 slice.24
  89.4 2.0 collective-permute-start.7
  91.4 2.4 %collective-permute-start.5 = (f32[512,512]{1,0:T(8,128)}, f32[512,512]{1,0:T(8,128)}, u32[]{:S(2)}, u32[]{:S(2)}) collective-permute-start(f32[512,512]{1,0:T(8,128)} %collective-permute-done.2.refs_1_), channel_id=1, source_target_pairs={{0,1},{1,0},{2,3},{3,2},{4,5},{5,4},{6,7},{7,6},{8,9},{9,8},{10,11... | collective-permute-start | bytes 3145736 | tf_op jit(solution)/shard_map/ppermute | solution.py:22
  93.7 2.0 collective-permute-start.6
  95.8 20.7 %collective-permute-done.8.refs_7_ = f32[256,512]{1,0:T(8,128)} collective-permute-done((f32[256,512]{1,0:T(8,128)S(1)}, f32[256,512]{1,0:T(8,128)}, u32[]{:S(2)}, u32[]{:S(2)}) %collective-permute-start.8) | collective-permute-done | bytes 524320 | tf_op jit(solution)/shard_map/ppermute | solution.py:17
  116.4 2.9 %collective-permute-start.10 = (f32[256,512]{1,0:T(8,128)}, f32[256,512]{1,0:T(8,128)}, u32[]{:S(2)}, u32[]{:S(2)}) collective-permute-start(f32[256,512]{1,0:T(8,128)} %collective-permute-done.8.refs_7_), channel_id=1, source_target_pairs={{0,1},{1,0},{2,3},{3,2},{4,5},{5,4},{6,7},{7,6},{8,9},{9,8},{10,11... | collective-permute-start | bytes 1572872 | tf_op jit(solution)/shard_map/ppermute | solution.py:22
  119.3 2.0 collective-permute-start.9
  121.3 0.1 stack.35.starts
  121.4 2.1 collective-permute-done.9.refs_8_
  123.5 8.2 %all-gather.2.cloned.1.call-done.strip = f32[4096,128]{1,0:T(8,128)} async-done(((f32[256,128]{1,0:T(8,128)}), f32[4096,128]{1,0:T(8,128)}) %all-gather.2.cloned.1.call-update) | async-done | bytes 2097168 | tf_op jit(solution)/shard_map/all_gather | solution.py:124
  131.7 8.3 %project.1 = f32[4,8,32,128]{3,2,1,0:T(8,128)S(1)} custom-call(s32[8]{0:T(128)S(1)} %stack.35.starts, f32[4096,128]{1,0:T(8,128)} %all-gather.2.cloned.1.call-done.strip, f32[1024,512]{1,0:T(8,128)S(1)} %bitcast.16, f32[512,512]{1,0:T(8,128)S(1)} %pad_maximum_fusion.refs_0_, f32[512,512]{1,0:T(8,128)} %collective-permute-done.2.refs_1_, ...), custom_call_target="tpu_custom_call" | custom-call | flops 2013265920 | bytes 12582912 | tf_op jit(solution)/shard_map/project/pallas_call | solution.py:91
  140.0 11.9 %all_to_all.15 = f32[4,8,32,128]{3,2,1,0:T(8,128)S(1)} all-to-all(f32[4,8,32,128]{3,2,1,0:T(8,128)S(1)} %project.1), channel_id=1, replica_groups={{0,8,16,24},{32,40,48,56},{64,72,80,88},{96,104,112,120},{128,136,144,1..., dimensions={0} | all-to-all | bytes 1048576 | tf_op jit(solution)/shard_map/all_to_all | solution.py:163
  151.8 0.7 reduce_sum.18
  152.5 17.4 %all-to-all-start.2 = ((f32[8,32,128]{2,1,0:T(8,128)}), f32[8,32,128]{2,1,0:T(8,128)S(1)}, u32[]{:S(2)}, u32[]{:S(2)}) async-start(f32[8,32,128]{2,1,0:T(8,128)} %reduce_sum.18), calls=%async_computation.2 | async-start | bytes 262144 | tf_op jit(solution)/shard_map/all_to_all | solution.py:166
  170.6 25.4 %all-to-all-done.2 = f32[8,32,128]{2,1,0:T(8,128)S(1)} async-done(((f32[8,32,128]{2,1,0:T(8,128)}), f32[8,32,128]{2,1,0:T(8,128)S(1)}, u32[]{:S(2)}, u32[]{:S(2)}) %all-to-all-start.2) | async-done | bytes 131104 | tf_op jit(solution)/shard_map/all_to_all | solution.py:166
  196.0 5.3 %all_gather.7 = f32[32,256]{1,0:T(8,128)S(1)} all-gather(f32[32,128]{1,0:T(8,128)S(1)} %reduce_sum.19), channel_id=1, replica_groups=mesh['groups'=2,'row'=32,'col'=4,'sub'=2] {'sub'}, dimensions={1}, use_global_device_ids=true | all-gather | bytes 49152 | tf_op jit(solution)/shard_map/all_gather | solution.py:170
  201.3 0.7 select_bitcast_fusion
  (16 shorter events, 0.1 us)
Async XLA Ops:
  6.5 125.1 %all-gather.2.cloned.1.call-start = ((), (), s32[]{:S(2)}) async-start(), calls=%async_computation.3 | async-start | bytes 2228224 | tf_op jit(solution)/shard_map/all_gather | solution.py:124
  8.6 23.9 %copy-start = (f32[256,128]{1,0:T(8,128)S(1)}, f32[256,128]{1,0:T(8,128)}, u32[]{:S(2)}) copy-start(f32[256,128]{1,0:T(8,128)} %param.4) | copy-start | bytes 393220
  8.7 11.8 %collective-permute-start.1 = (f32[256,512]{1,0:T(8,128)S(1)}, f32[256,512]{1,0:T(8,128)S(1)}, u32[]{:S(2)}, u32[]{:S(2)}) collective-permute-start(f32[256,512]{1,0:T(8,128)S(1)} %pad_maximum_fusion.1), channel_id=1, source_target_pairs={{0,8},{8,0},{16,24},{24,16},{32,40},{40,32},{48,56},{56,48},{64,72... | collective-permute-start | bytes 1572872 | tf_op jit(solution)/shard_map/ppermute | solution.py:22
  20.6 61.9 %collective-permute-start.3 = (f32[512,512]{1,0:T(8,128)S(1)}, f32[512,512]{1,0:T(8,128)}, u32[]{:S(2)}, u32[]{:S(2)}) collective-permute-start(f32[512,512]{1,0:T(8,128)S(1)} %pad_maximum_fusion.refs_0_), channel_id=1, source_target_pairs={{0,6},{2,0},{4,2},{6,4},{1,7},{3,1},{5,3},{7,5},{8,14},{10,8},{12,... | collective-permute-start | bytes 3145736 | tf_op jit(solution)/shard_map/ppermute | solution.py:17
  30.6 57.8 %collective-permute-start.2 = (f32[512,512]{1,0:T(8,128)S(1)}, f32[512,512]{1,0:T(8,128)}, u32[]{:S(2)}, u32[]{:S(2)}) collective-permute-start(f32[512,512]{1,0:T(8,128)S(1)} %pad_maximum_fusion.refs_0_), channel_id=1, source_target_pairs={{0,2},{2,4},{4,6},{6,0},{1,3},{3,5},{5,7},{7,1},{8,10},{10,12},{12... | collective-permute-start | bytes 3145736 | tf_op jit(solution)/shard_map/ppermute | solution.py:17
  32.5 5.7 %collective-permute-start = (f32[256,128]{1,0:T(8,128)S(1)}, f32[256,128]{1,0:T(8,128)S(1)}, u32[]{:S(2)}, u32[]{:S(2)}) collective-permute-start(f32[256,128]{1,0:T(8,128)S(1)} %copy-done), channel_id=1, source_target_pairs={{0,8},{8,0},{16,24},{24,16},{32,40},{40,32},{48,56},{56,48},{64,72... | collective-permute-start | bytes 393224 | tf_op jit(solution)/shard_map/ppermute | solution.py:22
  40.0 81.4 %all-to-all-start = ((f32[8,128,512]{2,1,0:T(8,128)}), f32[8,128,512]{2,1,0:T(8,128)S(1)}, u32[]{:S(2)}, u32[]{:S(2)}) async-start(f32[8,128,512]{2,1,0:T(8,128)} %broadcast_in_dim.7), calls=%async_computation | async-start | bytes 4194304 | tf_op jit(solution)/shard_map/all_to_all | solution.py:139
  80.3 41.1 %collective-permute-start.4 = (f32[512,512]{1,0:T(8,128)S(1)}, f32[512,512]{1,0:T(8,128)}, u32[]{:S(2)}, u32[]{:S(2)}) collective-permute-start(f32[512,512]{1,0:T(8,128)S(1)} %pad_maximum_fusion.refs_0_), channel_id=1, source_target_pairs={{0,1},{1,0},{2,3},{3,2},{4,5},{5,4},{6,7},{7,6},{8,9},{9,8},{10,11... | collective-permute-start | bytes 3145736 | tf_op jit(solution)/shard_map/ppermute | solution.py:22
  83.6 32.8 %collective-permute-start.8 = (f32[256,512]{1,0:T(8,128)S(1)}, f32[256,512]{1,0:T(8,128)}, u32[]{:S(2)}, u32[]{:S(2)}) collective-permute-start(f32[256,512]{1,0:T(8,128)S(1)} %slice.25), channel_id=1, source_target_pairs={{0,6},{2,0},{4,2},{6,4},{1,7},{3,1},{5,3},{7,5},{8,14},{10,8},{12,... | collective-permute-start | bytes 1572872 | tf_op jit(solution)/shard_map/ppermute | solution.py:17
  89.4 29.9 %collective-permute-start.7 = (f32[256,512]{1,0:T(8,128)S(1)}, f32[256,512]{1,0:T(8,128)}, u32[]{:S(2)}, u32[]{:S(2)}) collective-permute-start(f32[256,512]{1,0:T(8,128)S(1)} %slice.24), channel_id=1, source_target_pairs={{0,2},{2,4},{4,6},{6,0},{1,3},{3,5},{5,7},{7,1},{8,10},{10,12},{12... | collective-permute-start | bytes 1572872 | tf_op jit(solution)/shard_map/ppermute | solution.py:17
  91.4 32.1 %collective-permute-start.5 = (f32[512,512]{1,0:T(8,128)}, f32[512,512]{1,0:T(8,128)}, u32[]{:S(2)}, u32[]{:S(2)}) collective-permute-start(f32[512,512]{1,0:T(8,128)} %collective-permute-done.2.refs_1_), channel_id=1, source_target_pairs={{0,1},{1,0},{2,3},{3,2},{4,5},{5,4},{6,7},{7,6},{8,9},{9,8},{10,11... | collective-permute-start | bytes 3145736 | tf_op jit(solution)/shard_map/ppermute | solution.py:22
  93.7 29.8 %collective-permute-start.6 = (f32[512,512]{1,0:T(8,128)}, f32[512,512]{1,0:T(8,128)}, u32[]{:S(2)}, u32[]{:S(2)}) collective-permute-start(f32[512,512]{1,0:T(8,128)} %collective-permute-done.3.refs_2_), channel_id=1, source_target_pairs={{0,1},{1,0},{2,3},{3,2},{4,5},{5,4},{6,7},{7,6},{8,9},{9,8},{10,11... | collective-permute-start | bytes 3145736 | tf_op jit(solution)/shard_map/ppermute | solution.py:22
  116.4 5.0 %collective-permute-start.10 = (f32[256,512]{1,0:T(8,128)}, f32[256,512]{1,0:T(8,128)}, u32[]{:S(2)}, u32[]{:S(2)}) collective-permute-start(f32[256,512]{1,0:T(8,128)} %collective-permute-done.8.refs_7_), channel_id=1, source_target_pairs={{0,1},{1,0},{2,3},{3,2},{4,5},{5,4},{6,7},{7,6},{8,9},{9,8},{10,11... | collective-permute-start | bytes 1572872 | tf_op jit(solution)/shard_map/ppermute | solution.py:22
  119.3 4.2 %collective-permute-start.9 = (f32[256,512]{1,0:T(8,128)}, f32[256,512]{1,0:T(8,128)}, u32[]{:S(2)}, u32[]{:S(2)}) collective-permute-start(f32[256,512]{1,0:T(8,128)} %collective-permute-done.7.refs_6_), channel_id=1, source_target_pairs={{0,1},{1,0},{2,3},{3,2},{4,5},{5,4},{6,7},{7,6},{8,9},{9,8},{10,11... | collective-permute-start | bytes 1572872 | tf_op jit(solution)/shard_map/ppermute | solution.py:22
  152.5 43.5 %all-to-all-start.2 = ((f32[8,32,128]{2,1,0:T(8,128)}), f32[8,32,128]{2,1,0:T(8,128)S(1)}, u32[]{:S(2)}, u32[]{:S(2)}) async-start(f32[8,32,128]{2,1,0:T(8,128)} %reduce_sum.18), calls=%async_computation.2 | async-start | bytes 262144 | tf_op jit(solution)/shard_map/all_to_all | solution.py:166
Sparse Core Ops, SparseCore 0:
  9.4 122.1 all-gather.1

commit v4 on v3

--- a/solution.py
+++ b/solution.py
@@ -1,5 +1,3 @@
-import functools
-
 import jax
 import jax.numpy as jnp
 from jax import lax
@@ -10,6 +8,7 @@
 
 NEAR = 4
 TILE = 256
+AHEAD = 3
 
 
 def shifted(array, axis, step):
@@ -32,10 +31,8 @@
     return jnp.dot(left, right, preferred_element_type=jnp.float32)
 
 
-def project_kernel(starts, strip, basis_t, *refs, n_whole):
-    parts = [(ref,) for ref in refs[:n_whole]]
-    parts += [refs[n_whole : n_whole + 2], refs[n_whole + 2 : n_whole + 4]]
-    out, chunks, tiles, arrived, landed, image = refs[n_whole + 4 :]
+def project_kernel(starts, strip, basis_t, *refs):
+    *pieces, out, chunks, tiles, arrived, landed, image = refs
     wide = strip.shape[1]
     span = chunks.shape[1]
     per_piece = tiles.shape[1] // TILE
@@ -45,15 +42,19 @@
         return pltpu.make_async_copy(strip.at[rows], chunks.at[n], arrived.at[n])
 
     def tile_copy(n, t):
-        ref, row = parts[n][t * len(parts[n]) // per_piece], t * TILE
-        source = ref.at[pl.ds(row % ref.shape[0], TILE)]
-        return pltpu.make_async_copy(source, tiles.at[n, pl.ds(row, TILE)], landed.at[n, t])
+        rows = pl.ds(t * TILE, TILE)
+        return pltpu.make_async_copy(pieces[n].at[rows], tiles.at[n, rows], landed.at[n, t])
 
-    for n in range(len(parts)):
+    def begin(n):
         chunk_copy(n).start()
         for t in range(per_piece):
             tile_copy(n, t).start()
-    for n in range(len(parts)):
+
+    for n in range(AHEAD):
+        begin(n)
+    for n in range(len(pieces)):
+        if n + AHEAD < len(pieces):
+            begin(n + AHEAD)
         chunk_copy(n).wait()
         high, low = halves(chunks[n])
         right = jnp.concatenate([high, low], axis=1)
@@ -80,18 +81,18 @@
             out[q, f] = proj[q * share : (q + 1) * share]
 
 
-def projected(starts, strip, basis_t, whole, across, across_other, share):
-    rows, span = whole[0].shape
+def projected(starts, strip, basis_t, pieces, share):
+    rows, span = pieces[0].shape
     total, wide = basis_t.shape[0], strip.shape[1]
-    n_pieces = len(whole) + 2
+    n_pieces = len(pieces)
     out_shape = (NEAR, total // share // NEAR, share, wide)
     vmem = pl.BlockSpec(memory_space=pltpu.VMEM)
     anywhere = pl.BlockSpec(memory_space=pl.ANY)
     strip = pltpu.with_memory_space_constraint(strip, pltpu.HBM)
     return pl.pallas_call(
-        functools.partial(project_kernel, n_whole=len(whole)),
+        project_kernel,
         in_specs=[pl.BlockSpec(memory_space=pltpu.SMEM), anywhere, vmem]
-        + [anywhere] * (len(whole) + 4),
+        + [anywhere] * n_pieces,
         out_specs=vmem,
         scratch_shapes=[
             pltpu.VMEM((n_pieces, span, wide), jnp.float32),
@@ -108,7 +109,17 @@
             transcendentals=0,
         ),
         name="project",
-    )(starts, strip, basis_t, *whole, *across, *across_other)
+    )(starts, strip, basis_t, *pieces)
+
+
+def kept(leading, row, col, sub, height, width):
+    row_ids = jnp.arange(height, dtype=jnp.int32) + row * height
+    col_ids = jnp.arange(width, dtype=jnp.int32) + col * width
+    row_first = row_ids < leading
+    col_first = col_ids < leading
+    mask_one = row_first[:, None] & col_first[None, :]
+    mask_two = jnp.logical_not(row_first)[:, None] & jnp.logical_not(col_first)[None, :]
+    return jnp.where(sub == 0, mask_one, mask_two)
 
 
 def split_projection(matrix, basis_vectors, split_size):
@@ -142,20 +153,16 @@
 
     before = shifted(own, "col", 1)
     after = shifted(own, "col", -1)
-    across = (shifted(before[:block], "col", 1), shifted(after[block:], "col", -1))
-    mine = [own, before, after]
+    across = shifted(own, "col", 2)
+    mine = [own, before, after, across]
     theirs = [swapped(piece, "sub") for piece in mine]
-    across_other = tuple(swapped(piece, "sub") for piece in across)
 
-    sources = [col, (col - 1) % n_col, (col + 1) % n_col]
-    opposite = (col + 2) % n_col
-    starts = jnp.stack(
-        [2 * s + sub for s in sources]
-        + [2 * s + 1 - sub for s in sources]
-        + [2 * opposite + sub, 2 * opposite + 1 - sub]
-    ).astype(jnp.int32)
+    sources = [col, (col - 1) % n_col, (col + 1) % n_col, (col + 2) % n_col]
+    starts = jnp.stack([2 * s + sub for s in sources] + [2 * s + 1 - sub for s in sources])
     share = basis_t.shape[0] // n_row
-    partial = projected(starts, strip, basis_t, mine + theirs, across, across_other, share)
+    keep = kept(split_size[0], row, col, sub, share, 2 * basis_vectors.shape[1])
+    starts, keep = lax.optimization_barrier((starts.astype(jnp.int32), keep))
+    partial = projected(starts, strip, basis_t, mine + theirs, share)
 
     far = n_row // NEAR
     near_groups = [[NEAR * g + q for q in range(NEAR)] for g in range(far)]
@@ -168,15 +175,7 @@
     ).sum(0)
 
     child_block = lax.all_gather(proj_block, "sub", axis=1, tiled=True)
-    row_ids = jnp.arange(child_block.shape[0], dtype=jnp.int32) + row * child_block.shape[0]
-    col_ids = jnp.arange(child_block.shape[1], dtype=jnp.int32) + col * child_block.shape[1]
-    leading = split_size[0]
-    row_first = row_ids < leading
-    col_first = col_ids < leading
-    mask_one = row_first[:, None] & col_first[None, :]
-    mask_two = jnp.logical_not(row_first)[:, None] & jnp.logical_not(col_first)[None, :]
-    selected = jnp.where(sub == 0, mask_one, mask_two)
-    return jnp.where(selected, child_block, jnp.zeros((), jnp.float32))[None]
+    return jnp.where(keep, child_block, jnp.zeros((), jnp.float32))[None]
 
 
 def solution(mesh):

time: 210 us -> 209 us (level)
  blocking collectives: 17.1 us -> 60.3 us
  waiting for transfers between devices: 66.2 us -> 40 us
  starting transfers between devices: 96 us -> 80.6 us
  local copies, waits for them, and re-layouts: 3.97 us -> 1.8 us
    all_to_all x0 -> x1, blocking collectives: none -> 43.5 us  [split_projection(): lax.all_to_all(partial, 'row', 0, 0, tiled=True, axis_index_groups=far_gr...]
    all_to_all x1 -> x0, waiting for transfers between devices: 25.4 us -> none  [split_projection(): lax.all_to_all(partial, 'row', 0, 0, tiled=True, axis_index_groups=far_gr...]
    ppermute x4 -> x3, waiting for transfers between devices: 20.7 us -> 0.01 us  [shifted(): lax.ppermute(array, axis, [(i, (i + step) % size) for i in range(size)])]
    all_to_all x1 -> x0, starting transfers between devices: 17.4 us -> none  [split_projection(): lax.all_to_all(partial, 'row', 0, 0, tiled=True, axis_index_groups=far_gr...]
    all_to_all x1, waiting for transfers between devices: 0.01 us -> 11.6 us  [split_projection(): lax.all_to_all(pair_t, ('col', 'sub'), 0, 0, tiled=True)]
    all_gather x1, waiting for transfers between devices: 8.15 us -> 18.4 us  [split_projection(): lax.all_gather(basis_vectors, 'row', axis=0, tiled=True, axis_index_group...]
    ppermute x4 -> x3, starting transfers between devices: 18.5 us -> 15.4 us  [shifted(): lax.ppermute(array, axis, [(i, (i + step) % size) for i in range(size)])]
    all_to_all x1, starting transfers between devices: 40.3 us -> 43.1 us  [split_projection(): lax.all_to_all(pair_t, ('col', 'sub'), 0, 0, tiled=True)]
  transfers between devices with their start and end apart: 14 -> 11, of which waited for: 6 -> 4; matrix products, arithmetic and copies ran while one was open for 3% -> 2% of each run, Pallas kernels for 0% -> 0%
where the time goes in v4:
time: 209 us; the launch traced here: 207 us
  starting transfers between devices  80.6 us (39%)
  blocking collectives  60.3 us (29%)
  waiting for transfers between devices  40 us (19%)
  between operations  14.3 us (7%)
  Pallas kernels  7.72 us (4%)
  other arithmetic  2.22 us (1%)
    all_to_all x1, blocking collectives, split_projection(): lax.all_to_all(partial, 'row', 0, 0, tiled=True, axis_index_groups=far_gr...  43.5 us
    all_to_all x1, starting transfers between devices, split_projection(): lax.all_to_all(pair_t, ('col', 'sub'), 0, 0, tiled=True)  43.1 us
    ppermute x6, starting transfers between devices, swapped(): return lax.ppermute(array, axis, [(i, i ^ 1) for i in range(size)])  22.1 us
    all_gather x1, waiting for transfers between devices, split_projection(): lax.all_gather(basis_vectors, 'row', axis=0, tiled=True, axis_index_group...  18.4 us
    ppermute x3, starting transfers between devices, shifted(): lax.ppermute(array, axis, [(i, (i + step) % size) for i in range(size)])  15.4 us
    all_to_all x1, waiting for transfers between devices, split_projection(): lax.all_to_all(pair_t, ('col', 'sub'), 0, 0, tiled=True)  11.6 us
    all_to_all x1, blocking collectives, split_projection(): lax.all_to_all(partial, 'row', 0, 0, tiled=True, axis_index_groups=near_g...  11.6 us
    ppermute x6, waiting for transfers between devices, swapped(): return lax.ppermute(array, axis, [(i, i ^ 1) for i in range(size)])  9.19 us
  transfers between devices with their start and end apart: 11, of which 4 were waited for; matrix products, arithmetic and copies ran while one was open for 2% of the time, Pallas kernels for 0%

profile of v4, /device:TPU:33, one launch (start us, length us, event | category | flops | bytes accessed | tf_op | source)
XLA Modules:
  0.0 206.9 jit_solution(14299716941807689251)
XLA Ops:
  6.6 0.7 all-gather.2.cloned.1.call-update
  7.3 1.3 slice_select_fusion.3
  8.6 0.0 copy-start
  8.6 0.1 pad_maximum_fusion.1
  8.7 5.3 %collective-permute-start.1 = (f32[256,512]{1,0:T(8,128)S(1)}, f32[256,512]{1,0:T(8,128)S(1)}, u32[]{:S(2)}, u32[]{:S(2)}) collective-permute-start(f32[256,512]{1,0:T(8,128)S(1)} %pad_maximum_fusion.1), channel_id=1, source_target_pairs={{0,8},{8,0},{16,24},{24,16},{32,40},{40,32},{48,56},{56,48},{64,72... | collective-permute-start | bytes 1572872 | tf_op jit(solution)/shard_map/ppermute | solution.py:21
  13.9 6.6 %collective-permute-done.1 = f32[256,512]{1,0:T(8,128)S(1)} collective-permute-done((f32[256,512]{1,0:T(8,128)S(1)}, f32[256,512]{1,0:T(8,128)S(1)}, u32[]{:S(2)}, u32[]{:S(2)}) %collective-permute-start.1) | collective-permute-done | bytes 524320 | tf_op jit(solution)/shard_map/ppermute | solution.py:21
  20.5 0.1 pad_maximum_fusion.refs_0_
  20.6 8.4 %collective-permute-start.2 = (f32[512,512]{1,0:T(8,128)S(1)}, f32[512,512]{1,0:T(8,128)}, u32[]{:S(2)}, u32[]{:S(2)}) collective-permute-start(f32[512,512]{1,0:T(8,128)S(1)} %pad_maximum_fusion.refs_0_), channel_id=1, source_target_pairs={{0,2},{2,4},{4,6},{6,0},{1,3},{3,5},{5,7},{7,1},{8,10},{10,12},{12... | collective-permute-start | bytes 3145736 | tf_op jit(solution)/shard_map/ppermute | solution.py:16
  29.0 3.5 %collective-permute-start.3 = (f32[512,512]{1,0:T(8,128)S(1)}, f32[512,512]{1,0:T(8,128)}, u32[]{:S(2)}, u32[]{:S(2)}) collective-permute-start(f32[512,512]{1,0:T(8,128)S(1)} %pad_maximum_fusion.refs_0_), channel_id=1, source_target_pairs={{0,6},{2,0},{4,2},{6,4},{1,7},{3,1},{5,3},{7,5},{8,14},{10,8},{12,... | collective-permute-start | bytes 3145736 | tf_op jit(solution)/shard_map/ppermute | solution.py:16
  32.5 3.5 %collective-permute-start.4 = (f32[512,512]{1,0:T(8,128)S(1)}, f32[512,512]{1,0:T(8,128)}, u32[]{:S(2)}, u32[]{:S(2)}) collective-permute-start(f32[512,512]{1,0:T(8,128)S(1)} %pad_maximum_fusion.refs_0_), channel_id=1, source_target_pairs={{0,4},{2,6},{4,0},{6,2},{1,5},{3,7},{5,1},{7,3},{8,12},{10,14},{12... | collective-permute-start | bytes 3145736 | tf_op jit(solution)/shard_map/ppermute | solution.py:16
  36.1 3.1 %collective-permute-start = (f32[256,128]{1,0:T(8,128)S(1)}, f32[256,128]{1,0:T(8,128)S(1)}, u32[]{:S(2)}, u32[]{:S(2)}) collective-permute-start(f32[256,128]{1,0:T(8,128)S(1)} %copy-done), channel_id=1, source_target_pairs={{0,8},{8,0},{16,24},{24,16},{32,40},{40,32},{48,56},{56,48},{64,72... | collective-permute-start | bytes 393224 | tf_op jit(solution)/shard_map/ppermute | solution.py:21
  39.2 2.6 %collective-permute-done = f32[256,128]{1,0:T(8,128)S(1)} collective-permute-done((f32[256,128]{1,0:T(8,128)S(1)}, f32[256,128]{1,0:T(8,128)S(1)}, u32[]{:S(2)}, u32[]{:S(2)}) %collective-permute-start) | collective-permute-done | bytes 131104 | tf_op jit(solution)/shard_map/ppermute | solution.py:21
  41.8 0.1 copy.5
  42.0 1.6 broadcast_in_dim.7
  43.5 43.1 %all-to-all-start = ((f32[8,128,512]{2,1,0:T(8,128)}), f32[8,128,512]{2,1,0:T(8,128)S(1)}, u32[]{:S(2)}, u32[]{:S(2)}) async-start(f32[8,128,512]{2,1,0:T(8,128)} %broadcast_in_dim.7), calls=%async_computation | async-start | bytes 4194304 | tf_op jit(solution)/shard_map/all_to_all | solution.py:150
  86.6 1.9 collective-permute-start.5
  88.5 0.0 collective-permute-done.2.refs_1_
  88.6 4.0 %collective-permute-start.6 = (f32[512,512]{1,0:T(8,128)}, f32[512,512]{1,0:T(8,128)}, u32[]{:S(2)}, u32[]{:S(2)}) collective-permute-start(f32[512,512]{1,0:T(8,128)} %collective-permute-done.2.refs_1_), channel_id=1, source_target_pairs={{0,1},{1,0},{2,3},{3,2},{4,5},{5,4},{6,7},{7,6},{8,9},{9,8},{10,11... | collective-permute-start | bytes 3145736 | tf_op jit(solution)/shard_map/ppermute | solution.py:21
  92.5 0.0 collective-permute-done.3.refs_2_
  92.5 5.8 %collective-permute-start.7 = (f32[512,512]{1,0:T(8,128)}, f32[512,512]{1,0:T(8,128)}, u32[]{:S(2)}, u32[]{:S(2)}) collective-permute-start(f32[512,512]{1,0:T(8,128)} %collective-permute-done.3.refs_2_), channel_id=1, source_target_pairs={{0,1},{1,0},{2,3},{3,2},{4,5},{5,4},{6,7},{7,6},{8,9},{9,8},{10,11... | collective-permute-start | bytes 3145736 | tf_op jit(solution)/shard_map/ppermute | solution.py:21
  98.4 2.0 collective-permute-start.8
  101.1 0.1 stack.35.starts
  101.2 0.1 and_select_fusion
  101.3 0.0 collective-permute-done.5.refs_4_
  101.3 11.6 %all-to-all-done = f32[8,128,512]{2,1,0:T(8,128)S(1)} async-done(((f32[8,128,512]{2,1,0:T(8,128)}), f32[8,128,512]{2,1,0:T(8,128)S(1)}, u32[]{:S(2)}, u32[]{:S(2)}) %all-to-all-start) | async-done | bytes 2097184 | tf_op jit(solution)/shard_map/all_to_all | solution.py:150
  112.9 0.0 collective-permute-done.6.refs_5_
  112.9 18.4 %all-gather.2.cloned.1.call-done.strip = f32[4096,128]{1,0:T(8,128)} async-done(((f32[256,128]{1,0:T(8,128)}), f32[4096,128]{1,0:T(8,128)}) %all-gather.2.cloned.1.call-update) | async-done | bytes 2097168 | tf_op jit(solution)/shard_map/all_gather | solution.py:135
  131.4 7.7 %project.1 = f32[4,8,32,128]{3,2,1,0:T(8,128)S(1)} custom-call(s32[8]{0:T(128)S(1)} %stack.35.starts, f32[4096,128]{1,0:T(8,128)} %all-gather.2.cloned.1.call-done.strip, f32[1024,512]{1,0:T(8,128)S(1)} %bitcast.16, f32[512,512]{1,0:T(8,128)S(1)} %pad_maximum_fusion.refs_0_, f32[512,512]{1,0:T(8,128)} %collective-permute-done.2.refs_1_, ...), custom_call_target="tpu_custom_call" | custom-call | flops 2013265920 | bytes 12582912 | tf_op jit(solution)/shard_map/project/pallas_call | solution.py:92
  139.1 11.6 %all_to_all.15 = f32[4,8,32,128]{3,2,1,0:T(8,128)S(1)} all-to-all(f32[4,8,32,128]{3,2,1,0:T(8,128)S(1)} %project.1), channel_id=1, replica_groups={{0,8,16,24},{32,40,48,56},{64,72,80,88},{96,104,112,120},{128,136,144,1..., dimensions={0} | all-to-all | bytes 1048576 | tf_op jit(solution)/shard_map/all_to_all | solution.py:170
  150.7 43.5 %all_to_all.16 = f32[8,32,128]{2,1,0:T(8,128)S(1)} all-to-all(f32[8,32,128]{2,1,0:T(8,128)S(1)} %reduce_sum.18), channel_id=1, replica_groups={{0,32,64,96,128,160,192,224},{8,40,72,104,136,168,200,232},{16,48,80,11..., dimensions={0} | all-to-all | bytes 262144 | tf_op jit(solution)/shard_map/all_to_all | solution.py:173
  194.2 5.2 %all_gather.7 = f32[32,256]{1,0:T(8,128)S(1)} all-gather(f32[32,128]{1,0:T(8,128)S(1)} %reduce_sum.19), channel_id=1, replica_groups=mesh['groups'=2,'row'=32,'col'=4,'sub'=2] {'sub'}, dimensions={1}, use_global_device_ids=true | all-gather | bytes 49152 | tf_op jit(solution)/shard_map/all_gather | solution.py:177
  199.5 0.6 select_bitcast_fusion
  (10 shorter events, 0.1 us)
Async XLA Ops:
  6.5 124.8 %all-gather.2.cloned.1.call-start = ((), (), s32[]{:S(2)}) async-start(), calls=%async_computation.3 | async-start | bytes 2228224 | tf_op jit(solution)/shard_map/all_gather | solution.py:135
  8.6 27.4 %copy-start = (f32[256,128]{1,0:T(8,128)S(1)}, f32[256,128]{1,0:T(8,128)}, u32[]{:S(2)}) copy-start(f32[256,128]{1,0:T(8,128)} %param.4) | copy-start | bytes 393220
  8.7 11.8 %collective-permute-start.1 = (f32[256,512]{1,0:T(8,128)S(1)}, f32[256,512]{1,0:T(8,128)S(1)}, u32[]{:S(2)}, u32[]{:S(2)}) collective-permute-start(f32[256,512]{1,0:T(8,128)S(1)} %pad_maximum_fusion.1), channel_id=1, source_target_pairs={{0,8},{8,0},{16,24},{24,16},{32,40},{40,32},{48,56},{56,48},{64,72... | collective-permute-start | bytes 1572872 | tf_op jit(solution)/shard_map/ppermute | solution.py:21
  20.6 67.9 %collective-permute-start.2 = (f32[512,512]{1,0:T(8,128)S(1)}, f32[512,512]{1,0:T(8,128)}, u32[]{:S(2)}, u32[]{:S(2)}) collective-permute-start(f32[512,512]{1,0:T(8,128)S(1)} %pad_maximum_fusion.refs_0_), channel_id=1, source_target_pairs={{0,2},{2,4},{4,6},{6,0},{1,3},{3,5},{5,7},{7,1},{8,10},{10,12},{12... | collective-permute-start | bytes 3145736 | tf_op jit(solution)/shard_map/ppermute | solution.py:16
  29.0 63.5 %collective-permute-start.3 = (f32[512,512]{1,0:T(8,128)S(1)}, f32[512,512]{1,0:T(8,128)}, u32[]{:S(2)}, u32[]{:S(2)}) collective-permute-start(f32[512,512]{1,0:T(8,128)S(1)} %pad_maximum_fusion.refs_0_), channel_id=1, source_target_pairs={{0,6},{2,0},{4,2},{6,4},{1,7},{3,1},{5,3},{7,5},{8,14},{10,8},{12,... | collective-permute-start | bytes 3145736 | tf_op jit(solution)/shard_map/ppermute | solution.py:16
  32.5 65.9 %collective-permute-start.4 = (f32[512,512]{1,0:T(8,128)S(1)}, f32[512,512]{1,0:T(8,128)}, u32[]{:S(2)}, u32[]{:S(2)}) collective-permute-start(f32[512,512]{1,0:T(8,128)S(1)} %pad_maximum_fusion.refs_0_), channel_id=1, source_target_pairs={{0,4},{2,6},{4,0},{6,2},{1,5},{3,7},{5,1},{7,3},{8,12},{10,14},{12... | collective-permute-start | bytes 3145736 | tf_op jit(solution)/shard_map/ppermute | solution.py:16
  36.1 5.7 %collective-permute-start = (f32[256,128]{1,0:T(8,128)S(1)}, f32[256,128]{1,0:T(8,128)S(1)}, u32[]{:S(2)}, u32[]{:S(2)}) collective-permute-start(f32[256,128]{1,0:T(8,128)S(1)} %copy-done), channel_id=1, source_target_pairs={{0,8},{8,0},{16,24},{24,16},{32,40},{40,32},{48,56},{56,48},{64,72... | collective-permute-start | bytes 393224 | tf_op jit(solution)/shard_map/ppermute | solution.py:21
  43.5 69.4 %all-to-all-start = ((f32[8,128,512]{2,1,0:T(8,128)}), f32[8,128,512]{2,1,0:T(8,128)S(1)}, u32[]{:S(2)}, u32[]{:S(2)}) async-start(f32[8,128,512]{2,1,0:T(8,128)} %broadcast_in_dim.7), calls=%async_computation | async-start | bytes 4194304 | tf_op jit(solution)/shard_map/all_to_all | solution.py:150
  86.6 14.7 %collective-permute-start.5 = (f32[512,512]{1,0:T(8,128)S(1)}, f32[512,512]{1,0:T(8,128)}, u32[]{:S(2)}, u32[]{:S(2)}) collective-permute-start(f32[512,512]{1,0:T(8,128)S(1)} %pad_maximum_fusion.refs_0_), channel_id=1, source_target_pairs={{0,1},{1,0},{2,3},{3,2},{4,5},{5,4},{6,7},{7,6},{8,9},{9,8},{10,11... | collective-permute-start | bytes 3145736 | tf_op jit(solution)/shard_map/ppermute | solution.py:21
  88.6 24.4 %collective-permute-start.6 = (f32[512,512]{1,0:T(8,128)}, f32[512,512]{1,0:T(8,128)}, u32[]{:S(2)}, u32[]{:S(2)}) collective-permute-start(f32[512,512]{1,0:T(8,128)} %collective-permute-done.2.refs_1_), channel_id=1, source_target_pairs={{0,1},{1,0},{2,3},{3,2},{4,5},{5,4},{6,7},{7,6},{8,9},{9,8},{10,11... | collective-permute-start | bytes 3145736 | tf_op jit(solution)/shard_map/ppermute | solution.py:21
  92.5 20.4 %collective-permute-start.7 = (f32[512,512]{1,0:T(8,128)}, f32[512,512]{1,0:T(8,128)}, u32[]{:S(2)}, u32[]{:S(2)}) collective-permute-start(f32[512,512]{1,0:T(8,128)} %collective-permute-done.3.refs_2_), channel_id=1, source_target_pairs={{0,1},{1,0},{2,3},{3,2},{4,5},{5,4},{6,7},{7,6},{8,9},{9,8},{10,11... | collective-permute-start | bytes 3145736 | tf_op jit(solution)/shard_map/ppermute | solution.py:21
  98.4 14.5 %collective-permute-start.8 = (f32[512,512]{1,0:T(8,128)}, f32[512,512]{1,0:T(8,128)}, u32[]{:S(2)}, u32[]{:S(2)}) collective-permute-start(f32[512,512]{1,0:T(8,128)} %collective-permute-done.4.refs_3_), channel_id=1, source_target_pairs={{0,1},{1,0},{2,3},{3,2},{4,5},{5,4},{6,7},{7,6},{8,9},{9,8},{10,11... | collective-permute-start | bytes 3145736 | tf_op jit(solution)/shard_map/ppermute | solution.py:21
Sparse Core Ops, SparseCore 0:
  9.4 121.8 all-gather.1

commit v5 on v4

--- a/solution.py
+++ b/solution.py
@@ -7,7 +7,6 @@
 
 
 NEAR = 4
-TILE = 256
 AHEAD = 3
 
 
@@ -35,15 +34,15 @@
     *pieces, out, chunks, tiles, arrived, landed, image = refs
     wide = strip.shape[1]
     span = chunks.shape[1]
-    per_piece = tiles.shape[1] // TILE
+    tile = tiles.shape[2]
+    per_piece = tiles.shape[1]
 
     def chunk_copy(n):
         rows = pl.ds(pl.multiple_of(starts[n] * span, span), span)
         return pltpu.make_async_copy(strip.at[rows], chunks.at[n], arrived.at[n])
 
     def tile_copy(n, t):
-        rows = pl.ds(t * TILE, TILE)
-        return pltpu.make_async_copy(pieces[n].at[rows], tiles.at[n, rows], landed.at[n, t])
+        return pltpu.make_async_copy(pieces[n * per_piece + t], tiles.at[n, t], landed.at[n, t])
 
     def begin(n):
         chunk_copy(n).start()
@@ -52,16 +51,16 @@
 
     for n in range(AHEAD):
         begin(n)
-    for n in range(len(pieces)):
-        if n + AHEAD < len(pieces):
+    for n in range(chunks.shape[0]):
+        if n + AHEAD < chunks.shape[0]:
             begin(n + AHEAD)
         chunk_copy(n).wait()
         high, low = halves(chunks[n])
         right = jnp.concatenate([high, low], axis=1)
         for t in range(per_piece):
             tile_copy(n, t).wait()
-            here = slice(t * TILE, (t + 1) * TILE)
-            left_high, left_low = halves(tiles[n, here])
+            here = slice(t * tile, (t + 1) * tile)
+            left_high, left_low = halves(tiles[n, t])
             both = dot(left_high, right)
             value = both[:, :wide] + (both[:, wide:] + dot(left_low, high))
             if n == 0:
@@ -82,23 +81,28 @@
 
 
 def projected(starts, strip, basis_t, pieces, share):
-    rows, span = pieces[0].shape
+    per_piece = len(pieces[0])
+    tile, span = pieces[0][0].shape
+    rows = per_piece * tile
     total, wide = basis_t.shape[0], strip.shape[1]
     n_pieces = len(pieces)
     out_shape = (NEAR, total // share // NEAR, share, wide)
     vmem = pl.BlockSpec(memory_space=pltpu.VMEM)
     anywhere = pl.BlockSpec(memory_space=pl.ANY)
-    strip = pltpu.with_memory_space_constraint(strip, pltpu.HBM)
+    in_hbm = [
+        pltpu.with_memory_space_constraint(array, pltpu.HBM)
+        for array in (strip, *(part for piece in pieces for part in piece))
+    ]
     return pl.pallas_call(
         project_kernel,
         in_specs=[pl.BlockSpec(memory_space=pltpu.SMEM), anywhere, vmem]
-        + [anywhere] * n_pieces,
+        + [anywhere] * (n_pieces * per_piece),
         out_specs=vmem,
         scratch_shapes=[
             pltpu.VMEM((n_pieces, span, wide), jnp.float32),
-            pltpu.VMEM((n_pieces, rows, span), jnp.float32),
+            pltpu.VMEM((n_pieces, per_piece, tile, span), jnp.float32),
             pltpu.SemaphoreType.DMA((n_pieces,)),
-            pltpu.SemaphoreType.DMA((n_pieces, rows // TILE)),
+            pltpu.SemaphoreType.DMA((n_pieces, per_piece)),
             pltpu.VMEM((rows, wide), jnp.float32),
         ],
         out_shape=jax.ShapeDtypeStruct(out_shape, jnp.float32),
@@ -109,7 +113,7 @@
             transcendentals=0,
         ),
         name="project",
-    )(starts, strip, basis_t, *pieces)
+    )(starts, in_hbm[0], basis_t, *in_hbm[1:])
 
 
 def kept(leading, row, col, sub, height, width):
@@ -149,20 +153,22 @@
     )
     basis_t = lax.all_to_all(pair_t, ("col", "sub"), 0, 0, tiled=True).reshape(-1, 2 * block)
     received = swapped(give, "row")
-    own = jnp.concatenate([keep, received], axis=0)
 
-    before = shifted(own, "col", 1)
-    after = shifted(own, "col", -1)
-    across = shifted(own, "col", 2)
-    mine = [own, before, after, across]
-    theirs = [swapped(piece, "sub") for piece in mine]
+    mine, theirs = [], []
+    for half in (keep, received):
+        copies = [half]
+        for step in (1, -1, 2):
+            copies.append(shifted(half, "col", step))
+        mine.append(copies)
+        theirs.append([swapped(copy, "sub") for copy in copies])
+    pieces = [*zip(*mine), *zip(*theirs)]
 
     sources = [col, (col - 1) % n_col, (col + 1) % n_col, (col + 2) % n_col]
     starts = jnp.stack([2 * s + sub for s in sources] + [2 * s + 1 - sub for s in sources])
     share = basis_t.shape[0] // n_row
-    keep = kept(split_size[0], row, col, sub, share, 2 * basis_vectors.shape[1])
-    starts, keep = lax.optimization_barrier((starts.astype(jnp.int32), keep))
-    partial = projected(starts, strip, basis_t, mine + theirs, share)
+    inside = kept(split_size[0], row, col, sub, share, 2 * basis_vectors.shape[1])
+    starts, inside = lax.optimization_barrier((starts.astype(jnp.int32), inside))
+    partial = projected(starts, strip, basis_t, pieces, share)
 
     far = n_row // NEAR
     near_groups = [[NEAR * g + q for q in range(NEAR)] for g in range(far)]
@@ -175,7 +181,7 @@
     ).sum(0)
 
     child_block = lax.all_gather(proj_block, "sub", axis=1, tiled=True)
-    return jnp.where(keep, child_block, jnp.zeros((), jnp.float32))[None]
+    return jnp.where(inside, child_block, jnp.zeros((), jnp.float32))[None]
 
 
 def solution(mesh):

time: 209 us -> 216 us (1.033)
  starting transfers between devices: 80.6 us -> 94.9 us
  blocking collectives: 60.3 us -> 55.6 us
  waiting for transfers between devices: 40 us -> 37.3 us
    ppermute x3 -> x6, waiting for transfers between devices: 0.01 us -> 20.8 us  [shifted(): lax.ppermute(array, axis, [(i, (i + step) % size) for i in range(size)])]
    all_gather x1, waiting for transfers between devices: 18.4 us -> 0.01 us  [split_projection(): lax.all_gather(basis_vectors, 'row', axis=0, tiled=True, axis_index_group...]
    all_to_all x1, blocking collectives: 43.5 us -> 31 us  [split_projection(): lax.all_to_all(partial, 'row', 0, 0, tiled=True, axis_index_groups=far_gr...]
    all_to_all x1, waiting for transfers between devices: 11.6 us -> 0.01 us  [split_projection(): lax.all_to_all(pair_t, ('col', 'sub'), 0, 0, tiled=True)]
    ppermute x6 -> x10, starting transfers between devices: 22.1 us -> 31.3 us  [swapped(): return lax.ppermute(array, axis, [(i, i ^ 1) for i in range(size)])]
    ppermute x6 -> x10, waiting for transfers between devices: 9.19 us -> 15.7 us  [swapped(): return lax.ppermute(array, axis, [(i, i ^ 1) for i in range(size)])]
    all_to_all x1, blocking collectives: 11.6 us -> 16.6 us  [split_projection(): lax.all_to_all(partial, 'row', 0, 0, tiled=True, axis_index_groups=near_g...]
    ppermute x3 -> x6, starting transfers between devices: 15.4 us -> 19.2 us  [shifted(): lax.ppermute(array, axis, [(i, (i + step) % size) for i in range(size)])]
  transfers between devices with their start and end apart: 11 -> 18, of which waited for: 4 -> 7; matrix products, arithmetic and copies ran while one was open for 2% -> 1% of each run, Pallas kernels for 0% -> 0%
where the time goes in v5:
time: 216 us; the launch traced here: 215 us
  starting transfers between devices  94.9 us (44%)
  blocking collectives  55.6 us (26%)
  waiting for transfers between devices  37.3 us (17%)
  between operations  14.5 us (7%)
  Pallas kernels  8.43 us (4%)
  local copies, waits for them, and re-layouts  2.59 us (1%)
    all_to_all x1, starting transfers between devices, split_projection(): lax.all_to_all(pair_t, ('col', 'sub'), 0, 0, tiled=True)  44.4 us
    ppermute x10, starting transfers between devices, swapped(): return lax.ppermute(array, axis, [(i, i ^ 1) for i in range(size)])  31.3 us
    all_to_all x1, blocking collectives, split_projection(): lax.all_to_all(partial, 'row', 0, 0, tiled=True, axis_index_groups=far_gr...  31 us
    ppermute x6, waiting for transfers between devices, shifted(): lax.ppermute(array, axis, [(i, (i + step) % size) for i in range(size)])  20.8 us
    ppermute x6, starting transfers between devices, shifted(): lax.ppermute(array, axis, [(i, (i + step) % size) for i in range(size)])  19.2 us
    all_to_all x1, blocking collectives, split_projection(): lax.all_to_all(partial, 'row', 0, 0, tiled=True, axis_index_groups=near_g...  16.6 us
    ppermute x10, waiting for transfers between devices, swapped(): return lax.ppermute(array, axis, [(i, i ^ 1) for i in range(size)])  15.7 us
    pallas_call x1, Pallas kernels, projected(): pl.pallas_call(project_kernel, in_specs=[pl.BlockSpec(memory_space=pltpu....  8.43 us
  transfers between devices with their start and end apart: 18, of which 7 were waited for; matrix products, arithmetic and copies ran while one was open for 1% of the time, Pallas kernels for 0%

profile of v5, /device:TPU:33, one launch (start us, length us, event | category | flops | bytes accessed | tf_op | source)
XLA Modules:
  0.0 215.2 jit_solution(5558230334831195658)
XLA Ops:
  6.6 0.7 all-gather.2.cloned.1.call-update
  7.3 5.3 %collective-permute-start = (f32[256,128]{1,0:T(8,128)}, f32[256,128]{1,0:T(8,128)S(1)}, u32[]{:S(2)}, u32[]{:S(2)}) collective-permute-start(f32[256,128]{1,0:T(8,128)} %param.4), channel_id=1, source_target_pairs={{0,8},{8,0},{16,24},{24,16},{32,40},{40,32},{48,56},{56,48},{64,72... | collective-permute-start | bytes 393224 | tf_op jit(solution)/shard_map/ppermute | solution.py:20
  12.6 2.5 %collective-permute-done = f32[256,128]{1,0:T(8,128)S(1)} collective-permute-done((f32[256,128]{1,0:T(8,128)}, f32[256,128]{1,0:T(8,128)S(1)}, u32[]{:S(2)}, u32[]{:S(2)}) %collective-permute-start) | collective-permute-done | bytes 131104 | tf_op jit(solution)/shard_map/ppermute | solution.py:20
  15.1 0.9 maximum_bitcast_fusion
  16.2 1.6 broadcast_in_dim.7
  17.8 44.4 %all-to-all-start = ((f32[8,128,512]{2,1,0:T(8,128)}), f32[8,128,512]{2,1,0:T(8,128)S(1)}, u32[]{:S(2)}, u32[]{:S(2)}) async-start(f32[8,128,512]{2,1,0:T(8,128)} %broadcast_in_dim.7), calls=%async_computation | async-start | bytes 4194304 | tf_op jit(solution)/shard_map/all_to_all | solution.py:154
  62.3 2.0 collective-permute-start.1
  64.3 3.3 %collective-permute-start.2 = (f32[256,512]{1,0:T(8,128)S(1)}, f32[256,512]{1,0:T(8,128)S(1)}, u32[]{:S(2)}, u32[]{:S(2)}) collective-permute-start(f32[256,512]{1,0:T(8,128)S(1)} %pad_maximum_fusion.refs_0_), channel_id=1, source_target_pairs={{0,2},{2,4},{4,6},{6,0},{1,3},{3,5},{5,7},{7,1},{8,10},{10,12},{12... | collective-permute-start | bytes 1572872 | tf_op jit(solution)/shard_map/ppermute | solution.py:15
  67.6 3.2 %collective-permute-start.4 = (f32[256,512]{1,0:T(8,128)S(1)}, f32[256,512]{1,0:T(8,128)}, u32[]{:S(2)}, u32[]{:S(2)}) collective-permute-start(f32[256,512]{1,0:T(8,128)S(1)} %pad_maximum_fusion.refs_0_), channel_id=1, source_target_pairs={{0,6},{2,0},{4,2},{6,4},{1,7},{3,1},{5,3},{7,5},{8,14},{10,8},{12,... | collective-permute-start | bytes 1572872 | tf_op jit(solution)/shard_map/ppermute | solution.py:15
  70.9 3.6 %collective-permute-start.6 = (f32[256,512]{1,0:T(8,128)S(1)}, f32[256,512]{1,0:T(8,128)}, u32[]{:S(2)}, u32[]{:S(2)}) collective-permute-start(f32[256,512]{1,0:T(8,128)S(1)} %pad_maximum_fusion.refs_0_), channel_id=1, source_target_pairs={{0,4},{2,6},{4,0},{6,2},{1,5},{3,7},{5,1},{7,3},{8,12},{10,14},{12... | collective-permute-start | bytes 1572872 | tf_op jit(solution)/shard_map/ppermute | solution.py:15
  74.6 3.2 %collective-permute-start.8 = (f32[256,512]{1,0:T(8,128)S(1)}, f32[256,512]{1,0:T(8,128)S(1)}, u32[]{:S(2)}, u32[]{:S(2)}) collective-permute-start(f32[256,512]{1,0:T(8,128)S(1)} %pad_maximum_fusion.refs_0_), channel_id=1, source_target_pairs={{0,1},{1,0},{2,3},{3,2},{4,5},{5,4},{6,7},{7,6},{8,9},{9,8},{10,11... | collective-permute-start | bytes 1572872 | tf_op jit(solution)/shard_map/ppermute | solution.py:20
  77.7 12.2 %collective-permute-done.1.refs_1_ = f32[256,512]{1,0:T(8,128)S(1)} collective-permute-done((f32[256,512]{1,0:T(8,128)S(1)}, f32[256,512]{1,0:T(8,128)S(1)}, u32[]{:S(2)}, u32[]{:S(2)}) %collective-permute-start.1) | collective-permute-done | bytes 524320 | tf_op jit(solution)/shard_map/ppermute | solution.py:20
  89.9 4.4 %collective-permute-start.3 = (f32[256,512]{1,0:T(8,128)S(1)}, f32[256,512]{1,0:T(8,128)}, u32[]{:S(2)}, u32[]{:S(2)}) collective-permute-start(f32[256,512]{1,0:T(8,128)S(1)} %collective-permute-done.1.refs_1_), channel_id=1, source_target_pairs={{0,2},{2,4},{4,6},{6,0},{1,3},{3,5},{5,7},{7,1},{8,10},{10,12},{12... | collective-permute-start | bytes 1572872 | tf_op jit(solution)/shard_map/ppermute | solution.py:15
  94.4 5.2 %collective-permute-done.2.refs_2_ = f32[256,512]{1,0:T(8,128)S(1)} collective-permute-done((f32[256,512]{1,0:T(8,128)S(1)}, f32[256,512]{1,0:T(8,128)S(1)}, u32[]{:S(2)}, u32[]{:S(2)}) %collective-permute-start.2) | collective-permute-done | bytes 524320 | tf_op jit(solution)/shard_map/ppermute | solution.py:15
  99.6 2.4 %collective-permute-start.5 = (f32[256,512]{1,0:T(8,128)S(1)}, f32[256,512]{1,0:T(8,128)}, u32[]{:S(2)}, u32[]{:S(2)}) collective-permute-start(f32[256,512]{1,0:T(8,128)S(1)} %collective-permute-done.1.refs_1_), channel_id=1, source_target_pairs={{0,6},{2,0},{4,2},{6,4},{1,7},{3,1},{5,3},{7,5},{8,14},{10,8},{12,... | collective-permute-start | bytes 1572872 | tf_op jit(solution)/shard_map/ppermute | solution.py:15
  102.0 2.2 %collective-permute-start.7 = (f32[256,512]{1,0:T(8,128)S(1)}, f32[256,512]{1,0:T(8,128)}, u32[]{:S(2)}, u32[]{:S(2)}) collective-permute-start(f32[256,512]{1,0:T(8,128)S(1)} %collective-permute-done.1.refs_1_), channel_id=1, source_target_pairs={{0,4},{2,6},{4,0},{6,2},{1,5},{3,7},{5,1},{7,3},{8,12},{10,14},{12... | collective-permute-start | bytes 1572872 | tf_op jit(solution)/shard_map/ppermute | solution.py:15
  104.2 6.9 %collective-permute-done.6.refs_6_ = f32[256,512]{1,0:T(8,128)} collective-permute-done((f32[256,512]{1,0:T(8,128)S(1)}, f32[256,512]{1,0:T(8,128)}, u32[]{:S(2)}, u32[]{:S(2)}) %collective-permute-start.6) | collective-permute-done | bytes 524320 | tf_op jit(solution)/shard_map/ppermute | solution.py:15
  111.1 6.9 %collective-permute-start.9 = (f32[256,512]{1,0:T(8,128)S(1)}, f32[256,512]{1,0:T(8,128)S(1)}, u32[]{:S(2)}, u32[]{:S(2)}) collective-permute-start(f32[256,512]{1,0:T(8,128)S(1)} %collective-permute-done.1.refs_1_), channel_id=1, source_target_pairs={{0,1},{1,0},{2,3},{3,2},{4,5},{5,4},{6,7},{7,6},{8,9},{9,8},{10,11... | collective-permute-start | bytes 1572872 | tf_op jit(solution)/shard_map/ppermute | solution.py:20
  118.0 2.0 collective-permute-start.10
  120.0 2.2 %collective-permute-done.3.refs_3_ = f32[256,512]{1,0:T(8,128)} collective-permute-done((f32[256,512]{1,0:T(8,128)S(1)}, f32[256,512]{1,0:T(8,128)}, u32[]{:S(2)}, u32[]{:S(2)}) %collective-permute-start.3) | collective-permute-done | bytes 524320 | tf_op jit(solution)/shard_map/ppermute | solution.py:15
  122.2 2.9 %collective-permute-start.12 = (f32[256,512]{1,0:T(8,128)}, f32[256,512]{1,0:T(8,128)}, u32[]{:S(2)}, u32[]{:S(2)}) collective-permute-start(f32[256,512]{1,0:T(8,128)} %collective-permute-done.4.refs_4_), channel_id=1, source_target_pairs={{0,1},{1,0},{2,3},{3,2},{4,5},{5,4},{6,7},{7,6},{8,9},{9,8},{10,11... | collective-permute-start | bytes 1572872 | tf_op jit(solution)/shard_map/ppermute | solution.py:20
  125.1 2.0 collective-permute-start.14
  127.0 6.5 %collective-permute-done.7.refs_7_ = f32[256,512]{1,0:T(8,128)} collective-permute-done((f32[256,512]{1,0:T(8,128)S(1)}, f32[256,512]{1,0:T(8,128)}, u32[]{:S(2)}, u32[]{:S(2)}) %collective-permute-start.7) | collective-permute-done | bytes 524320 | tf_op jit(solution)/shard_map/ppermute | solution.py:15
  133.6 2.9 %collective-permute-start.11 = (f32[256,512]{1,0:T(8,128)}, f32[256,512]{1,0:T(8,128)}, u32[]{:S(2)}, u32[]{:S(2)}) collective-permute-start(f32[256,512]{1,0:T(8,128)} %collective-permute-done.3.refs_3_), channel_id=1, source_target_pairs={{0,1},{1,0},{2,3},{3,2},{4,5},{5,4},{6,7},{7,6},{8,9},{9,8},{10,11... | collective-permute-start | bytes 1572872 | tf_op jit(solution)/shard_map/ppermute | solution.py:20
  136.5 2.0 collective-permute-start.13
  138.5 0.8 copy-done.6
  139.3 2.4 %collective-permute-start.15 = (f32[256,512]{1,0:T(8,128)}, f32[256,512]{1,0:T(8,128)}, u32[]{:S(2)}, u32[]{:S(2)}) collective-permute-start(f32[256,512]{1,0:T(8,128)} %collective-permute-done.7.refs_7_), channel_id=1, source_target_pairs={{0,1},{1,0},{2,3},{3,2},{4,5},{5,4},{6,7},{7,6},{8,9},{9,8},{10,11... | collective-permute-start | bytes 1572872 | tf_op jit(solution)/shard_map/ppermute | solution.py:20
  142.6 0.9 collective-permute-done.15.refs_15_
  143.6 8.4 %project.1 = f32[4,8,32,128]{3,2,1,0:T(8,128)S(1)} custom-call(s32[8]{0:T(128)S(1)} %stack.35.starts, f32[4096,128]{1,0:T(8,128)} %all-gather.2.cloned.1.call-done.strip, f32[1024,512]{1,0:T(8,128)S(1)} %bitcast.16, f32[256,512]{1,0:T(8,128)} %copy-done, f32[256,512]{1,0:T(8,128)} %copy-done.2, f32[256,512]{1,0:T(8,128)} %copy-done.3, ...), custom_call_target="tpu_custom_call" | custom-call | flops 2013265920 | bytes 12582912 | tf_op jit(solution)/shard_map/project/pallas_call | solution.py:96
  152.0 16.6 %all_to_all.15 = f32[4,8,32,128]{3,2,1,0:T(8,128)S(1)} all-to-all(f32[4,8,32,128]{3,2,1,0:T(8,128)S(1)} %project.1), channel_id=1, replica_groups={{0,8,16,24},{32,40,48,56},{64,72,80,88},{96,104,112,120},{128,136,144,1..., dimensions={0} | all-to-all | bytes 1048576 | tf_op jit(solution)/shard_map/all_to_all | solution.py:176
  168.7 31.0 %all_to_all.16 = f32[8,32,128]{2,1,0:T(8,128)S(1)} all-to-all(f32[8,32,128]{2,1,0:T(8,128)S(1)} %reduce_sum.18), channel_id=1, replica_groups={{0,32,64,96,128,160,192,224},{8,40,72,104,136,168,200,232},{16,48,80,11..., dimensions={0} | all-to-all | bytes 262144 | tf_op jit(solution)/shard_map/all_to_all | solution.py:179
  199.7 8.0 %all_gather.7 = f32[32,256]{1,0:T(8,128)S(1)} all-gather(f32[32,128]{1,0:T(8,128)S(1)} %reduce_sum.19), channel_id=1, replica_groups=mesh['groups'=2,'row'=32,'col'=4,'sub'=2] {'sub'}, dimensions={1}, use_global_device_ids=true | all-gather | bytes 49152 | tf_op jit(solution)/shard_map/all_gather | solution.py:183
  (36 shorter events, 1.2 us)
Async XLA Ops:
  6.5 137.0 %all-gather.2.cloned.1.call-start = ((), (), s32[]{:S(2)}) async-start(), calls=%async_computation.3 | async-start | bytes 2228224 | tf_op jit(solution)/shard_map/all_gather | solution.py:139
  7.3 7.8 %collective-permute-start = (f32[256,128]{1,0:T(8,128)}, f32[256,128]{1,0:T(8,128)S(1)}, u32[]{:S(2)}, u32[]{:S(2)}) collective-permute-start(f32[256,128]{1,0:T(8,128)} %param.4), channel_id=1, source_target_pairs={{0,8},{8,0},{16,24},{24,16},{32,40},{40,32},{48,56},{56,48},{64,72... | collective-permute-start | bytes 393224 | tf_op jit(solution)/shard_map/ppermute | solution.py:20
  17.8 44.4 %copy-start.1 = (f32[256,1024]{1,0:T(8,128)S(1)}, f32[256,1024]{1,0:T(8,128)}, u32[]{:S(2)}) copy-start(f32[256,1024]{1,0:T(8,128)} %param.3) | copy-start | bytes 3145732
  17.8 125.8 %all-to-all-start = ((f32[8,128,512]{2,1,0:T(8,128)}), f32[8,128,512]{2,1,0:T(8,128)S(1)}, u32[]{:S(2)}, u32[]{:S(2)}) async-start(f32[8,128,512]{2,1,0:T(8,128)} %broadcast_in_dim.7), calls=%async_computation | async-start | bytes 4194304 | tf_op jit(solution)/shard_map/all_to_all | solution.py:154
  62.3 27.7 %collective-permute-start.1 = (f32[256,512]{1,0:T(8,128)S(1)}, f32[256,512]{1,0:T(8,128)S(1)}, u32[]{:S(2)}, u32[]{:S(2)}) collective-permute-start(f32[256,512]{1,0:T(8,128)S(1)} %pad_maximum_fusion.1), channel_id=1, source_target_pairs={{0,8},{8,0},{16,24},{24,16},{32,40},{40,32},{48,56},{56,48},{64,72... | collective-permute-start | bytes 1572872 | tf_op jit(solution)/shard_map/ppermute | solution.py:20
  64.3 79.3 %copy-start = (f32[256,512]{1,0:T(8,128)}, f32[256,512]{1,0:T(8,128)S(1)}, u32[]{:S(2)}) copy-start(f32[256,512]{1,0:T(8,128)S(1)} %pad_maximum_fusion.refs_0_) | copy-start | bytes 1572868
  64.3 35.3 %collective-permute-start.2 = (f32[256,512]{1,0:T(8,128)S(1)}, f32[256,512]{1,0:T(8,128)S(1)}, u32[]{:S(2)}, u32[]{:S(2)}) collective-permute-start(f32[256,512]{1,0:T(8,128)S(1)} %pad_maximum_fusion.refs_0_), channel_id=1, source_target_pairs={{0,2},{2,4},{4,6},{6,0},{1,3},{3,5},{5,7},{7,1},{8,10},{10,12},{12... | collective-permute-start | bytes 1572872 | tf_op jit(solution)/shard_map/ppermute | solution.py:15
  67.6 34.4 %collective-permute-start.4 = (f32[256,512]{1,0:T(8,128)S(1)}, f32[256,512]{1,0:T(8,128)}, u32[]{:S(2)}, u32[]{:S(2)}) collective-permute-start(f32[256,512]{1,0:T(8,128)S(1)} %pad_maximum_fusion.refs_0_), channel_id=1, source_target_pairs={{0,6},{2,0},{4,2},{6,4},{1,7},{3,1},{5,3},{7,5},{8,14},{10,8},{12,... | collective-permute-start | bytes 1572872 | tf_op jit(solution)/shard_map/ppermute | solution.py:15
  70.9 40.2 %collective-permute-start.6 = (f32[256,512]{1,0:T(8,128)S(1)}, f32[256,512]{1,0:T(8,128)}, u32[]{:S(2)}, u32[]{:S(2)}) collective-permute-start(f32[256,512]{1,0:T(8,128)S(1)} %pad_maximum_fusion.refs_0_), channel_id=1, source_target_pairs={{0,4},{2,6},{4,0},{6,2},{1,5},{3,7},{5,1},{7,3},{8,12},{10,14},{12... | collective-permute-start | bytes 1572872 | tf_op jit(solution)/shard_map/ppermute | solution.py:15
  74.6 43.4 %collective-permute-start.8 = (f32[256,512]{1,0:T(8,128)S(1)}, f32[256,512]{1,0:T(8,128)S(1)}, u32[]{:S(2)}, u32[]{:S(2)}) collective-permute-start(f32[256,512]{1,0:T(8,128)S(1)} %pad_maximum_fusion.refs_0_), channel_id=1, source_target_pairs={{0,1},{1,0},{2,3},{3,2},{4,5},{5,4},{6,7},{7,6},{8,9},{9,8},{10,11... | collective-permute-start | bytes 1572872 | tf_op jit(solution)/shard_map/ppermute | solution.py:20
  89.9 53.6 %copy-start.2 = (f32[256,512]{1,0:T(8,128)}, f32[256,512]{1,0:T(8,128)S(1)}, u32[]{:S(2)}) copy-start(f32[256,512]{1,0:T(8,128)S(1)} %collective-permute-done.1.refs_1_) | copy-start | bytes 1572868
  89.9 32.2 %collective-permute-start.3 = (f32[256,512]{1,0:T(8,128)S(1)}, f32[256,512]{1,0:T(8,128)}, u32[]{:S(2)}, u32[]{:S(2)}) collective-permute-start(f32[256,512]{1,0:T(8,128)S(1)} %collective-permute-done.1.refs_1_), channel_id=1, source_target_pairs={{0,2},{2,4},{4,6},{6,0},{1,3},{3,5},{5,7},{7,1},{8,10},{10,12},{12... | collective-permute-start | bytes 1572872 | tf_op jit(solution)/shard_map/ppermute | solution.py:15
  99.6 36.9 %copy-start.3 = (f32[256,512]{1,0:T(8,128)}, f32[256,512]{1,0:T(8,128)S(1)}, u32[]{:S(2)}) copy-start(f32[256,512]{1,0:T(8,128)S(1)} %collective-permute-done.2.refs_2_) | copy-start | bytes 1572868
  99.6 25.5 %collective-permute-start.5 = (f32[256,512]{1,0:T(8,128)S(1)}, f32[256,512]{1,0:T(8,128)}, u32[]{:S(2)}, u32[]{:S(2)}) collective-permute-start(f32[256,512]{1,0:T(8,128)S(1)} %collective-permute-done.1.refs_1_), channel_id=1, source_target_pairs={{0,6},{2,0},{4,2},{6,4},{1,7},{3,1},{5,3},{7,5},{8,14},{10,8},{12,... | collective-permute-start | bytes 1572872 | tf_op jit(solution)/shard_map/ppermute | solution.py:15
  102.0 31.5 %collective-permute-start.7 = (f32[256,512]{1,0:T(8,128)S(1)}, f32[256,512]{1,0:T(8,128)}, u32[]{:S(2)}, u32[]{:S(2)}) collective-permute-start(f32[256,512]{1,0:T(8,128)S(1)} %collective-permute-done.1.refs_1_), channel_id=1, source_target_pairs={{0,4},{2,6},{4,0},{6,2},{1,5},{3,7},{5,1},{7,3},{8,12},{10,14},{12... | collective-permute-start | bytes 1572872 | tf_op jit(solution)/shard_map/ppermute | solution.py:15
  111.1 25.4 %collective-permute-start.9 = (f32[256,512]{1,0:T(8,128)S(1)}, f32[256,512]{1,0:T(8,128)S(1)}, u32[]{:S(2)}, u32[]{:S(2)}) collective-permute-start(f32[256,512]{1,0:T(8,128)S(1)} %collective-permute-done.1.refs_1_), channel_id=1, source_target_pairs={{0,1},{1,0},{2,3},{3,2},{4,5},{5,4},{6,7},{7,6},{8,9},{9,8},{10,11... | collective-permute-start | bytes 1572872 | tf_op jit(solution)/shard_map/ppermute | solution.py:20
  118.0 20.4 %copy-start.4 = (f32[256,512]{1,0:T(8,128)}, f32[256,512]{1,0:T(8,128)S(1)}, u32[]{:S(2)}) copy-start(f32[256,512]{1,0:T(8,128)S(1)} %collective-permute-done.8.refs_8_) | copy-start | bytes 1572868
  118.0 20.4 %collective-permute-start.10 = (f32[256,512]{1,0:T(8,128)S(1)}, f32[256,512]{1,0:T(8,128)S(1)}, u32[]{:S(2)}, u32[]{:S(2)}) collective-permute-start(f32[256,512]{1,0:T(8,128)S(1)} %collective-permute-done.2.refs_2_), channel_id=1, source_target_pairs={{0,1},{1,0},{2,3},{3,2},{4,5},{5,4},{6,7},{7,6},{8,9},{9,8},{10,11... | collective-permute-start | bytes 1572872 | tf_op jit(solution)/shard_map/ppermute | solution.py:20
  122.2 20.4 %collective-permute-start.12 = (f32[256,512]{1,0:T(8,128)}, f32[256,512]{1,0:T(8,128)}, u32[]{:S(2)}, u32[]{:S(2)}) collective-permute-start(f32[256,512]{1,0:T(8,128)} %collective-permute-done.4.refs_4_), channel_id=1, source_target_pairs={{0,1},{1,0},{2,3},{3,2},{4,5},{5,4},{6,7},{7,6},{8,9},{9,8},{10,11... | collective-permute-start | bytes 1572872 | tf_op jit(solution)/shard_map/ppermute | solution.py:20
  125.1 17.5 %collective-permute-start.14 = (f32[256,512]{1,0:T(8,128)}, f32[256,512]{1,0:T(8,128)}, u32[]{:S(2)}, u32[]{:S(2)}) collective-permute-start(f32[256,512]{1,0:T(8,128)} %collective-permute-done.6.refs_6_), channel_id=1, source_target_pairs={{0,1},{1,0},{2,3},{3,2},{4,5},{5,4},{6,7},{7,6},{8,9},{9,8},{10,11... | collective-permute-start | bytes 1572872 | tf_op jit(solution)/shard_map/ppermute | solution.py:20
  133.6 9.1 %collective-permute-start.11 = (f32[256,512]{1,0:T(8,128)}, f32[256,512]{1,0:T(8,128)}, u32[]{:S(2)}, u32[]{:S(2)}) collective-permute-start(f32[256,512]{1,0:T(8,128)} %collective-permute-done.3.refs_3_), channel_id=1, source_target_pairs={{0,1},{1,0},{2,3},{3,2},{4,5},{5,4},{6,7},{7,6},{8,9},{9,8},{10,11... | collective-permute-start | bytes 1572872 | tf_op jit(solution)/shard_map/ppermute | solution.py:20
  136.5 2.0 copy-start.5
  136.5 6.1 %collective-permute-start.13 = (f32[256,512]{1,0:T(8,128)}, f32[256,512]{1,0:T(8,128)}, u32[]{:S(2)}, u32[]{:S(2)}) collective-permute-start(f32[256,512]{1,0:T(8,128)} %collective-permute-done.5.refs_5_), channel_id=1, source_target_pairs={{0,1},{1,0},{2,3},{3,2},{4,5},{5,4},{6,7},{7,6},{8,9},{9,8},{10,11... | collective-permute-start | bytes 1572872 | tf_op jit(solution)/shard_map/ppermute | solution.py:20
  138.5 0.8 copy-start.6
  139.3 4.3 %collective-permute-start.15 = (f32[256,512]{1,0:T(8,128)}, f32[256,512]{1,0:T(8,128)}, u32[]{:S(2)}, u32[]{:S(2)}) collective-permute-start(f32[256,512]{1,0:T(8,128)} %collective-permute-done.7.refs_7_), channel_id=1, source_target_pairs={{0,1},{1,0},{2,3},{3,2},{4,5},{5,4},{6,7},{7,6},{8,9},{9,8},{10,11... | collective-permute-start | bytes 1572872 | tf_op jit(solution)/shard_map/ppermute | solution.py:20
Sparse Core Ops, SparseCore 0:
  9.4 120.2 all-gather.1

commit v6 on v4

--- a/solution.py
+++ b/solution.py
@@ -31,11 +31,14 @@
     return jnp.dot(left, right, preferred_element_type=jnp.float32)
 
 
-def project_kernel(starts, strip, basis_t, *refs):
-    *pieces, out, chunks, tiles, arrived, landed, image = refs
+def project_kernel(starts, strip, basis_mine, basis_theirs, *refs):
+    *pieces, out, chunks, tiles, other, arrived, landed, given, image = refs
     wide = strip.shape[1]
     span = chunks.shape[1]
     per_piece = tiles.shape[1] // TILE
+    n_pieces = chunks.shape[0]
+    n_whole = (n_pieces * per_piece - len(pieces)) // (per_piece - 1)
+    core = starts[n_pieces]
 
     def chunk_copy(n):
         rows = pl.ds(pl.multiple_of(starts[n] * span, span), span)
@@ -43,7 +46,11 @@
 
     def tile_copy(n, t):
         rows = pl.ds(t * TILE, TILE)
-        return pltpu.make_async_copy(pieces[n].at[rows], tiles.at[n, rows], landed.at[n, t])
+        if n < n_whole:
+            source = pieces[n].at[rows]
+        else:
+            source = pieces[n_whole + (n - n_whole) * per_piece + t]
+        return pltpu.make_async_copy(source, tiles.at[n, rows], landed.at[n, t])
 
     def begin(n):
         chunk_copy(n).start()
@@ -52,9 +59,12 @@
 
     for n in range(AHEAD):
         begin(n)
-    for n in range(len(pieces)):
-        if n + AHEAD < len(pieces):
+    fetch_basis = pltpu.make_async_copy(basis_theirs, other, given)
+    for n in range(n_pieces):
+        if n + AHEAD < n_pieces:
             begin(n + AHEAD)
+        if n + AHEAD == n_pieces:
+            fetch_basis.start()
         chunk_copy(n).wait()
         high, low = halves(chunks[n])
         right = jnp.concatenate([high, low], axis=1)
@@ -71,45 +81,51 @@
 
     high, low = halves(image[...])
     right = jnp.concatenate([high, low], axis=1)
+    fetch_basis.wait()
     near, far, share = out.shape[:3]
-    for f in range(far):
-        rows = near * share
-        left_high, left_low = halves(basis_t[f * rows : (f + 1) * rows, :])
-        both = dot(left_high, right)
-        proj = both[:, :wide] + (both[:, wide:] + dot(left_low, high))
-        for q in range(near):
-            out[q, f] = proj[q * share : (q + 1) * share]
-
-
-def projected(starts, strip, basis_t, pieces, share):
-    rows, span = pieces[0].shape
-    total, wide = basis_t.shape[0], strip.shape[1]
-    n_pieces = len(pieces)
+    for basis, which in ((basis_mine, core), (other, 1 - core)):
+        for f in range(far // 2):
+            left_high, left_low = halves(basis[f])
+            both = dot(left_high, right)
+            proj = both[:, :wide] + (both[:, wide:] + dot(left_low, high))
+            for q in range(near):
+                out[q, 2 * f + which] = proj[q * share : (q + 1) * share]
+
+
+def projected(starts, strip, basis, whole, halved, share):
+    rows, span = whole[0].shape
+    wide = strip.shape[1]
+    total = 2 * basis[0].shape[0] * basis[0].shape[1]
+    n_pieces = len(whole) + len(halved)
+    pieces = [*whole, *(half for pair in halved for half in pair)]
     out_shape = (NEAR, total // share // NEAR, share, wide)
     vmem = pl.BlockSpec(memory_space=pltpu.VMEM)
     anywhere = pl.BlockSpec(memory_space=pl.ANY)
     strip = pltpu.with_memory_space_constraint(strip, pltpu.HBM)
+    basis_theirs = pltpu.with_memory_space_constraint(basis[1], pltpu.HBM)
     return pl.pallas_call(
         project_kernel,
-        in_specs=[pl.BlockSpec(memory_space=pltpu.SMEM), anywhere, vmem]
-        + [anywhere] * n_pieces,
+        in_specs=[pl.BlockSpec(memory_space=pltpu.SMEM), anywhere, vmem, anywhere]
+        + [anywhere] * len(pieces),
         out_specs=vmem,
         scratch_shapes=[
             pltpu.VMEM((n_pieces, span, wide), jnp.float32),
             pltpu.VMEM((n_pieces, rows, span), jnp.float32),
+            pltpu.VMEM(basis[1].shape, jnp.float32),
             pltpu.SemaphoreType.DMA((n_pieces,)),
             pltpu.SemaphoreType.DMA((n_pieces, rows // TILE)),
+            pltpu.SemaphoreType.DMA(()),
             pltpu.VMEM((rows, wide), jnp.float32),
         ],
         out_shape=jax.ShapeDtypeStruct(out_shape, jnp.float32),
         compiler_params=pltpu.CompilerParams(vmem_limit_bytes=32 * 2**20),
         cost_estimate=pl.CostEstimate(
             flops=3 * 2 * rows * wide * (strip.shape[0] + total),
-            bytes_accessed=4 * (strip.size + basis_t.size + rows * strip.shape[0]),
+            bytes_accessed=4 * (strip.size + 2 * basis[0].size + rows * strip.shape[0]),
             transcendentals=0,
         ),
         name="project",
-    )(starts, strip, basis_t, *pieces)
+    )(starts, strip, basis[0], basis_theirs, *pieces)
 
 
 def kept(leading, row, col, sub, height, width):
@@ -138,7 +154,7 @@
 
     mate = swapped(basis_vectors, "row")
     pair_t = jnp.concatenate([basis_vectors, mate], axis=0).T
-    pair_t = jnp.broadcast_to(pair_t[None], (n_col * lax.axis_size("sub"), *pair_t.shape))
+    pair_t = jnp.broadcast_to(pair_t[None], (n_col, *pair_t.shape))
 
     blocks = [matrix[:, i * block : (i + 1) * block] for i in range(width // block)]
     keep = jnp.concatenate(
@@ -147,22 +163,29 @@
     give = jnp.concatenate(
         [jnp.where(even, b, a) for a, b in zip(blocks[::2], blocks[1::2])], axis=1
     )
-    basis_t = lax.all_to_all(pair_t, ("col", "sub"), 0, 0, tiled=True).reshape(-1, 2 * block)
+    basis_mine = lax.all_to_all(pair_t, "col", 0, 0, tiled=True)
     received = swapped(give, "row")
     own = jnp.concatenate([keep, received], axis=0)
 
     before = shifted(own, "col", 1)
     after = shifted(own, "col", -1)
-    across = shifted(own, "col", 2)
-    mine = [own, before, after, across]
+    across = (shifted(before[:block], "col", 1), shifted(after[block:], "col", -1))
+    mine = [own, before, after]
     theirs = [swapped(piece, "sub") for piece in mine]
-
-    sources = [col, (col - 1) % n_col, (col + 1) % n_col, (col + 2) % n_col]
-    starts = jnp.stack([2 * s + sub for s in sources] + [2 * s + 1 - sub for s in sources])
-    share = basis_t.shape[0] // n_row
+    across_other = tuple(swapped(piece, "sub") for piece in across)
+    basis = (basis_mine, swapped(basis_mine, "sub"))
+
+    sources = [col, (col - 1) % n_col, (col + 1) % n_col]
+    opposite = (col + 2) % n_col
+    starts = jnp.stack(
+        [2 * s + sub for s in sources]
+        + [2 * s + 1 - sub for s in sources]
+        + [2 * opposite + sub, 2 * opposite + 1 - sub, sub]
+    )
+    share = 2 * n_col * basis_vectors.shape[1] // n_row
     keep = kept(split_size[0], row, col, sub, share, 2 * basis_vectors.shape[1])
     starts, keep = lax.optimization_barrier((starts.astype(jnp.int32), keep))
-    partial = projected(starts, strip, basis_t, mine + theirs, share)
+    partial = projected(starts, strip, basis, mine + theirs, (across, across_other), share)
 
     far = n_row // NEAR
     near_groups = [[NEAR * g + q for q in range(NEAR)] for g in range(far)]

time: 209 us -> 209 us (level)
  blocking collectives: 60.3 us -> 74.8 us
  waiting for transfers between devices: 40 us -> 31.8 us
  starting transfers between devices: 80.6 us -> 75.2 us
    all_to_all x1 -> x0, starting transfers between devices: 43.1 us -> none  [split_projection(): lax.all_to_all(pair_t, ('col', 'sub'), 0, 0, tiled=True)]
    ppermute x6 -> x8, starting transfers between devices: 22.1 us -> 58 us  [swapped(): return lax.ppermute(array, axis, [(i, i ^ 1) for i in range(size)])]
    all_to_all x0 -> x1, blocking collectives: none -> 16.7 us  [split_projection(): basis_mine = lax.all_to_all(pair_t, 'col', 0, 0, tiled=True)]
    all_to_all x1 -> x0, waiting for transfers between devices: 11.6 us -> none  [split_projection(): lax.all_to_all(pair_t, ('col', 'sub'), 0, 0, tiled=True)]
    all_gather x1, waiting for transfers between devices: 18.4 us -> 7.58 us  [split_projection(): lax.all_gather(basis_vectors, 'row', axis=0, tiled=True, axis_index_group...]
    ppermute x6 -> x8, waiting for transfers between devices: 9.19 us -> 16.9 us  [swapped(): return lax.ppermute(array, axis, [(i, i ^ 1) for i in range(size)])]
    ppermute x3 -> x4, waiting for transfers between devices: 0.01 us -> 6.59 us  [shifted(): lax.ppermute(array, axis, [(i, (i + step) % size) for i in range(size)])]
    all_to_all x1, blocking collectives: 43.5 us -> 40.8 us  [split_projection(): lax.all_to_all(partial, 'row', 0, 0, tiled=True, axis_index_groups=far_gr...]
  transfers between devices with their start and end apart: 11 -> 13, of which waited for: 4 -> 6; matrix products, arithmetic and copies ran while one was open for 2% -> 1% of each run, Pallas kernels for 0% -> 0%
where the time goes in v6:
time: 209 us; the launch traced here: 208 us
  starting transfers between devices  75.2 us (36%)
  blocking collectives  74.8 us (36%)
  waiting for transfers between devices  31.8 us (15%)
  between operations  14.4 us (7%)
  Pallas kernels  7.66 us (4%)
  other arithmetic  2.22 us (1%)
    ppermute x8, starting transfers between devices, swapped(): return lax.ppermute(array, axis, [(i, i ^ 1) for i in range(size)])  58 us
    all_to_all x1, blocking collectives, split_projection(): lax.all_to_all(partial, 'row', 0, 0, tiled=True, axis_index_groups=far_gr...  40.8 us
    ppermute x4, starting transfers between devices, shifted(): lax.ppermute(array, axis, [(i, (i + step) % size) for i in range(size)])  17.3 us
    ppermute x8, waiting for transfers between devices, swapped(): return lax.ppermute(array, axis, [(i, i ^ 1) for i in range(size)])  16.9 us
    all_to_all x1, blocking collectives, split_projection(): basis_mine = lax.all_to_all(pair_t, 'col', 0, 0, tiled=True)  16.7 us
    all_to_all x1, blocking collectives, split_projection(): lax.all_to_all(partial, 'row', 0, 0, tiled=True, axis_index_groups=near_g...  11.6 us
    pallas_call x1, Pallas kernels, projected(): pl.pallas_call(project_kernel, in_specs=[pl.BlockSpec(memory_space=pltpu....  7.66 us
    all_gather x1, waiting for transfers between devices, split_projection(): lax.all_gather(basis_vectors, 'row', axis=0, tiled=True, axis_index_group...  7.58 us
  transfers between devices with their start and end apart: 13, of which 6 were waited for; matrix products, arithmetic and copies ran while one was open for 1% of the time, Pallas kernels for 0%

profile of v6, /device:TPU:33, one launch (start us, length us, event | category | flops | bytes accessed | tf_op | source)
XLA Modules:
  0.0 207.6 jit_solution(3818459067177279738)
XLA Ops:
  6.6 0.7 all-gather.2.cloned.1.call-update
  7.3 1.3 slice_select_fusion.3
  8.7 5.3 %collective-permute-start.2 = (f32[256,512]{1,0:T(8,128)S(1)}, f32[256,512]{1,0:T(8,128)S(1)}, u32[]{:S(2)}, u32[]{:S(2)}) collective-permute-start(f32[256,512]{1,0:T(8,128)S(1)} %pad_maximum_fusion.1), channel_id=1, source_target_pairs={{0,8},{8,0},{16,24},{24,16},{32,40},{40,32},{48,56},{56,48},{64,72... | collective-permute-start | bytes 1572872 | tf_op jit(solution)/shard_map/ppermute | solution.py:21
  14.0 6.6 %collective-permute-done.2 = f32[256,512]{1,0:T(8,128)S(1)} collective-permute-done((f32[256,512]{1,0:T(8,128)S(1)}, f32[256,512]{1,0:T(8,128)S(1)}, u32[]{:S(2)}, u32[]{:S(2)}) %collective-permute-start.2) | collective-permute-done | bytes 524320 | tf_op jit(solution)/shard_map/ppermute | solution.py:21
  20.5 0.1 pad_maximum_fusion.refs_0_
  20.6 9.9 %collective-permute-start.4 = (f32[512,512]{1,0:T(8,128)S(1)}, f32[512,512]{1,0:T(8,128)S(1)}, u32[]{:S(2)}, u32[]{:S(2)}) collective-permute-start(f32[512,512]{1,0:T(8,128)S(1)} %pad_maximum_fusion.refs_0_), channel_id=1, source_target_pairs={{0,6},{2,0},{4,2},{6,4},{1,7},{3,1},{5,3},{7,5},{8,14},{10,8},{12,... | collective-permute-start | bytes 3145736 | tf_op jit(solution)/shard_map/ppermute | solution.py:16
  30.6 2.0 collective-permute-start.3
  32.5 36.7 %collective-permute-start.5 = (f32[512,512]{1,0:T(8,128)S(1)}, f32[512,512]{1,0:T(8,128)}, u32[]{:S(2)}, u32[]{:S(2)}) collective-permute-start(f32[512,512]{1,0:T(8,128)S(1)} %pad_maximum_fusion.refs_0_), channel_id=1, source_target_pairs={{0,1},{1,0},{2,3},{3,2},{4,5},{5,4},{6,7},{7,6},{8,9},{9,8},{10,11... | collective-permute-start | bytes 3145736 | tf_op jit(solution)/shard_map/ppermute | solution.py:21
  69.2 2.0 collective-permute-start
  71.2 9.4 %collective-permute-done = f32[256,128]{1,0:T(8,128)S(1)} collective-permute-done((f32[256,128]{1,0:T(8,128)S(1)}, f32[256,128]{1,0:T(8,128)S(1)}, u32[]{:S(2)}, u32[]{:S(2)}) %collective-permute-start) | collective-permute-done | bytes 131104 | tf_op jit(solution)/shard_map/ppermute | solution.py:21
  80.6 0.1 copy.5
  80.8 0.1 broadcast_in_dim.7
  80.9 16.7 %all_to_all.15.basis_mine = f32[4,128,512]{2,1,0:T(8,128)S(1)} all-to-all(f32[4,128,512]{2,1,0:T(8,128)S(1)} %broadcast_in_dim.7), channel_id=1, replica_groups=mesh['groups'=2,'row'=32,'col'=4,'sub'=2] {'col'}, dimensions={0} | all-to-all | bytes 2097152 | tf_op jit(solution)/shard_map/all_to_all | solution.py:166
  97.5 3.8 %collective-permute-start.1 = (f32[4,128,512]{2,1,0:T(8,128)S(1)}, f32[4,128,512]{2,1,0:T(8,128)}, u32[]{:S(2)}, u32[]{:S(2)}) collective-permute-start(f32[4,128,512]{2,1,0:T(8,128)S(1)} %all_to_all.15.basis_mine), channel_id=1, source_target_pairs={{0,1},{1,0},{2,3},{3,2},{4,5},{5,4},{6,7},{7,6},{8,9},{9,8},{10,11... | collective-permute-start | bytes 3145736 | tf_op jit(solution)/shard_map/ppermute | solution.py:21
  101.4 2.8 %collective-permute-start.9 = (f32[256,512]{1,0:T(8,128)S(1)}, f32[256,512]{1,0:T(8,128)}, u32[]{:S(2)}, u32[]{:S(2)}) collective-permute-start(f32[256,512]{1,0:T(8,128)S(1)} %slice.25), channel_id=1, source_target_pairs={{0,6},{2,0},{4,2},{6,4},{1,7},{3,1},{5,3},{7,5},{8,14},{10,8},{12,... | collective-permute-start | bytes 1572872 | tf_op jit(solution)/shard_map/ppermute | solution.py:16
  104.2 1.1 slice.24
  105.3 2.5 %collective-permute-start.8 = (f32[256,512]{1,0:T(8,128)S(1)}, f32[256,512]{1,0:T(8,128)}, u32[]{:S(2)}, u32[]{:S(2)}) collective-permute-start(f32[256,512]{1,0:T(8,128)S(1)} %slice.24), channel_id=1, source_target_pairs={{0,2},{2,4},{4,6},{6,0},{1,3},{3,5},{5,7},{7,1},{8,10},{10,12},{12... | collective-permute-start | bytes 1572872 | tf_op jit(solution)/shard_map/ppermute | solution.py:16
  107.8 2.5 %collective-permute-start.7 = (f32[512,512]{1,0:T(8,128)S(1)}, f32[512,512]{1,0:T(8,128)}, u32[]{:S(2)}, u32[]{:S(2)}) collective-permute-start(f32[512,512]{1,0:T(8,128)S(1)} %collective-permute-done.4.refs_2_), channel_id=1, source_target_pairs={{0,1},{1,0},{2,3},{3,2},{4,5},{5,4},{6,7},{7,6},{8,9},{9,8},{10,11... | collective-permute-start | bytes 3145736 | tf_op jit(solution)/shard_map/ppermute | solution.py:21
  110.4 2.0 collective-permute-start.6
  112.3 4.6 %collective-permute-done.9.refs_7_ = f32[256,512]{1,0:T(8,128)} collective-permute-done((f32[256,512]{1,0:T(8,128)S(1)}, f32[256,512]{1,0:T(8,128)}, u32[]{:S(2)}, u32[]{:S(2)}) %collective-permute-start.9) | collective-permute-done | bytes 524320 | tf_op jit(solution)/shard_map/ppermute | solution.py:16
  116.9 2.8 %collective-permute-start.11 = (f32[256,512]{1,0:T(8,128)}, f32[256,512]{1,0:T(8,128)}, u32[]{:S(2)}, u32[]{:S(2)}) collective-permute-start(f32[256,512]{1,0:T(8,128)} %collective-permute-done.9.refs_7_), channel_id=1, source_target_pairs={{0,1},{1,0},{2,3},{3,2},{4,5},{5,4},{6,7},{7,6},{8,9},{9,8},{10,11... | collective-permute-start | bytes 1572872 | tf_op jit(solution)/shard_map/ppermute | solution.py:21
  119.7 2.0 collective-permute-done.8.refs_6_
  121.7 3.1 %collective-permute-start.10 = (f32[256,512]{1,0:T(8,128)}, f32[256,512]{1,0:T(8,128)}, u32[]{:S(2)}, u32[]{:S(2)}) collective-permute-start(f32[256,512]{1,0:T(8,128)} %collective-permute-done.8.refs_6_), channel_id=1, source_target_pairs={{0,1},{1,0},{2,3},{3,2},{4,5},{5,4},{6,7},{7,6},{8,9},{9,8},{10,11... | collective-permute-start | bytes 1572872 | tf_op jit(solution)/shard_map/ppermute | solution.py:21
  125.5 0.1 stack.39.starts
  125.6 0.1 and_select_fusion
  125.7 0.9 collective-permute-done.10.refs_8_
  126.7 7.6 %all-gather.2.cloned.1.call-done.strip = f32[4096,128]{1,0:T(8,128)} async-done(((f32[256,128]{1,0:T(8,128)}), f32[4096,128]{1,0:T(8,128)}) %all-gather.2.cloned.1.call-update) | async-done | bytes 2097168 | tf_op jit(solution)/shard_map/all_gather | solution.py:151
  134.2 7.7 %project.1 = f32[4,8,32,128]{3,2,1,0:T(8,128)S(1)} custom-call(s32[9]{0:T(128)S(1)} %stack.39.starts, f32[4096,128]{1,0:T(8,128)} %all-gather.2.cloned.1.call-done.strip, f32[4,128,512]{2,1,0:T(8,128)S(1)} %all_to_all.15.basis_mine, f32[4,128,512]{2,1,0:T(8,128)} %collective-permute-done.1.basis_theirs, f32[512,512]{1,0:T(8,128)S(1)} %pad_maximum_fusion.refs_0_, ...), custom_call_target="tpu_custom_call" | custom-call | flops 2013265920 | bytes 12582912 | tf_op jit(solution)/shard_map/project/pallas_call | solution.py:106
  141.9 11.6 %all_to_all.16 = f32[4,8,32,128]{3,2,1,0:T(8,128)S(1)} all-to-all(f32[4,8,32,128]{3,2,1,0:T(8,128)S(1)} %project.1), channel_id=1, replica_groups={{0,8,16,24},{32,40,48,56},{64,72,80,88},{96,104,112,120},{128,136,144,1..., dimensions={0} | all-to-all | bytes 1048576 | tf_op jit(solution)/shard_map/all_to_all | solution.py:193
  153.5 40.8 %all_to_all.17 = f32[8,32,128]{2,1,0:T(8,128)S(1)} all-to-all(f32[8,32,128]{2,1,0:T(8,128)S(1)} %reduce_sum.18), channel_id=1, replica_groups={{0,32,64,96,128,160,192,224},{8,40,72,104,136,168,200,232},{16,48,80,11..., dimensions={0} | all-to-all | bytes 262144 | tf_op jit(solution)/shard_map/all_to_all | solution.py:196
  194.3 5.7 %all_gather.7 = f32[32,256]{1,0:T(8,128)S(1)} all-gather(f32[32,128]{1,0:T(8,128)S(1)} %reduce_sum.19), channel_id=1, replica_groups=mesh['groups'=2,'row'=32,'col'=4,'sub'=2] {'sub'}, dimensions={1}, use_global_device_ids=true | all-gather | bytes 49152 | tf_op jit(solution)/shard_map/all_gather | solution.py:200
  200.1 0.6 select_bitcast_fusion
  (17 shorter events, 0.2 us)
Async XLA Ops:
  6.5 127.7 %all-gather.2.cloned.1.call-start = ((), (), s32[]{:S(2)}) async-start(), calls=%async_computation.3 | async-start | bytes 2228224 | tf_op jit(solution)/shard_map/all_gather | solution.py:151
  8.6 60.6 %copy-start = (f32[256,128]{1,0:T(8,128)S(1)}, f32[256,128]{1,0:T(8,128)}, u32[]{:S(2)}) copy-start(f32[256,128]{1,0:T(8,128)} %param.4) | copy-start | bytes 393220
  8.7 11.8 %collective-permute-start.2 = (f32[256,512]{1,0:T(8,128)S(1)}, f32[256,512]{1,0:T(8,128)S(1)}, u32[]{:S(2)}, u32[]{:S(2)}) collective-permute-start(f32[256,512]{1,0:T(8,128)S(1)} %pad_maximum_fusion.1), channel_id=1, source_target_pairs={{0,8},{8,0},{16,24},{24,16},{32,40},{40,32},{48,56},{56,48},{64,72... | collective-permute-start | bytes 1572872 | tf_op jit(solution)/shard_map/ppermute | solution.py:21
  20.6 80.7 %collective-permute-start.4 = (f32[512,512]{1,0:T(8,128)S(1)}, f32[512,512]{1,0:T(8,128)S(1)}, u32[]{:S(2)}, u32[]{:S(2)}) collective-permute-start(f32[512,512]{1,0:T(8,128)S(1)} %pad_maximum_fusion.refs_0_), channel_id=1, source_target_pairs={{0,6},{2,0},{4,2},{6,4},{1,7},{3,1},{5,3},{7,5},{8,14},{10,8},{12,... | collective-permute-start | bytes 3145736 | tf_op jit(solution)/shard_map/ppermute | solution.py:16
  30.6 73.6 %collective-permute-start.3 = (f32[512,512]{1,0:T(8,128)S(1)}, f32[512,512]{1,0:T(8,128)}, u32[]{:S(2)}, u32[]{:S(2)}) collective-permute-start(f32[512,512]{1,0:T(8,128)S(1)} %pad_maximum_fusion.refs_0_), channel_id=1, source_target_pairs={{0,2},{2,4},{4,6},{6,0},{1,3},{3,5},{5,7},{7,1},{8,10},{10,12},{12... | collective-permute-start | bytes 3145736 | tf_op jit(solution)/shard_map/ppermute | solution.py:16
  32.5 77.8 %collective-permute-start.5 = (f32[512,512]{1,0:T(8,128)S(1)}, f32[512,512]{1,0:T(8,128)}, u32[]{:S(2)}, u32[]{:S(2)}) collective-permute-start(f32[512,512]{1,0:T(8,128)S(1)} %pad_maximum_fusion.refs_0_), channel_id=1, source_target_pairs={{0,1},{1,0},{2,3},{3,2},{4,5},{5,4},{6,7},{7,6},{8,9},{9,8},{10,11... | collective-permute-start | bytes 3145736 | tf_op jit(solution)/shard_map/ppermute | solution.py:21
  69.2 11.4 %collective-permute-start = (f32[256,128]{1,0:T(8,128)S(1)}, f32[256,128]{1,0:T(8,128)S(1)}, u32[]{:S(2)}, u32[]{:S(2)}) collective-permute-start(f32[256,128]{1,0:T(8,128)S(1)} %copy-done), channel_id=1, source_target_pairs={{0,8},{8,0},{16,24},{24,16},{32,40},{40,32},{48,56},{56,48},{64,72... | collective-permute-start | bytes 393224 | tf_op jit(solution)/shard_map/ppermute | solution.py:21
  97.5 28.2 %collective-permute-start.1 = (f32[4,128,512]{2,1,0:T(8,128)S(1)}, f32[4,128,512]{2,1,0:T(8,128)}, u32[]{:S(2)}, u32[]{:S(2)}) collective-permute-start(f32[4,128,512]{2,1,0:T(8,128)S(1)} %all_to_all.15.basis_mine), channel_id=1, source_target_pairs={{0,1},{1,0},{2,3},{3,2},{4,5},{5,4},{6,7},{7,6},{8,9},{9,8},{10,11... | collective-permute-start | bytes 3145736 | tf_op jit(solution)/shard_map/ppermute | solution.py:21
  101.4 15.5 %collective-permute-start.9 = (f32[256,512]{1,0:T(8,128)S(1)}, f32[256,512]{1,0:T(8,128)}, u32[]{:S(2)}, u32[]{:S(2)}) collective-permute-start(f32[256,512]{1,0:T(8,128)S(1)} %slice.25), channel_id=1, source_target_pairs={{0,6},{2,0},{4,2},{6,4},{1,7},{3,1},{5,3},{7,5},{8,14},{10,8},{12,... | collective-permute-start | bytes 1572872 | tf_op jit(solution)/shard_map/ppermute | solution.py:16
  105.3 16.4 %collective-permute-start.8 = (f32[256,512]{1,0:T(8,128)S(1)}, f32[256,512]{1,0:T(8,128)}, u32[]{:S(2)}, u32[]{:S(2)}) collective-permute-start(f32[256,512]{1,0:T(8,128)S(1)} %slice.24), channel_id=1, source_target_pairs={{0,2},{2,4},{4,6},{6,0},{1,3},{3,5},{5,7},{7,1},{8,10},{10,12},{12... | collective-permute-start | bytes 1572872 | tf_op jit(solution)/shard_map/ppermute | solution.py:16
  107.8 17.9 %collective-permute-start.7 = (f32[512,512]{1,0:T(8,128)S(1)}, f32[512,512]{1,0:T(8,128)}, u32[]{:S(2)}, u32[]{:S(2)}) collective-permute-start(f32[512,512]{1,0:T(8,128)S(1)} %collective-permute-done.4.refs_2_), channel_id=1, source_target_pairs={{0,1},{1,0},{2,3},{3,2},{4,5},{5,4},{6,7},{7,6},{8,9},{9,8},{10,11... | collective-permute-start | bytes 3145736 | tf_op jit(solution)/shard_map/ppermute | solution.py:21
  110.4 16.3 %collective-permute-start.6 = (f32[512,512]{1,0:T(8,128)}, f32[512,512]{1,0:T(8,128)}, u32[]{:S(2)}, u32[]{:S(2)}) collective-permute-start(f32[512,512]{1,0:T(8,128)} %collective-permute-done.3.refs_1_), channel_id=1, source_target_pairs={{0,1},{1,0},{2,3},{3,2},{4,5},{5,4},{6,7},{7,6},{8,9},{9,8},{10,11... | collective-permute-start | bytes 3145736 | tf_op jit(solution)/shard_map/ppermute | solution.py:21
  116.9 8.8 %collective-permute-start.11 = (f32[256,512]{1,0:T(8,128)}, f32[256,512]{1,0:T(8,128)}, u32[]{:S(2)}, u32[]{:S(2)}) collective-permute-start(f32[256,512]{1,0:T(8,128)} %collective-permute-done.9.refs_7_), channel_id=1, source_target_pairs={{0,1},{1,0},{2,3},{3,2},{4,5},{5,4},{6,7},{7,6},{8,9},{9,8},{10,11... | collective-permute-start | bytes 1572872 | tf_op jit(solution)/shard_map/ppermute | solution.py:21
  121.7 4.9 %collective-permute-start.10 = (f32[256,512]{1,0:T(8,128)}, f32[256,512]{1,0:T(8,128)}, u32[]{:S(2)}, u32[]{:S(2)}) collective-permute-start(f32[256,512]{1,0:T(8,128)} %collective-permute-done.8.refs_6_), channel_id=1, source_target_pairs={{0,1},{1,0},{2,3},{3,2},{4,5},{5,4},{6,7},{7,6},{8,9},{9,8},{10,11... | collective-permute-start | bytes 1572872 | tf_op jit(solution)/shard_map/ppermute | solution.py:21
Sparse Core Ops, SparseCore 0:
  9.4 124.7 all-gather.1

commit v7 on v6

--- a/solution.py
+++ b/solution.py
@@ -29,6 +29,32 @@
 
 def dot(left, right):
     return jnp.dot(left, right, preferred_element_type=jnp.float32)
+
+
+def split_kernel(piece, out):
+    width = piece.shape[1]
+    high, low = halves(piece[...])
+    out[:, :width] = high
+    out[:, width:] = low
+
+
+def split(piece):
+    rows, width = piece.shape
+    tile = TILE // 2
+    return pl.pallas_call(
+        split_kernel,
+        grid=(rows // tile,),
+        in_specs=[pl.BlockSpec((tile, width), lambda i: (i, 0))],
+        out_specs=pl.BlockSpec((tile, 2 * width), lambda i: (i, 0)),
+        out_shape=pltpu.HBM((rows, 2 * width), jnp.bfloat16),
+        compiler_params=pltpu.CompilerParams(
+            dimension_semantics=("arbitrary",), vmem_limit_bytes=8 * 2**20
+        ),
+        cost_estimate=pl.CostEstimate(
+            flops=3 * piece.size, bytes_accessed=8 * piece.size, transcendentals=0
+        ),
+        name="split",
+    )(piece)
 
 
 def project_kernel(starts, strip, basis_mine, basis_theirs, *refs):
@@ -71,9 +97,8 @@
         for t in range(per_piece):
             tile_copy(n, t).wait()
             here = slice(t * TILE, (t + 1) * TILE)
-            left_high, left_low = halves(tiles[n, here])
-            both = dot(left_high, right)
-            value = both[:, :wide] + (both[:, wide:] + dot(left_low, high))
+            both = dot(tiles[n, here, :span], right)
+            value = both[:, :wide] + (both[:, wide:] + dot(tiles[n, here, span:], high))
             if n == 0:
                 image[here, :] = value
             else:
@@ -93,11 +118,14 @@
 
 
 def projected(starts, strip, basis, whole, halved, share):
-    rows, span = whole[0].shape
+    rows, span = whole[0].shape[0], whole[0].shape[1] // 2
     wide = strip.shape[1]
     total = 2 * basis[0].shape[0] * basis[0].shape[1]
     n_pieces = len(whole) + len(halved)
-    pieces = [*whole, *(half for pair in halved for half in pair)]
+    pieces = [
+        pltpu.with_memory_space_constraint(piece, pltpu.HBM)
+        for piece in (*whole, *(half for pair in halved for half in pair))
+    ]
     out_shape = (NEAR, total // share // NEAR, share, wide)
     vmem = pl.BlockSpec(memory_space=pltpu.VMEM)
     anywhere = pl.BlockSpec(memory_space=pl.ANY)
@@ -110,7 +138,7 @@
         out_specs=vmem,
         scratch_shapes=[
             pltpu.VMEM((n_pieces, span, wide), jnp.float32),
-            pltpu.VMEM((n_pieces, rows, span), jnp.float32),
+            pltpu.VMEM((n_pieces, rows, 2 * span), jnp.bfloat16),
             pltpu.VMEM(basis[1].shape, jnp.float32),
             pltpu.SemaphoreType.DMA((n_pieces,)),
             pltpu.SemaphoreType.DMA((n_pieces, rows // TILE)),
@@ -185,7 +213,9 @@
     share = 2 * n_col * basis_vectors.shape[1] // n_row
     keep = kept(split_size[0], row, col, sub, share, 2 * basis_vectors.shape[1])
     starts, keep = lax.optimization_barrier((starts.astype(jnp.int32), keep))
-    partial = projected(starts, strip, basis, mine + theirs, (across, across_other), share)
+    whole = [split(piece) for piece in mine + theirs]
+    halved = [tuple(split(half) for half in pair) for pair in (across, across_other)]
+    partial = projected(starts, strip, basis, whole, halved, share)
 
     far = n_row // NEAR
     near_groups = [[NEAR * g + q for q in range(NEAR)] for g in range(far)]

time: 209 us -> 223 us (1.067)
  Pallas kernels: 7.66 us -> 32.5 us
  waiting for transfers between devices: 31.8 us -> 21.5 us
  blocking collectives: 74.8 us -> 64.6 us
  starting transfers between devices: 75.2 us -> 81.5 us
  local copies, waits for them, and re-layouts: 1.45 us -> 4.09 us
    pallas_call x0 -> x10, Pallas kernels: none -> 24.1 us  [split(): pl.pallas_call(split_kernel, grid=(rows // tile,), in_specs=[pl.BlockSpec...]
    all_to_all x1 -> x0, blocking collectives: 16.7 us -> none  [split_projection(): basis_mine = lax.all_to_all(pair_t, 'col', 0, 0, tiled=True)]
    all_gather x1, waiting for transfers between devices: 7.58 us -> 0.01 us  [split_projection(): lax.all_gather(basis_vectors, 'row', axis=0, tiled=True, axis_index_group...]
    all_to_all x1, blocking collectives: 11.6 us -> 15.9 us  [split_projection(): lax.all_to_all(partial, 'row', 0, 0, tiled=True, axis_index_groups=near_g...]
    all_to_all x0 -> x1, starting transfers between devices: none -> 3.61 us  [split_projection(): basis_mine = lax.all_to_all(pair_t, 'col', 0, 0, tiled=True)]
  transfers between devices with their start and end apart: 13 -> 14, of which waited for: 6 -> 3; matrix products, arithmetic and copies ran while one was open for 1% -> 3% of each run, Pallas kernels for 0% -> 11%
where the time goes in v7:
time: 223 us; the launch traced here: 221 us
  starting transfers between devices  81.5 us (37%)
  blocking collectives  64.6 us (29%)
  Pallas kernels  32.5 us (15%)
  waiting for transfers between devices  21.5 us (10%)
  between operations  14.4 us (6%)
  local copies, waits for them, and re-layouts  4.09 us (2%)
    ppermute x8, starting transfers between devices, swapped(): return lax.ppermute(array, axis, [(i, i ^ 1) for i in range(size)])  59.5 us
    all_to_all x1, blocking collectives, split_projection(): lax.all_to_all(partial, 'row', 0, 0, tiled=True, axis_index_groups=far_gr...  41.5 us
    pallas_call x10, Pallas kernels, split(): pl.pallas_call(split_kernel, grid=(rows // tile,), in_specs=[pl.BlockSpec...  24.1 us
    ppermute x4, starting transfers between devices, shifted(): lax.ppermute(array, axis, [(i, (i + step) % size) for i in range(size)])  18.4 us
    ppermute x8, waiting for transfers between devices, swapped(): return lax.ppermute(array, axis, [(i, i ^ 1) for i in range(size)])  16 us
    all_to_all x1, blocking collectives, split_projection(): lax.all_to_all(partial, 'row', 0, 0, tiled=True, axis_index_groups=near_g...  15.9 us
    pallas_call x1, Pallas kernels, projected(): pl.pallas_call(project_kernel, in_specs=[pl.BlockSpec(memory_space=pltpu....  8.4 us
    all_gather x1, blocking collectives, split_projection(): child_block = lax.all_gather(proj_block, 'sub', axis=1, tiled=True)  7.13 us
  transfers between devices with their start and end apart: 14, of which 3 were waited for; matrix products, arithmetic and copies ran while one was open for 3% of the time, Pallas kernels for 11%

profile of v7, /device:TPU:33, one launch (start us, length us, event | category | flops | bytes accessed | tf_op | source)
XLA Modules:
  0.0 220.7 jit_solution(6086371374923033455)
XLA Ops:
  7.3 1.3 slice_select_fusion.3
  8.7 5.3 %collective-permute-start.2 = (f32[256,512]{1,0:T(8,128)S(1)}, f32[256,512]{1,0:T(8,128)S(1)}, u32[]{:S(2)}, u32[]{:S(2)}) collective-permute-start(f32[256,512]{1,0:T(8,128)S(1)} %pad_maximum_fusion.1), channel_id=1, source_target_pairs={{0,8},{8,0},{16,24},{24,16},{32,40},{40,32},{48,56},{56,48},{64,72... | collective-permute-start | bytes 1572872 | tf_op jit(solution)/shard_map/ppermute | solution.py:21
  13.9 6.6 %collective-permute-done.2 = f32[256,512]{1,0:T(8,128)S(1)} collective-permute-done((f32[256,512]{1,0:T(8,128)S(1)}, f32[256,512]{1,0:T(8,128)S(1)}, u32[]{:S(2)}, u32[]{:S(2)}) %collective-permute-start.2) | collective-permute-done | bytes 524320 | tf_op jit(solution)/shard_map/ppermute | solution.py:21
  20.6 9.9 %collective-permute-start.4 = (f32[512,512]{1,0:T(8,128)S(1)}, f32[512,512]{1,0:T(8,128)}, u32[]{:S(2)}, u32[]{:S(2)}) collective-permute-start(f32[512,512]{1,0:T(8,128)S(1)} %pad_maximum_fusion.piece), channel_id=1, source_target_pairs={{0,6},{2,0},{4,2},{6,4},{1,7},{3,1},{5,3},{7,5},{8,14},{10,8},{12,... | collective-permute-start | bytes 3145736 | tf_op jit(solution)/shard_map/ppermute | solution.py:16
  30.6 2.0 collective-permute-start.3
  32.5 36.7 %collective-permute-start.5 = (f32[512,512]{1,0:T(8,128)S(1)}, f32[512,512]{1,0:T(8,128)}, u32[]{:S(2)}, u32[]{:S(2)}) collective-permute-start(f32[512,512]{1,0:T(8,128)S(1)} %pad_maximum_fusion.piece), channel_id=1, source_target_pairs={{0,1},{1,0},{2,3},{3,2},{4,5},{5,4},{6,7},{7,6},{8,9},{9,8},{10,11... | collective-permute-start | bytes 3145736 | tf_op jit(solution)/shard_map/ppermute | solution.py:21
  69.2 2.0 collective-permute-start
  71.2 9.4 %collective-permute-done = f32[256,128]{1,0:T(8,128)S(1)} collective-permute-done((f32[256,128]{1,0:T(8,128)S(1)}, f32[256,128]{1,0:T(8,128)S(1)}, u32[]{:S(2)}, u32[]{:S(2)}) %collective-permute-start) | collective-permute-done | bytes 131104 | tf_op jit(solution)/shard_map/ppermute | solution.py:21
  81.9 3.6 %all-to-all-start = ((f32[4,128,512]{2,1,0:T(8,128)}), f32[4,128,512]{2,1,0:T(8,128)S(1)}, u32[]{:S(2)}, u32[]{:S(2)}) async-start(f32[4,128,512]{2,1,0:T(8,128)} %broadcast_in_dim.7), calls=%async_computation | async-start | bytes 2097152 | tf_op jit(solution)/shard_map/all_to_all | solution.py:194
  85.5 1.9 slice.25
  87.4 4.5 %collective-permute-start.9 = (f32[256,512]{1,0:T(8,128)}, f32[256,512]{1,0:T(8,128)}, u32[]{:S(2)}, u32[]{:S(2)}) collective-permute-start(f32[256,512]{1,0:T(8,128)} %slice.25), channel_id=1, source_target_pairs={{0,6},{2,0},{4,2},{6,4},{1,7},{3,1},{5,3},{7,5},{8,14},{10,8},{12,... | collective-permute-start | bytes 1572872 | tf_op jit(solution)/shard_map/ppermute | solution.py:16
  92.8 1.9 collective-permute-start.8
  94.7 3.4 %collective-permute-start.7 = (f32[512,512]{1,0:T(8,128)}, f32[512,512]{1,0:T(8,128)}, u32[]{:S(2)}, u32[]{:S(2)}) collective-permute-start(f32[512,512]{1,0:T(8,128)} %collective-permute-done.4.piece), channel_id=1, source_target_pairs={{0,1},{1,0},{2,3},{3,2},{4,5},{5,4},{6,7},{7,6},{8,9},{9,8},{10,11... | collective-permute-start | bytes 3145736 | tf_op jit(solution)/shard_map/ppermute | solution.py:21
  98.1 2.0 collective-permute-start.6
  100.1 4.6 %collective-permute-start.1 = (f32[4,128,512]{2,1,0:T(8,128)S(1)}, f32[4,128,512]{2,1,0:T(8,128)}, u32[]{:S(2)}, u32[]{:S(2)}) collective-permute-start(f32[4,128,512]{2,1,0:T(8,128)S(1)} %all-to-all-done.basis_mine), channel_id=1, source_target_pairs={{0,1},{1,0},{2,3},{3,2},{4,5},{5,4},{6,7},{7,6},{8,9},{9,8},{10,11... | collective-permute-start | bytes 3145736 | tf_op jit(solution)/shard_map/ppermute | solution.py:21
  104.7 4.8 %collective-permute-done.9.piece = f32[256,512]{1,0:T(8,128)} collective-permute-done((f32[256,512]{1,0:T(8,128)}, f32[256,512]{1,0:T(8,128)}, u32[]{:S(2)}, u32[]{:S(2)}) %collective-permute-start.9) | collective-permute-done | bytes 524320 | tf_op jit(solution)/shard_map/ppermute | solution.py:16
  109.5 3.7 %collective-permute-start.11 = (f32[256,512]{1,0:T(8,128)}, f32[256,512]{1,0:T(8,128)}, u32[]{:S(2)}, u32[]{:S(2)}) collective-permute-start(f32[256,512]{1,0:T(8,128)} %collective-permute-done.9.piece), channel_id=1, source_target_pairs={{0,1},{1,0},{2,3},{3,2},{4,5},{5,4},{6,7},{7,6},{8,9},{9,8},{10,11... | collective-permute-start | bytes 1572872 | tf_op jit(solution)/shard_map/ppermute | solution.py:21
  113.2 2.0 collective-permute-start.10
  116.1 1.6 split.10.refs_0_
  117.7 3.4 %split.12.refs_2_ = bf16[512,1024]{1,0:T(8,128)(2,1)} custom-call(f32[512,512]{1,0:T(8,128)} %collective-permute-done.4.piece), custom_call_target="tpu_custom_call" | custom-call | flops 786432 | bytes 2097152 | tf_op jit(solution)/shard_map/split/pallas_call | solution.py:44
  121.2 1.6 split.11.refs_1_
  122.8 3.4 %split.13.refs_3_ = bf16[512,1024]{1,0:T(8,128)(2,1)} custom-call(f32[512,512]{1,0:T(8,128)} %collective-permute-done.5.piece), custom_call_target="tpu_custom_call" | custom-call | flops 786432 | bytes 2097152 | tf_op jit(solution)/shard_map/split/pallas_call | solution.py:44
  126.2 1.8 split.17.refs_7_
  128.0 1.8 split.16.refs_6_
  129.8 1.8 split.19.refs_9_
  131.6 1.8 split.18.refs_8_
  133.4 3.4 %split.15.refs_5_ = bf16[512,1024]{1,0:T(8,128)(2,1)} custom-call(f32[512,512]{1,0:T(8,128)} %collective-permute-done.7.piece), custom_call_target="tpu_custom_call" | custom-call | flops 786432 | bytes 2097152 | tf_op jit(solution)/shard_map/split/pallas_call | solution.py:44
  136.8 3.4 %split.14.refs_4_ = bf16[512,1024]{1,0:T(8,128)(2,1)} custom-call(f32[512,512]{1,0:T(8,128)} %collective-permute-done.6.piece), custom_call_target="tpu_custom_call" | custom-call | flops 786432 | bytes 2097152 | tf_op jit(solution)/shard_map/split/pallas_call | solution.py:44
  140.2 8.4 %project.1 = f32[4,8,32,128]{3,2,1,0:T(8,128)S(1)} custom-call(s32[9]{0:T(128)S(1)} %stack.39.starts, f32[4096,128]{1,0:T(8,128)} %all-gather.2.cloned.1.call-done.strip, f32[4,128,512]{2,1,0:T(8,128)S(1)} %all-to-all-done.basis_mine, f32[4,128,512]{2,1,0:T(8,128)} %collective-permute-done.1.basis_theirs, bf16[512,1024]{1,0:T(8,128)(2,1)} %split.10.refs_0_, ...), custom_call_target="tpu_custom_call" | custom-call | flops 2013265920 | bytes 12582912 | tf_op jit(solution)/shard_map/project/pallas_call | solution.py:134
  148.6 15.9 %all_to_all.15 = f32[4,8,32,128]{3,2,1,0:T(8,128)S(1)} all-to-all(f32[4,8,32,128]{3,2,1,0:T(8,128)S(1)} %project.1), channel_id=1, replica_groups={{0,8,16,24},{32,40,48,56},{64,72,80,88},{96,104,112,120},{128,136,144,1..., dimensions={0} | all-to-all | bytes 1048576 | tf_op jit(solution)/shard_map/all_to_all | solution.py:223
  164.6 41.5 %all_to_all.16 = f32[8,32,128]{2,1,0:T(8,128)S(1)} all-to-all(f32[8,32,128]{2,1,0:T(8,128)S(1)} %reduce_sum.18), channel_id=1, replica_groups={{0,32,64,96,128,160,192,224},{8,40,72,104,136,168,200,232},{16,48,80,11..., dimensions={0} | all-to-all | bytes 262144 | tf_op jit(solution)/shard_map/all_to_all | solution.py:226
  206.1 7.1 %all_gather.7 = f32[32,256]{1,0:T(8,128)S(1)} all-gather(f32[32,128]{1,0:T(8,128)S(1)} %reduce_sum.19), channel_id=1, replica_groups=mesh['groups'=2,'row'=32,'col'=4,'sub'=2] {'sub'}, dimensions={1}, use_global_device_ids=true | all-gather | bytes 49152 | tf_op jit(solution)/shard_map/all_gather | solution.py:230
  (28 shorter events, 3.9 us)
Async XLA Ops:
  6.5 133.7 %all-gather.2.cloned.1.call-start = ((), (), s32[]{:S(2)}) async-start(), calls=%async_computation.3 | async-start | bytes 2228224 | tf_op jit(solution)/shard_map/all_gather | solution.py:179
  8.6 60.6 %copy-start = (f32[256,128]{1,0:T(8,128)S(1)}, f32[256,128]{1,0:T(8,128)}, u32[]{:S(2)}) copy-start(f32[256,128]{1,0:T(8,128)} %param.4) | copy-start | bytes 393220
  8.7 11.8 %collective-permute-start.2 = (f32[256,512]{1,0:T(8,128)S(1)}, f32[256,512]{1,0:T(8,128)S(1)}, u32[]{:S(2)}, u32[]{:S(2)}) collective-permute-start(f32[256,512]{1,0:T(8,128)S(1)} %pad_maximum_fusion.1), channel_id=1, source_target_pairs={{0,8},{8,0},{16,24},{24,16},{32,40},{40,32},{48,56},{56,48},{64,72... | collective-permute-start | bytes 1572872 | tf_op jit(solution)/shard_map/ppermute | solution.py:21
  20.6 64.9 %collective-permute-start.4 = (f32[512,512]{1,0:T(8,128)S(1)}, f32[512,512]{1,0:T(8,128)}, u32[]{:S(2)}, u32[]{:S(2)}) collective-permute-start(f32[512,512]{1,0:T(8,128)S(1)} %pad_maximum_fusion.piece), channel_id=1, source_target_pairs={{0,6},{2,0},{4,2},{6,4},{1,7},{3,1},{5,3},{7,5},{8,14},{10,8},{12,... | collective-permute-start | bytes 3145736 | tf_op jit(solution)/shard_map/ppermute | solution.py:16
  30.6 61.3 %collective-permute-start.3 = (f32[512,512]{1,0:T(8,128)S(1)}, f32[512,512]{1,0:T(8,128)S(1)}, u32[]{:S(2)}, u32[]{:S(2)}) collective-permute-start(f32[512,512]{1,0:T(8,128)S(1)} %pad_maximum_fusion.piece), channel_id=1, source_target_pairs={{0,2},{2,4},{4,6},{6,0},{1,3},{3,5},{5,7},{7,1},{8,10},{10,12},{12... | collective-permute-start | bytes 3145736 | tf_op jit(solution)/shard_map/ppermute | solution.py:16
  32.5 67.6 %collective-permute-start.5 = (f32[512,512]{1,0:T(8,128)S(1)}, f32[512,512]{1,0:T(8,128)}, u32[]{:S(2)}, u32[]{:S(2)}) collective-permute-start(f32[512,512]{1,0:T(8,128)S(1)} %pad_maximum_fusion.piece), channel_id=1, source_target_pairs={{0,1},{1,0},{2,3},{3,2},{4,5},{5,4},{6,7},{7,6},{8,9},{9,8},{10,11... | collective-permute-start | bytes 3145736 | tf_op jit(solution)/shard_map/ppermute | solution.py:21
  69.2 11.4 %collective-permute-start = (f32[256,128]{1,0:T(8,128)S(1)}, f32[256,128]{1,0:T(8,128)S(1)}, u32[]{:S(2)}, u32[]{:S(2)}) collective-permute-start(f32[256,128]{1,0:T(8,128)S(1)} %copy-done), channel_id=1, source_target_pairs={{0,8},{8,0},{16,24},{24,16},{32,40},{40,32},{48,56},{56,48},{64,72... | collective-permute-start | bytes 393224 | tf_op jit(solution)/shard_map/ppermute | solution.py:21
  81.9 18.2 %all-to-all-start = ((f32[4,128,512]{2,1,0:T(8,128)}), f32[4,128,512]{2,1,0:T(8,128)S(1)}, u32[]{:S(2)}, u32[]{:S(2)}) async-start(f32[4,128,512]{2,1,0:T(8,128)} %broadcast_in_dim.7), calls=%async_computation | async-start | bytes 2097152 | tf_op jit(solution)/shard_map/all_to_all | solution.py:194
  87.4 22.2 %collective-permute-start.9 = (f32[256,512]{1,0:T(8,128)}, f32[256,512]{1,0:T(8,128)}, u32[]{:S(2)}, u32[]{:S(2)}) collective-permute-start(f32[256,512]{1,0:T(8,128)} %slice.25), channel_id=1, source_target_pairs={{0,6},{2,0},{4,2},{6,4},{1,7},{3,1},{5,3},{7,5},{8,14},{10,8},{12,... | collective-permute-start | bytes 1572872 | tf_op jit(solution)/shard_map/ppermute | solution.py:16
  92.8 20.5 %collective-permute-start.8 = (f32[256,512]{1,0:T(8,128)}, f32[256,512]{1,0:T(8,128)}, u32[]{:S(2)}, u32[]{:S(2)}) collective-permute-start(f32[256,512]{1,0:T(8,128)} %slice.24), channel_id=1, source_target_pairs={{0,2},{2,4},{4,6},{6,0},{1,3},{3,5},{5,7},{7,1},{8,10},{10,12},{12... | collective-permute-start | bytes 1572872 | tf_op jit(solution)/shard_map/ppermute | solution.py:16
  94.7 38.7 %collective-permute-start.7 = (f32[512,512]{1,0:T(8,128)}, f32[512,512]{1,0:T(8,128)}, u32[]{:S(2)}, u32[]{:S(2)}) collective-permute-start(f32[512,512]{1,0:T(8,128)} %collective-permute-done.4.piece), channel_id=1, source_target_pairs={{0,1},{1,0},{2,3},{3,2},{4,5},{5,4},{6,7},{7,6},{8,9},{9,8},{10,11... | collective-permute-start | bytes 3145736 | tf_op jit(solution)/shard_map/ppermute | solution.py:21
  98.1 38.7 %collective-permute-start.6 = (f32[512,512]{1,0:T(8,128)S(1)}, f32[512,512]{1,0:T(8,128)}, u32[]{:S(2)}, u32[]{:S(2)}) collective-permute-start(f32[512,512]{1,0:T(8,128)S(1)} %collective-permute-done.3.piece), channel_id=1, source_target_pairs={{0,1},{1,0},{2,3},{3,2},{4,5},{5,4},{6,7},{7,6},{8,9},{9,8},{10,11... | collective-permute-start | bytes 3145736 | tf_op jit(solution)/shard_map/ppermute | solution.py:21
  100.1 40.1 %collective-permute-start.1 = (f32[4,128,512]{2,1,0:T(8,128)S(1)}, f32[4,128,512]{2,1,0:T(8,128)}, u32[]{:S(2)}, u32[]{:S(2)}) collective-permute-start(f32[4,128,512]{2,1,0:T(8,128)S(1)} %all-to-all-done.basis_mine), channel_id=1, source_target_pairs={{0,1},{1,0},{2,3},{3,2},{4,5},{5,4},{6,7},{7,6},{8,9},{9,8},{10,11... | collective-permute-start | bytes 3145736 | tf_op jit(solution)/shard_map/ppermute | solution.py:21
  109.5 20.3 %collective-permute-start.11 = (f32[256,512]{1,0:T(8,128)}, f32[256,512]{1,0:T(8,128)}, u32[]{:S(2)}, u32[]{:S(2)}) collective-permute-start(f32[256,512]{1,0:T(8,128)} %collective-permute-done.9.piece), channel_id=1, source_target_pairs={{0,1},{1,0},{2,3},{3,2},{4,5},{5,4},{6,7},{7,6},{8,9},{9,8},{10,11... | collective-permute-start | bytes 1572872 | tf_op jit(solution)/shard_map/ppermute | solution.py:21
  113.2 18.3 %collective-permute-start.10 = (f32[256,512]{1,0:T(8,128)}, f32[256,512]{1,0:T(8,128)}, u32[]{:S(2)}, u32[]{:S(2)}) collective-permute-start(f32[256,512]{1,0:T(8,128)} %collective-permute-done.8.piece), channel_id=1, source_target_pairs={{0,1},{1,0},{2,3},{3,2},{4,5},{5,4},{6,7},{7,6},{8,9},{9,8},{10,11... | collective-permute-start | bytes 1572872 | tf_op jit(solution)/shard_map/ppermute | solution.py:21
Sparse Core Ops, SparseCore 0:
  9.4 123.9 all-gather.1
